TPU v7x, 256 devices: a whole 4x4x8 slice. The times are simulated.
256 devices in a mesh: row: 4 (over y_lo, core), blk: 64 (over y_hi, x, z).
Axes of the slice: x: 4, y: 4 (y_hi: 2, y_lo: 2; y = y_hi * 2 + y_lo), z: 8, core: 2. Of those that a mesh axis runs over, the one named last changes fastest.
Arguments:
- matrix: float32 [16384, 16384], P('row', 'blk'), may hold values from -6 to 6
Outputs:
- rotated: float32 [16384, 16384], P('row', 'blk')
- off_measure: float32 [2], replicated
All inputs are finite; a program needn't handle non-finite values.
Results may differ from a plain program's by a relative error of at most 0.00012.
Values sent between devices are 32-bit elements; how exact they have to be, the bound alone decides.
No kernel may reach another device: no remote copies, remote signals or barrier semaphores. Data moves between devices by JAX's collectives and lax.ppermute only.
A program may use at most 64 MiB of HBM per device.

v0:
```python
import functools

import jax
import jax.numpy as jnp
from jax import lax
from jax.experimental import pallas as pl
from jax.experimental.pallas import tpu as pltpu
from jax.sharding import PartitionSpec as P


STEPS = 2
NS_ITERS = 4
B = 128
PACK = 136
UNITS = 32
FRONT = (2, 4, 4, 4, 4, 4)
BACK = (5, 5)

VM = pl.BlockSpec(memory_space=pltpu.VMEM)
ANY = pl.BlockSpec(memory_space=pl.ANY)
HBM = pl.BlockSpec(memory_space=pltpu.HBM)
F32 = jnp.float32
BF16 = jnp.bfloat16


def params(mib=24):
    return pltpu.CompilerParams(vmem_limit_bytes=mib * 1024 * 1024)


def cost(flops, moved):
    return pl.CostEstimate(flops=int(flops), bytes_accessed=int(moved), transcendentals=0)


def halves(x):
    high = x.astype(BF16)
    low = (x - high.astype(F32)).astype(BF16)
    return high, low


def dot(a, b):
    return jnp.dot(a, b, preferred_element_type=F32)


def dot_rows(a, b):
    return lax.dot_general(a, b, (((0,), (0,)), ((), ())), preferred_element_type=F32)


def split_dot(a, b):
    ah, al = a
    bh, bl = b
    return dot(ah, bh) + (dot(ah, bl) + dot(al, bh))


def gram_tile(left, right):
    lh, ll = halves(left)
    rh, rl = halves(right)
    full = dot_rows(jnp.concatenate([lh, ll], 1), jnp.concatenate([rh, rl], 1))
    return (full[:B, :B] + full[B:, B:]) + (full[:B, B:] + full[B:, :B])


def column_squares(x):
    return jnp.sum((x * x).reshape(x.shape[0] // 8, 8, x.shape[1]), axis=0)


def gram_body(blocks, m_ref, o_ref, held_ref, c_acc, n_acc, sems):
    block = m_ref.shape[0] // blocks

    def load(i):
        rows = pl.ds(i * block, block)
        return pltpu.make_async_copy(m_ref.at[rows, :], held_ref.at[rows, :], sems.at[i])

    for i in range(blocks):
        load(i).start()
    for i in range(blocks):
        load(i).wait()
        x = held_ref[i * block : (i + 1) * block, :]
        squares = column_squares(x)
        product = gram_tile(x[:, :B], x[:, B:])
        if i == 0:
            n_acc[...] = squares
            c_acc[...] = product
        else:
            n_acc[...] += squares
            c_acc[...] += product
    norms = jnp.sum(n_acc[...], axis=0, keepdims=True)
    o_ref[:B, :] = c_acc[...]
    o_ref[B:, :] = jnp.concatenate(
        [norms[:, :B], norms[:, B:], jnp.zeros((PACK - B - 2, B), F32)], axis=0
    )


def first_gram(matrix):
    rows = matrix.shape[0]
    return pl.pallas_call(
        functools.partial(gram_body, 8),
        in_specs=[HBM],
        out_specs=VM,
        out_shape=jax.ShapeDtypeStruct((PACK, B), F32),
        scratch_shapes=[
            pltpu.VMEM(matrix.shape, F32),
            pltpu.VMEM((B, B), F32),
            pltpu.VMEM((8, 2 * B), F32),
            pltpu.SemaphoreType.DMA((8,)),
        ],
        compiler_params=params(52),
        cost_estimate=cost(rows * B * B * 8, rows * B * 8),
        name="first_gram",
    )(matrix)


def root_body(a_ref, b_ref, c_ref, d_ref, wh_ref, wl_ref, s_ref):
    total = (a_ref[...] + b_ref[...]) + (c_ref[...] + d_ref[...])
    inverse = lax.rsqrt(total[B : B + 8, :])
    first = jnp.broadcast_to(inverse[0:1, :], (B, B)).T
    cosines = total[:B, :] * first * inverse[1:2, :]
    squares = jnp.sum(cosines * cosines)
    k = 0.5 * cosines
    scale = 1.0 + jnp.sum(k * k)
    kt = k.T
    row = lax.broadcasted_iota(jnp.int32, (B, B), 0)
    col = lax.broadcasted_iota(jnp.int32, (B, B), 1)
    eye = (row == col).astype(F32)
    ks, kts = halves(k), halves(kt)
    current = [(eye + split_dot(ks, kts)) / scale, (eye + split_dot(kts, ks)) / scale]
    result = [None, None]
    for step in range(NS_ITERS):
        for side in range(2):
            ys = halves(current[side])
            if step == 0:
                factor = 1.5 * eye - 0.5 * current[side]
                fs = halves(factor)
                result[side] = factor
            else:
                zs = halves(result[side])
                factor = 1.5 * eye - 0.5 * split_dot(zs, ys)
                fs = halves(factor)
                result[side] = split_dot(fs, zs)
            if step < NS_ITERS - 1:
                current[side] = split_dot(ys, fs)
    root = lax.sqrt(jnp.full((1, B), scale, F32))
    q1 = result[0] / root
    q2 = result[1] / root
    q1s, q2s = halves(q1), halves(q2)
    corner = split_dot(ks, q2s)
    lower = -split_dot(kts, q1s)
    for value, rows, cols in ((q1, 0, 0), (corner, 0, B), (lower, B, 0), (q2, B, B)):
        high, low = halves(value)
        wh_ref[rows : rows + B, cols : cols + B] = high
        wl_ref[rows : rows + B, cols : cols + B] = low
    s_ref[...] = jnp.full((8, B), squares, F32)


def roots(parts):
    return pl.pallas_call(
        root_body,
        in_specs=[VM] * 4,
        out_specs=[VM] * 3,
        out_shape=[
            jax.ShapeDtypeStruct((2 * B, 2 * B), BF16),
            jax.ShapeDtypeStruct((2 * B, 2 * B), BF16),
            jax.ShapeDtypeStruct((8, B), F32),
        ],
        compiler_params=params(8),
        cost_estimate=cost(30e6, 1e6),
        name="roots",
    )(*parts)


def mixed(x, wh, wl):
    rows = x.shape[0]
    xh, xl = halves(x)
    both = dot(jnp.concatenate([xh, xl], axis=0), wh)
    return both[:rows] + (both[rows:] + dot(xh, wl))


def update_body(start, sizes, m_ref, wh_ref, wl_ref, *outs):
    wh, wl = wh_ref[...], wl_ref[...]
    at = start
    for n, size in enumerate(sizes):
        value = mixed(m_ref[at : at + size, :], wh, wl)
        outs[2 * n][...] = value[:, :B]
        outs[2 * n + 1][...] = value[:, B:]
        at += size


def update(matrix, w, start, sizes):
    shapes = []
    for size in sizes:
        shapes += [jax.ShapeDtypeStruct((size, B), F32)] * 2
    total = sum(sizes)
    outs = pl.pallas_call(
        functools.partial(update_body, start, tuple(sizes)),
        in_specs=[VM] * 3,
        out_specs=[VM] * len(shapes),
        out_shape=shapes,
        compiler_params=params(12),
        cost_estimate=cost(6 * total * 256 * 256, total * B * 16),
    )(matrix, *w)
    return outs[0::2], outs[1::2]


def partial_body(count, right_only, with_right, *refs):
    lefts = refs[:count]
    rights = refs[count : 2 * count]
    extra = refs[2 * count : 2 * count + right_only]
    o_ref = refs[-1]
    acc = jnp.zeros((B, B), F32)
    lsq = jnp.zeros((8, B), F32)
    rsq = jnp.zeros((8, B), F32)
    for left, right in zip(lefts, rights):
        x, y = left[...], right[...]
        acc = acc + gram_tile(x, y)
        lsq = lsq + column_squares(x)
        if with_right:
            rsq = rsq + column_squares(y)
    for right in extra:
        rsq = rsq + column_squares(right[...])
    tail = jnp.concatenate(
        [
            jnp.sum(lsq, axis=0, keepdims=True),
            jnp.sum(rsq, axis=0, keepdims=True),
            jnp.zeros((PACK - B - 2, B), F32),
        ],
        axis=0,
    )
    for base in refs[2 * count + right_only : -1]:
        acc = acc + base[:B, :]
        tail = tail + base[B:, :]
    o_ref[:B, :] = acc
    o_ref[B:, :] = tail


def partial(lefts, rights, extra, bases, with_right=True):
    total = sum(x.shape[0] for x in lefts)
    operands = [*lefts, *rights, *extra, *bases]
    return pl.pallas_call(
        functools.partial(partial_body, len(lefts), len(extra), with_right),
        in_specs=[VM] * len(operands),
        out_specs=VM,
        out_shape=jax.ShapeDtypeStruct((PACK, B), F32),
        compiler_params=params(12),
        cost_estimate=cost(total * B * B * 8, total * B * 8),
    )(*operands)


def second_body(rows0, aliased, count, *refs):
    xs = refs[:count]
    rs = refs[count : 2 * count]
    wh_ref, wl_ref = refs[2 * count : 2 * count + 2]
    rest = refs[2 * count + 2 + (1 if aliased else 0) :]
    out = rest[0]
    ys = rest[1 : 1 + count]
    held, sem = rest[1 + count :]
    wh, wl = wh_ref[...], wl_ref[...]
    at = 0
    for x, r, y in zip(xs, rs, ys):
        size = x.shape[0]
        value = mixed(jnp.concatenate([x[...], r[...]], axis=1), wh, wl)
        held[at : at + size, :] = value[:, :B]
        y[...] = value[:, B:]
        at += size
    copy = pltpu.make_async_copy(held, out.at[pl.ds(rows0, at), pl.ds(0, B)], sem)
    copy.start()
    copy.wait()


def second(xs, rs, w, out, rows, rows0):
    total = sum(x.shape[0] for x in xs)
    shapes = [jax.ShapeDtypeStruct((rows, 2 * B), F32)] + [
        jax.ShapeDtypeStruct(x.shape, F32) for x in xs
    ]
    operands = [*xs, *rs, *w] + ([out] if out is not None else [])
    specs = [VM] * (2 * len(xs) + 2) + ([HBM] if out is not None else [])
    return pl.pallas_call(
        functools.partial(second_body, rows0, out is not None, len(xs)),
        in_specs=specs,
        out_specs=[HBM] + [VM] * len(xs),
        out_shape=shapes,
        scratch_shapes=[pltpu.VMEM((total, B), F32), pltpu.SemaphoreType.DMA],
        input_output_aliases={} if out is None else {len(operands) - 1: 0},
        compiler_params=params(12),
        cost_estimate=cost(6 * total * 256 * 256, total * B * 20),
    )(*operands)


def place_body(starts, *refs):
    count = len(starts)
    ys = refs[:count]
    out = refs[count + 1]
    sems = refs[count + 2]
    copies = []
    for n, (y, start) in enumerate(zip(ys, starts)):
        copies.append(
            pltpu.make_async_copy(
                y, out.at[pl.ds(start, y.shape[0]), pl.ds(B, B)], sems.at[n]
            )
        )
    for copy in copies:
        copy.start()
    for copy in copies:
        copy.wait()


def place(ys, starts, out):
    return pl.pallas_call(
        functools.partial(place_body, tuple(starts)),
        in_specs=[ANY] * len(ys) + [HBM],
        out_specs=HBM,
        out_shape=jax.ShapeDtypeStruct(out.shape, F32),
        scratch_shapes=[pltpu.SemaphoreType.DMA((len(ys),))],
        input_output_aliases={len(ys): 0},
        compiler_params=params(8),
        cost_estimate=cost(1, sum(y.size for y in ys) * 8),
    )(*ys, out)


def shifted(value, steps):
    count = lax.axis_size("blk")
    return lax.ppermute(value, "blk", [(s, (s + steps) % count) for s in range(count)])


def of_group(value):
    count = lax.axis_size("row")
    parts = [value]
    for mask in range(1, count):
        parts.append(lax.ppermute(value, "row", [(s, s ^ mask) for s in range(count)]))
    return parts


def moved(value, where):
    count = lax.axis_size("blk")
    return lax.ppermute(value, "blk", [(s, where(s)) for s in range(count)])


def of_all_pairs(values):
    count = lax.axis_size("blk")
    inner = 8 if count % 8 == 0 else count
    middle = 4 if count % (4 * inner) == 0 else 1

    def along_inner(steps):
        return lambda s: s // inner * inner + (s + steps) % inner

    def along_middle(steps):
        ring = inner * middle
        return lambda s: s // ring * ring + (s + steps * inner) % ring

    def gathered(tile, moves):
        for part in [moved(tile, where) for where in moves]:
            tile = jnp.maximum(tile, part)
        return tile

    lane = lax.broadcasted_iota(jnp.int32, (8, B), 1)
    at = STEPS * lax.axis_index("blk")
    tile = jnp.zeros((8, B), F32)
    for step, value in enumerate(values):
        tile = jnp.where(lane == at + step, value, tile)
    if middle > 1:
        tile = gathered(tile, [along_middle(n) for n in range(1, middle)])
    outer = count // (inner * middle)
    if outer > 1:
        tile = gathered(
            tile,
            [
                lambda s, n=n: (s + n * inner * middle) % count
                for n in range(1, outer)
            ],
        )
    reach = 1
    for width in (3, 1, 1):
        if reach >= inner:
            break
        if width == 3:
            tile = gathered(tile, [along_inner(-n) for n in range(1, min(4, inner))])
            reach = min(4, inner)
        else:
            step = min(3, inner - reach)
            tile = gathered(tile, [along_inner(-step)])
            reach += step
    return tile[0, : STEPS * count].reshape(count, STEPS)


def steps(matrix):
    rows = matrix.shape[0]
    unit = rows // UNITS
    front = [n * unit for n in FRONT]
    back = [n * unit for n in BACK]
    front_rows = sum(front)

    wh, wl, squares0 = roots(of_group(first_gram(matrix)))
    w = (wh, wl)

    xf, rf = update(matrix, w, 0, front[:1])
    xb, rb = update(matrix, w, front_rows, back)
    more_x, more_r = update(matrix, w, front[0], front[1:])
    xf, rf = [*xf, *more_x], [*rf, *more_r]

    got = [shifted(x, 1) for x in xf]
    behind = [shifted(r, -1) for r in rb]
    helped = shifted(partial(xb, behind, [], [], False), 1)
    got_back = [shifted(x, 1) for x in xb]

    cut = len(got) - 1
    sums = partial(got[:cut], rf[:cut], rb, [])
    sums = partial(got[cut:], rf[cut:], [], [sums, helped])
    wh, wl, squares1 = roots(of_group(sums))
    w = (wh, wl)

    out, *ys = second(got[:1], rf[:1], w, None, rows, 0)
    out, *more_y = second(got[1:], rf[1:], w, out, rows, front[0])
    out, *back_y = second(got_back, rb, w, out, rows, front_rows)
    ys = [*ys, *more_y, *back_y]
    arrived = [shifted(y, 1) for y in ys]

    totals = jnp.sum(of_all_pairs([squares0, squares1]), axis=0)
    off_measure = totals / float(lax.axis_size("blk"))
    places, at = [], 0
    for y in ys:
        places.append(at)
        at += y.shape[0]
    out = place(arrived, places, out)
    return out, off_measure


def solution(mesh):
    return jax.shard_map(
        steps,
        mesh=mesh,
        in_specs=(P("row", "blk"),),
        out_specs=(P("row", "blk"), P()),
        check_vma=False,
    )
```

profile of v0, /device:TPU:8, one launch (start us, length us, event | category | flops | bytes accessed | tf_op | source)
XLA Modules:
  0.0 144.8 jit_solution(14489614486546801556)
XLA Ops:
  0.6 3.8 %first_gram.1.a_ref = f32[136,128]{1,0:T(8,128)S(1)} custom-call(f32[4096,256]{1,0:T(8,128)} %m_ref.7), custom_call_target="tpu_custom_call" | custom-call | flops 536870912 | bytes 4194304 | tf_op jit(solution)/shard_map/first_gram/pallas_call | solution.py:94
  4.5 2.2 %collective-permute-start.1 = (f32[136,128]{1,0:T(8,128)S(1)}, f32[136,128]{1,0:T(8,128)S(1)}, u32[]{:S(2)}, u32[]{:S(2)}) collective-permute-start(f32[136,128]{1,0:T(8,128)S(1)} %first_gram.1.a_ref), channel_id=1, source_target_pairs={{0,128},{64,192},{128,0},{192,64},{1,129},{65,193},{129,1},{193,65... | collective-permute-start | bytes 208904 | tf_op jit(solution)/shard_map/ppermute | solution.py:326
  10.1 2.1 %roots.2 = (bf16[256,256]{1,0:T(8,128)(2,1)S(1)}, bf16[256,256]{1,0:T(8,128)(2,1)S(1)}, f32[8,128]{1,0:T(8,128)S(1)}) custom-call(f32[136,128]{1,0:T(8,128)S(1)} %first_gram.1.a_ref, f32[136,128]{1,0:T(8,128)S(1)} %collective-permute-done.b_ref, f32[136,128]{1,0:T(8,128)S(1)} %collective-permute-done.1.c_ref, f32[136,128]{1,0:T(8,128)S(1)} %collective-permute-done.2.d_ref), custom_call_target="tpu_custom_call" | custom-call | flops 30000000 | bytes 1000000 | tf_op jit(solution)/shard_map/roots/pallas_call | solution.py:154
  12.8 10.3 %collective-permute-start.9 = (f32[640,128]{1,0:T(8,128)S(1)}, f32[640,128]{1,0:T(8,128)S(1)}, u32[]{:S(2)}, u32[]{:S(2)}) collective-permute-start(f32[640,128]{1,0:T(8,128)S(1)} %get-tuple-element.49.refs_10_.refs_2_), channel_id=1, source_target_pairs={{0,63},{1,0},{2,1},{3,2},{4,3},{5,4},{6,5},{7,6},{8,7},{9,8},{10,9... | collective-permute-start | bytes 983048 | tf_op jit(solution)/shard_map/ppermute | solution.py:319
  27.5 7.8 %collective-permute-done.3.refs_0_ = f32[256,128]{1,0:T(8,128)S(1)} collective-permute-done((f32[256,128]{1,0:T(8,128)S(1)}, f32[256,128]{1,0:T(8,128)S(1)}, u32[]{:S(2)}, u32[]{:S(2)}) %collective-permute-start.3) | collective-permute-done | bytes 131104 | tf_op jit(solution)/shard_map/ppermute | solution.py:319
  35.3 2.1 %collective-permute-done.10.refs_3_ = f32[640,128]{1,0:T(8,128)S(1)} collective-permute-done((f32[640,128]{1,0:T(8,128)S(1)}, f32[640,128]{1,0:T(8,128)S(1)}, u32[]{:S(2)}, u32[]{:S(2)}) %collective-permute-start.10) | collective-permute-done | bytes 327712 | tf_op jit(solution)/shard_map/ppermute | solution.py:319
  38.4 3.9 %collective-permute-done.5.refs_1_.refs_0_ = f32[512,128]{1,0:T(8,128)S(1)} collective-permute-done((f32[512,128]{1,0:T(8,128)S(1)}, f32[512,128]{1,0:T(8,128)S(1)}, u32[]{:S(2)}, u32[]{:S(2)}) %collective-permute-start.5) | collective-permute-done | bytes 262176 | tf_op jit(solution)/shard_map/ppermute | solution.py:319
  42.4 5.6 %collective-permute-done.6.refs_2_.refs_1_ = f32[512,128]{1,0:T(8,128)S(1)} collective-permute-done((f32[512,128]{1,0:T(8,128)}, f32[512,128]{1,0:T(8,128)S(1)}, u32[]{:S(2)}, u32[]{:S(2)}) %collective-permute-start.6) | collective-permute-done | bytes 262176 | tf_op jit(solution)/shard_map/ppermute | solution.py:319
  48.0 5.6 %collective-permute-done.7.refs_3_.refs_2_ = f32[512,128]{1,0:T(8,128)S(1)} collective-permute-done((f32[512,128]{1,0:T(8,128)}, f32[512,128]{1,0:T(8,128)S(1)}, u32[]{:S(2)}, u32[]{:S(2)}) %collective-permute-start.7) | collective-permute-done | bytes 262176 | tf_op jit(solution)/shard_map/ppermute | solution.py:319
  53.6 5.6 %collective-permute-done.8.refs_4_.refs_3_ = f32[512,128]{1,0:T(8,128)S(1)} collective-permute-done((f32[512,128]{1,0:T(8,128)}, f32[512,128]{1,0:T(8,128)S(1)}, u32[]{:S(2)}, u32[]{:S(2)}) %collective-permute-start.8) | collective-permute-done | bytes 262176 | tf_op jit(solution)/shard_map/ppermute | solution.py:319
  59.8 4.2 %collective-permute-done.4.refs_0_.refs_4_ = f32[512,128]{1,0:T(8,128)S(1)} collective-permute-done((f32[512,128]{1,0:T(8,128)}, f32[512,128]{1,0:T(8,128)S(1)}, u32[]{:S(2)}, u32[]{:S(2)}) %collective-permute-start.4) | collective-permute-done | bytes 262176 | tf_op jit(solution)/shard_map/ppermute | solution.py:319
  68.0 2.6 %collective-permute-done.14.d_ref = f32[136,128]{1,0:T(8,128)S(1)} collective-permute-done((f32[136,128]{1,0:T(8,128)S(1)}, f32[136,128]{1,0:T(8,128)S(1)}, u32[]{:S(2)}, u32[]{:S(2)}) %collective-permute-start.14) | collective-permute-done | bytes 69664 | tf_op jit(solution)/shard_map/ppermute | solution.py:326
  71.9 2.1 %roots.3 = (bf16[256,256]{1,0:T(8,128)(2,1)S(1)}, bf16[256,256]{1,0:T(8,128)(2,1)S(1)}, f32[8,128]{1,0:T(8,128)S(1)}) custom-call(f32[136,128]{1,0:T(8,128)S(1)} %shard_map.35.a_ref, f32[136,128]{1,0:T(8,128)S(1)} %collective-permute-done.12.b_ref, f32[136,128]{1,0:T(8,128)S(1)} %collective-permute-done.13.c_ref, f32[136,128]{1,0:T(8,128)S(1)} %collective-permute-done.14.d_ref), custom_call_target="tpu_custom_call" | custom-call | flops 30000000 | bytes 1000000 | tf_op jit(solution)/shard_map/roots/pallas_call | solution.py:154
  81.9 4.0 %collective-permute-done.28 = f32[8,128]{1,0:T(8,128)S(1)} collective-permute-done((f32[8,128]{1,0:T(8,128)S(1)}, f32[8,128]{1,0:T(8,128)S(1)}, u32[]{:S(2)}, u32[]{:S(2)}) %collective-permute-start.28) | collective-permute-done | bytes 4128 | tf_op jit(solution)/shard_map/ppermute | solution.py:332
  87.0 3.2 %shard_map.37 = (f32[4096,256]{1,0:T(8,128)}, f32[512,128]{1,0:T(8,128)S(1)}, f32[512,128]{1,0:T(8,128)S(1)}, f32[512,128]{1,0:T(8,128)}, f32[512,128]{1,0:T(8,128)}, /*index=5*/f32[512,128]{1,0:T(8,128)}) custom-call(f32[512,128]{1,0:T(8,128)S(1)} %collective-permute-done.5.refs_1_.refs_0_, ...), custom_call_target="tpu_custom_call", output_to_operand_aliasing={{0}: (12, {})} | custom-call | flops 1006632960 | bytes 6553600 | tf_op jit(solution)/shard_map/pallas_call | solution.py:274
  94.0 4.1 %collective-permute-start.32 = (f32[8,128]{1,0:T(8,128)S(1)}, f32[8,128]{1,0:T(8,128)S(1)}, u32[]{:S(2)}, u32[]{:S(2)}) collective-permute-start(f32[8,128]{1,0:T(8,128)S(1)} %maximum_maximum_fusion), channel_id=1, source_target_pairs={{0,5},{1,6},{2,7},{3,0},{4,1},{5,2},{6,3},{7,4},{8,13},{9,14},{10,... | collective-permute-start | bytes 12296 | tf_op jit(solution)/shard_map/ppermute | solution.py:332
  99.6 2.6 %collective-permute-start.15 = (f32[256,128]{1,0:T(8,128)S(1)}, f32[256,128]{1,0:T(8,128)S(1)}, u32[]{:S(2)}, u32[]{:S(2)}) collective-permute-start(f32[256,128]{1,0:T(8,128)S(1)} %get-tuple-element.55), channel_id=1, source_target_pairs={{0,1},{1,2},{2,3},{3,4},{4,5},{5,6},{6,7},{7,8},{8,9},{9,10},{10,1... | collective-permute-start | bytes 393224 | tf_op jit(solution)/shard_map/ppermute | solution.py:319
  102.2 3.2 %collective-permute-start.18 = (f32[512,128]{1,0:T(8,128)}, f32[512,128]{1,0:T(8,128)S(1)}, u32[]{:S(2)}, u32[]{:S(2)}) collective-permute-start(f32[512,128]{1,0:T(8,128)} %get-tuple-element.59), channel_id=1, source_target_pairs={{0,1},{1,2},{2,3},{3,4},{4,5},{5,6},{6,7},{7,8},{8,9},{9,10},{10,1... | collective-permute-start | bytes 786440 | tf_op jit(solution)/shard_map/ppermute | solution.py:319
  109.3 5.3 %collective-permute-done.15.refs_0_ = f32[256,128]{1,0:T(8,128)S(1)} collective-permute-done((f32[256,128]{1,0:T(8,128)S(1)}, f32[256,128]{1,0:T(8,128)S(1)}, u32[]{:S(2)}, u32[]{:S(2)}) %collective-permute-start.15) | collective-permute-done | bytes 131104 | tf_op jit(solution)/shard_map/ppermute | solution.py:319
  115.5 4.8 %collective-permute-done.18.refs_3_ = f32[512,128]{1,0:T(8,128)S(1)} collective-permute-done((f32[512,128]{1,0:T(8,128)}, f32[512,128]{1,0:T(8,128)S(1)}, u32[]{:S(2)}, u32[]{:S(2)}) %collective-permute-start.18) | collective-permute-done | bytes 262176 | tf_op jit(solution)/shard_map/ppermute | solution.py:319
  120.3 5.6 %collective-permute-done.19.refs_4_ = f32[512,128]{1,0:T(8,128)S(1)} collective-permute-done((f32[512,128]{1,0:T(8,128)}, f32[512,128]{1,0:T(8,128)S(1)}, u32[]{:S(2)}, u32[]{:S(2)}) %collective-permute-start.19) | collective-permute-done | bytes 262176 | tf_op jit(solution)/shard_map/ppermute | solution.py:319
  125.9 5.6 %collective-permute-done.20.refs_5_ = f32[512,128]{1,0:T(8,128)S(1)} collective-permute-done((f32[512,128]{1,0:T(8,128)}, f32[512,128]{1,0:T(8,128)S(1)}, u32[]{:S(2)}, u32[]{:S(2)}) %collective-permute-start.20) | collective-permute-done | bytes 262176 | tf_op jit(solution)/shard_map/ppermute | solution.py:319
  131.5 7.0 %collective-permute-done.23.refs_6_ = f32[640,128]{1,0:T(8,128)S(1)} collective-permute-done((f32[640,128]{1,0:T(8,128)S(1)}, f32[640,128]{1,0:T(8,128)S(1)}, u32[]{:S(2)}, u32[]{:S(2)}) %collective-permute-start.23) | collective-permute-done | bytes 327712 | tf_op jit(solution)/shard_map/ppermute | solution.py:319
  138.5 4.7 %collective-permute-done.24.refs_7_ = f32[640,128]{1,0:T(8,128)S(1)} collective-permute-done((f32[640,128]{1,0:T(8,128)S(1)}, f32[640,128]{1,0:T(8,128)S(1)}, u32[]{:S(2)}, u32[]{:S(2)}) %collective-permute-start.24) | collective-permute-done | bytes 327712 | tf_op jit(solution)/shard_map/ppermute | solution.py:319
  (74 shorter events, 35.9 us)
Async XLA Ops:
  4.5 5.6 %collective-permute-start.1 = (f32[136,128]{1,0:T(8,128)S(1)}, f32[136,128]{1,0:T(8,128)S(1)}, u32[]{:S(2)}, u32[]{:S(2)}) collective-permute-start(f32[136,128]{1,0:T(8,128)S(1)} %first_gram.1.a_ref), channel_id=1, source_target_pairs={{0,128},{64,192},{128,0},{192,64},{1,129},{65,193},{129,1},{193,65... | collective-permute-start | bytes 208904 | tf_op jit(solution)/shard_map/ppermute | solution.py:326
  12.8 22.4 %collective-permute-start.9 = (f32[640,128]{1,0:T(8,128)S(1)}, f32[640,128]{1,0:T(8,128)S(1)}, u32[]{:S(2)}, u32[]{:S(2)}) collective-permute-start(f32[640,128]{1,0:T(8,128)S(1)} %get-tuple-element.49.refs_10_.refs_2_), channel_id=1, source_target_pairs={{0,63},{1,0},{2,1},{3,2},{4,3},{5,4},{6,5},{7,6},{8,7},{9,8},{10,9... | collective-permute-start | bytes 983048 | tf_op jit(solution)/shard_map/ppermute | solution.py:319
  23.1 14.3 %collective-permute-start.10 = (f32[640,128]{1,0:T(8,128)S(1)}, f32[640,128]{1,0:T(8,128)S(1)}, u32[]{:S(2)}, u32[]{:S(2)}) collective-permute-start(f32[640,128]{1,0:T(8,128)S(1)} %get-tuple-element.50.refs_11_.refs_3_), channel_id=1, source_target_pairs={{0,63},{1,0},{2,1},{3,2},{4,3},{5,4},{6,5},{7,6},{8,7},{9,8},{10,9... | collective-permute-start | bytes 983048 | tf_op jit(solution)/shard_map/ppermute | solution.py:319
  24.4 10.9 %collective-permute-start.3 = (f32[256,128]{1,0:T(8,128)S(1)}, f32[256,128]{1,0:T(8,128)S(1)}, u32[]{:S(2)}, u32[]{:S(2)}) collective-permute-start(f32[256,128]{1,0:T(8,128)S(1)} %get-tuple-element.37), channel_id=1, source_target_pairs={{0,1},{1,2},{2,3},{3,4},{4,5},{5,6},{6,7},{7,8},{8,9},{9,10},{10,1... | collective-permute-start | bytes 393224 | tf_op jit(solution)/shard_map/ppermute | solution.py:319
  27.5 14.9 %collective-permute-start.5 = (f32[512,128]{1,0:T(8,128)S(1)}, f32[512,128]{1,0:T(8,128)S(1)}, u32[]{:S(2)}, u32[]{:S(2)}) collective-permute-start(f32[512,128]{1,0:T(8,128)S(1)} %get-tuple-element.41), channel_id=1, source_target_pairs={{0,1},{1,2},{2,3},{3,4},{4,5},{5,6},{6,7},{7,8},{8,9},{9,10},{10,1... | collective-permute-start | bytes 786440 | tf_op jit(solution)/shard_map/ppermute | solution.py:319
  27.5 20.5 %collective-permute-start.6 = (f32[512,128]{1,0:T(8,128)}, f32[512,128]{1,0:T(8,128)S(1)}, u32[]{:S(2)}, u32[]{:S(2)}) collective-permute-start(f32[512,128]{1,0:T(8,128)} %get-tuple-element.42), channel_id=1, source_target_pairs={{0,1},{1,2},{2,3},{3,4},{4,5},{5,6},{6,7},{7,8},{8,9},{9,10},{10,1... | collective-permute-start | bytes 786440 | tf_op jit(solution)/shard_map/ppermute | solution.py:319
  35.3 18.3 %collective-permute-start.7 = (f32[512,128]{1,0:T(8,128)}, f32[512,128]{1,0:T(8,128)S(1)}, u32[]{:S(2)}, u32[]{:S(2)}) collective-permute-start(f32[512,128]{1,0:T(8,128)} %get-tuple-element.43), channel_id=1, source_target_pairs={{0,1},{1,2},{2,3},{3,4},{4,5},{5,6},{6,7},{7,8},{8,9},{9,10},{10,1... | collective-permute-start | bytes 786440 | tf_op jit(solution)/shard_map/ppermute | solution.py:319
  35.3 23.9 %collective-permute-start.8 = (f32[512,128]{1,0:T(8,128)}, f32[512,128]{1,0:T(8,128)S(1)}, u32[]{:S(2)}, u32[]{:S(2)}) collective-permute-start(f32[512,128]{1,0:T(8,128)} %get-tuple-element.44), channel_id=1, source_target_pairs={{0,1},{1,2},{2,3},{3,4},{4,5},{5,6},{6,7},{7,8},{8,9},{9,10},{10,1... | collective-permute-start | bytes 786440 | tf_op jit(solution)/shard_map/ppermute | solution.py:319
  37.4 26.6 %collective-permute-start.4 = (f32[512,128]{1,0:T(8,128)}, f32[512,128]{1,0:T(8,128)S(1)}, u32[]{:S(2)}, u32[]{:S(2)}) collective-permute-start(f32[512,128]{1,0:T(8,128)} %get-tuple-element.39), channel_id=1, source_target_pairs={{0,1},{1,2},{2,3},{3,4},{4,5},{5,6},{6,7},{7,8},{8,9},{9,10},{10,1... | collective-permute-start | bytes 786440 | tf_op jit(solution)/shard_map/ppermute | solution.py:319
  42.4 22.5 %collective-permute-start.11 = (f32[136,128]{1,0:T(8,128)}, f32[136,128]{1,0:T(8,128)}, u32[]{:S(2)}, u32[]{:S(2)}) collective-permute-start(f32[136,128]{1,0:T(8,128)} %shard_map.34), channel_id=1, source_target_pairs={{0,1},{1,2},{2,3},{3,4},{4,5},{5,6},{6,7},{7,8},{8,9},{9,10},{10,1... | collective-permute-start | bytes 208904 | tf_op jit(solution)/shard_map/ppermute | solution.py:319
  66.1 5.8 %collective-permute-start.13 = (f32[136,128]{1,0:T(8,128)S(1)}, f32[136,128]{1,0:T(8,128)S(1)}, u32[]{:S(2)}, u32[]{:S(2)}) collective-permute-start(f32[136,128]{1,0:T(8,128)S(1)} %shard_map.35.a_ref), channel_id=1, source_target_pairs={{0,128},{64,192},{128,0},{192,64},{1,129},{65,193},{129,1},{193,65... | collective-permute-start | bytes 208904 | tf_op jit(solution)/shard_map/ppermute | solution.py:326
  74.2 6.2 %collective-permute-start.25 = (f32[8,128]{1,0:T(8,128)S(1)}, f32[8,128]{1,0:T(8,128)S(1)}, u32[]{:S(2)}, u32[]{:S(2)}) collective-permute-start(f32[8,128]{1,0:T(8,128)S(1)} %select_select_fusion), channel_id=1, source_target_pairs={{0,8},{1,9},{2,10},{3,11},{4,12},{5,13},{6,14},{7,15},{8,16},{9,17... | collective-permute-start | bytes 12296 | tf_op jit(solution)/shard_map/ppermute | solution.py:332
  76.1 26.1 %collective-permute-start.21 = (f32[640,128]{1,0:T(8,128)}, f32[640,128]{1,0:T(8,128)S(1)}, u32[]{:S(2)}, u32[]{:S(2)}) collective-permute-start(f32[640,128]{1,0:T(8,128)} %copy-done.2), channel_id=1, source_target_pairs={{0,1},{1,2},{2,3},{3,4},{4,5},{5,6},{6,7},{7,8},{8,9},{9,10},{10,1... | collective-permute-start | bytes 983048 | tf_op jit(solution)/shard_map/ppermute | solution.py:319
  76.1 29.3 %collective-permute-start.22 = (f32[640,128]{1,0:T(8,128)}, f32[640,128]{1,0:T(8,128)S(1)}, u32[]{:S(2)}, u32[]{:S(2)}) collective-permute-start(f32[640,128]{1,0:T(8,128)} %copy-done.1), channel_id=1, source_target_pairs={{0,1},{1,2},{2,3},{3,4},{4,5},{5,6},{6,7},{7,8},{8,9},{9,10},{10,1... | collective-permute-start | bytes 983048 | tf_op jit(solution)/shard_map/ppermute | solution.py:319
  85.9 6.7 %collective-permute-start.30 = (f32[8,128]{1,0:T(8,128)S(1)}, f32[8,128]{1,0:T(8,128)S(1)}, u32[]{:S(2)}, u32[]{:S(2)}) collective-permute-start(f32[8,128]{1,0:T(8,128)S(1)} %max.30), channel_id=1, source_target_pairs={{0,6},{1,7},{2,0},{3,1},{4,2},{5,3},{6,4},{7,5},{8,14},{9,15},{10,... | collective-permute-start | bytes 12296 | tf_op jit(solution)/shard_map/ppermute | solution.py:332
  87.0 7.0 %collective-permute-start.29 = (f32[8,128]{1,0:T(8,128)S(1)}, f32[8,128]{1,0:T(8,128)S(1)}, u32[]{:S(2)}, u32[]{:S(2)}) collective-permute-start(f32[8,128]{1,0:T(8,128)S(1)} %max.30), channel_id=1, source_target_pairs={{0,7},{1,0},{2,1},{3,2},{4,3},{5,4},{6,5},{7,6},{8,15},{9,8},{10,9... | collective-permute-start | bytes 12296 | tf_op jit(solution)/shard_map/ppermute | solution.py:332
  91.3 23.4 %collective-permute-start.16 = (f32[512,128]{1,0:T(8,128)S(1)}, f32[512,128]{1,0:T(8,128)S(1)}, u32[]{:S(2)}, u32[]{:S(2)}) collective-permute-start(f32[512,128]{1,0:T(8,128)S(1)} %get-tuple-element.57), channel_id=1, source_target_pairs={{0,1},{1,2},{2,3},{3,4},{4,5},{5,6},{6,7},{7,8},{8,9},{9,10},{10,1... | collective-permute-start | bytes 786440 | tf_op jit(solution)/shard_map/ppermute | solution.py:319
  92.5 22.1 %collective-permute-start.17 = (f32[512,128]{1,0:T(8,128)S(1)}, f32[512,128]{1,0:T(8,128)S(1)}, u32[]{:S(2)}, u32[]{:S(2)}) collective-permute-start(f32[512,128]{1,0:T(8,128)S(1)} %get-tuple-element.58), channel_id=1, source_target_pairs={{0,1},{1,2},{2,3},{3,4},{4,5},{5,6},{6,7},{7,8},{8,9},{9,10},{10,1... | collective-permute-start | bytes 786440 | tf_op jit(solution)/shard_map/ppermute | solution.py:319
  99.6 15.1 %collective-permute-start.15 = (f32[256,128]{1,0:T(8,128)S(1)}, f32[256,128]{1,0:T(8,128)S(1)}, u32[]{:S(2)}, u32[]{:S(2)}) collective-permute-start(f32[256,128]{1,0:T(8,128)S(1)} %get-tuple-element.55), channel_id=1, source_target_pairs={{0,1},{1,2},{2,3},{3,4},{4,5},{5,6},{6,7},{7,8},{8,9},{9,10},{10,1... | collective-permute-start | bytes 393224 | tf_op jit(solution)/shard_map/ppermute | solution.py:319
  102.2 18.1 %collective-permute-start.18 = (f32[512,128]{1,0:T(8,128)}, f32[512,128]{1,0:T(8,128)S(1)}, u32[]{:S(2)}, u32[]{:S(2)}) collective-permute-start(f32[512,128]{1,0:T(8,128)} %get-tuple-element.59), channel_id=1, source_target_pairs={{0,1},{1,2},{2,3},{3,4},{4,5},{5,6},{6,7},{7,8},{8,9},{9,10},{10,1... | collective-permute-start | bytes 786440 | tf_op jit(solution)/shard_map/ppermute | solution.py:319
  109.0 16.8 %collective-permute-start.19 = (f32[512,128]{1,0:T(8,128)}, f32[512,128]{1,0:T(8,128)S(1)}, u32[]{:S(2)}, u32[]{:S(2)}) collective-permute-start(f32[512,128]{1,0:T(8,128)} %get-tuple-element.60), channel_id=1, source_target_pairs={{0,1},{1,2},{2,3},{3,4},{4,5},{5,6},{6,7},{7,8},{8,9},{9,10},{10,1... | collective-permute-start | bytes 786440 | tf_op jit(solution)/shard_map/ppermute | solution.py:319
  114.6 16.9 %collective-permute-start.20 = (f32[512,128]{1,0:T(8,128)}, f32[512,128]{1,0:T(8,128)S(1)}, u32[]{:S(2)}, u32[]{:S(2)}) collective-permute-start(f32[512,128]{1,0:T(8,128)} %get-tuple-element.61), channel_id=1, source_target_pairs={{0,1},{1,2},{2,3},{3,4},{4,5},{5,6},{6,7},{7,8},{8,9},{9,10},{10,1... | collective-permute-start | bytes 786440 | tf_op jit(solution)/shard_map/ppermute | solution.py:319
  114.6 23.9 %collective-permute-start.23 = (f32[640,128]{1,0:T(8,128)S(1)}, f32[640,128]{1,0:T(8,128)S(1)}, u32[]{:S(2)}, u32[]{:S(2)}) collective-permute-start(f32[640,128]{1,0:T(8,128)S(1)} %get-tuple-element.63), channel_id=1, source_target_pairs={{0,1},{1,2},{2,3},{3,4},{4,5},{5,6},{6,7},{7,8},{8,9},{9,10},{10,1... | collective-permute-start | bytes 983048 | tf_op jit(solution)/shard_map/ppermute | solution.py:319
  114.7 28.5 %collective-permute-start.24 = (f32[640,128]{1,0:T(8,128)S(1)}, f32[640,128]{1,0:T(8,128)S(1)}, u32[]{:S(2)}, u32[]{:S(2)}) collective-permute-start(f32[640,128]{1,0:T(8,128)S(1)} %get-tuple-element.64), channel_id=1, source_target_pairs={{0,1},{1,2},{2,3},{3,4},{4,5},{5,6},{6,7},{7,8},{8,9},{9,10},{10,1... | collective-permute-start | bytes 983048 | tf_op jit(solution)/shard_map/ppermute | solution.py:319
  (13 other events, 105.6 us)
where the time goes:
time: 145 us
  waiting for transfers between devices  86.8 us (60%)
  starting transfers between devices  35.6 us (25%)
  Pallas kernels  20.7 us (14%)
    ppermute x19, waiting for transfers between devices, shifted(): lax.ppermute(value, 'blk', [(s, (s + steps) % count) for s in range(count)])  68.7 us
    ppermute x19, starting transfers between devices, shifted(): lax.ppermute(value, 'blk', [(s, (s + steps) % count) for s in range(count)])  21.4 us
    ppermute x9, waiting for transfers between devices, moved(): return lax.ppermute(value, 'blk', [(s, where(s)) for s in range(count)])  10.9 us
    ppermute x9, starting transfers between devices, moved(): return lax.ppermute(value, 'blk', [(s, where(s)) for s in range(count)])  9.88 us
    ppermute x6, waiting for transfers between devices, of_group(): lax.ppermute(value, 'row', [(s, s ^ mask) for s in range(count)])  7.21 us
    pallas_call x3, Pallas kernels, second(): pl.pallas_call(functools.partial(second_body, rows0, out is not None, len...  5.63 us
    ppermute x6, starting transfers between devices, of_group(): lax.ppermute(value, 'row', [(s, s ^ mask) for s in range(count)])  4.29 us
    pallas_call x2, Pallas kernels, roots(): pl.pallas_call(root_body, in_specs=[VM] * 4, out_specs=[VM] * 3, out_shap...  4.14 us
  transfers between devices with their start and end apart: 34, of which 25 were waited for; matrix products, arithmetic and copies ran while one was open for 0% of the time, Pallas kernels for 7%

commit v1 on v0

--- a/solution.py
+++ b/solution.py
@@ -13,8 +13,8 @@
 B = 128
 PACK = 136
 UNITS = 32
-FRONT = (2, 4, 4, 4, 4, 4)
-BACK = (5, 5)
+FRONT = (4, 4, 4, 4, 4, 2)
+BACK = (5, 3, 2)
 
 VM = pl.BlockSpec(memory_space=pltpu.VMEM)
 ANY = pl.BlockSpec(memory_space=pl.ANY)
@@ -108,8 +108,8 @@
     )(matrix)
 
 
-def root_body(a_ref, b_ref, c_ref, d_ref, wh_ref, wl_ref, s_ref):
-    total = (a_ref[...] + b_ref[...]) + (c_ref[...] + d_ref[...])
+def root_body(a_ref, b_ref, wh_ref, wl_ref, s_ref):
+    total = a_ref[...] + b_ref[...]
     inverse = lax.rsqrt(total[B : B + 8, :])
     first = jnp.broadcast_to(inverse[0:1, :], (B, B)).T
     cosines = total[:B, :] * first * inverse[1:2, :]
@@ -153,7 +153,7 @@
 def roots(parts):
     return pl.pallas_call(
         root_body,
-        in_specs=[VM] * 4,
+        in_specs=[VM] * 2,
         out_specs=[VM] * 3,
         out_shape=[
             jax.ShapeDtypeStruct((2 * B, 2 * B), BF16),
@@ -304,7 +304,7 @@
 def place(ys, starts, out):
     return pl.pallas_call(
         functools.partial(place_body, tuple(starts)),
-        in_specs=[ANY] * len(ys) + [HBM],
+        in_specs=[VM] * len(ys) + [HBM],
         out_specs=HBM,
         out_shape=jax.ShapeDtypeStruct(out.shape, F32),
         scratch_shapes=[pltpu.SemaphoreType.DMA((len(ys),))],
@@ -321,10 +321,15 @@
 
 def of_group(value):
     count = lax.axis_size("row")
-    parts = [value]
-    for mask in range(1, count):
-        parts.append(lax.ppermute(value, "row", [(s, s ^ mask) for s in range(count)]))
-    return parts
+
+    def from_other(part, mask):
+        return lax.ppermute(part, "row", [(s, s ^ mask) for s in range(count)])
+
+    mask = 1
+    while 2 * mask < count:
+        value = value + from_other(value, mask)
+        mask *= 2
+    return value, from_other(value, mask)
 
 
 def moved(value, where):
@@ -354,28 +359,18 @@
     tile = jnp.zeros((8, B), F32)
     for step, value in enumerate(values):
         tile = jnp.where(lane == at + step, value, tile)
-    if middle > 1:
-        tile = gathered(tile, [along_middle(n) for n in range(1, middle)])
+    reach = min(4, inner)
+    if inner > 1:
+        tile = gathered(tile, [along_inner(-n) for n in range(1, reach)])
+    while reach < inner:
+        step = min(3, inner - reach)
+        tile = gathered(tile, [along_inner(-step)])
+        reach += step
+    for _ in range(1, middle):
+        tile = gathered(tile, [along_middle(-1)])
     outer = count // (inner * middle)
-    if outer > 1:
-        tile = gathered(
-            tile,
-            [
-                lambda s, n=n: (s + n * inner * middle) % count
-                for n in range(1, outer)
-            ],
-        )
-    reach = 1
-    for width in (3, 1, 1):
-        if reach >= inner:
-            break
-        if width == 3:
-            tile = gathered(tile, [along_inner(-n) for n in range(1, min(4, inner))])
-            reach = min(4, inner)
-        else:
-            step = min(3, inner - reach)
-            tile = gathered(tile, [along_inner(-step)])
-            reach += step
+    for n in range(1, outer):
+        tile = gathered(tile, [lambda s, n=n: (s + n * inner * middle) % count])
     return tile[0, : STEPS * count].reshape(count, STEPS)
 
 
@@ -390,8 +385,8 @@
     w = (wh, wl)
 
     xf, rf = update(matrix, w, 0, front[:1])
+    more_x, more_r = update(matrix, w, front[0], front[1:])
     xb, rb = update(matrix, w, front_rows, back)
-    more_x, more_r = update(matrix, w, front[0], front[1:])
     xf, rf = [*xf, *more_x], [*rf, *more_r]
 
     got = [shifted(x, 1) for x in xf]
@@ -417,7 +412,8 @@
     for y in ys:
         places.append(at)
         at += y.shape[0]
-    out = place(arrived, places, out)
+    for lo, hi in ((0, 6), (6, 8), (8, 9)):
+        out = place(arrived[lo:hi], places[lo:hi], out)
     return out, off_measure
 
 

time: 145 us -> 149 us (1.028)
  starting transfers between devices: 35.6 us -> 56.3 us
  waiting for transfers between devices: 86.8 us -> 68 us
    ppermute x19 -> x22, waiting for transfers between devices: 68.7 us -> 52.9 us  [shifted(): lax.ppermute(value, 'blk', [(s, (s + steps) % count) for s in range(count)])]
    ppermute x19 -> x22, starting transfers between devices: 21.4 us -> 32.3 us  [shifted(): lax.ppermute(value, 'blk', [(s, (s + steps) % count) for s in range(count)])]
    ppermute x9, starting transfers between devices: 9.88 us -> 20.2 us  [moved(): return lax.ppermute(value, 'blk', [(s, where(s)) for s in range(count)])]
    ppermute x9, waiting for transfers between devices: 10.9 us -> 6.8 us  [moved(): return lax.ppermute(value, 'blk', [(s, where(s)) for s in range(count)])]
    pallas_call x3 -> x5, Pallas kernels: 5.52 us -> 6.74 us  [the longest x2 4.13 us: roots(): pl.pallas_call(root_body, in_specs=[VM] * 2, out_specs=[VM] * 3, out_shap...]
    ppermute x6 -> x4, waiting for transfers between devices: 7.21 us -> 8.21 us  [from_other(): return lax.ppermute(part, 'row', [(s, s ^ mask) for s in range(count)])]
    ppermute x6 -> x4, starting transfers between devices: 4.29 us -> 3.77 us  [from_other(): return lax.ppermute(part, 'row', [(s, s ^ mask) for s in range(count)])]
  transfers between devices with their start and end apart: 34 -> 35, of which waited for: 25 -> 20; matrix products, arithmetic and copies ran while one was open for 0% -> 0% of each run, Pallas kernels for 7% -> 9%
where the time goes in v1:
time: 149 us; the launch traced here: 148 us
  waiting for transfers between devices  68 us (46%)
  starting transfers between devices  56.3 us (38%)
  Pallas kernels  21 us (14%)
  other arithmetic  1.51 us (1%)
    ppermute x22, waiting for transfers between devices, shifted(): lax.ppermute(value, 'blk', [(s, (s + steps) % count) for s in range(count)])  52.9 us
    ppermute x22, starting transfers between devices, shifted(): lax.ppermute(value, 'blk', [(s, (s + steps) % count) for s in range(count)])  32.3 us
    ppermute x9, starting transfers between devices, moved(): return lax.ppermute(value, 'blk', [(s, where(s)) for s in range(count)])  20.2 us
    ppermute x4, waiting for transfers between devices, from_other(): return lax.ppermute(part, 'row', [(s, s ^ mask) for s in range(count)])  8.21 us
    ppermute x9, waiting for transfers between devices, moved(): return lax.ppermute(value, 'blk', [(s, where(s)) for s in range(count)])  6.8 us
    pallas_call x3, Pallas kernels, second(): pl.pallas_call(functools.partial(second_body, rows0, out is not None, len...  6.39 us
    pallas_call x2, Pallas kernels, roots(): pl.pallas_call(root_body, in_specs=[VM] * 2, out_specs=[VM] * 3, out_shap...  4.13 us
    ppermute x4, starting transfers between devices, from_other(): return lax.ppermute(part, 'row', [(s, s ^ mask) for s in range(count)])  3.77 us
  transfers between devices with their start and end apart: 35, of which 20 were waited for; matrix products, arithmetic and copies ran while one was open for 0% of the time, Pallas kernels for 9%

profile of v1, /device:TPU:8, one launch (start us, length us, event | category | flops | bytes accessed | tf_op | source)
XLA Modules:
  0.0 148.0 jit_solution(7451127314886318882)
XLA Ops:
  0.6 3.8 %first_gram.1 = f32[136,128]{1,0:T(8,128)S(1)} custom-call(f32[4096,256]{1,0:T(8,128)} %m_ref.7), custom_call_target="tpu_custom_call" | custom-call | flops 536870912 | bytes 4194304 | tf_op jit(solution)/shard_map/first_gram/pallas_call | solution.py:94
  5.8 2.2 %collective-permute-start.1 = (f32[136,128]{1,0:T(8,128)S(1)}, f32[136,128]{1,0:T(8,128)S(1)}, u32[]{:S(2)}, u32[]{:S(2)}) collective-permute-start(f32[136,128]{1,0:T(8,128)S(1)} %add.9.a_ref), channel_id=1, source_target_pairs={{0,128},{64,192},{128,0},{192,64},{1,129},{65,193},{129,1},{193,65... | collective-permute-start | bytes 208904 | tf_op jit(solution)/shard_map/ppermute | solution.py:326
  8.0 2.5 %collective-permute-done.1.b_ref = f32[136,128]{1,0:T(8,128)S(1)} collective-permute-done((f32[136,128]{1,0:T(8,128)S(1)}, f32[136,128]{1,0:T(8,128)S(1)}, u32[]{:S(2)}, u32[]{:S(2)}) %collective-permute-start.1) | collective-permute-done | bytes 69664 | tf_op jit(solution)/shard_map/ppermute | solution.py:326
  10.5 2.1 %roots.2 = (bf16[256,256]{1,0:T(8,128)(2,1)S(1)}, bf16[256,256]{1,0:T(8,128)(2,1)S(1)}, f32[8,128]{1,0:T(8,128)S(1)}) custom-call(f32[136,128]{1,0:T(8,128)S(1)} %add.9.a_ref, f32[136,128]{1,0:T(8,128)S(1)} %collective-permute-done.1.b_ref), custom_call_target="tpu_custom_call" | custom-call | flops 30000000 | bytes 1000000 | tf_op jit(solution)/shard_map/roots/pallas_call | solution.py:154
  15.3 8.0 %collective-permute-start.12 = (f32[384,128]{1,0:T(8,128)S(1)}, f32[384,128]{1,0:T(8,128)S(1)}, u32[]{:S(2)}, u32[]{:S(2)}) collective-permute-start(f32[384,128]{1,0:T(8,128)S(1)} %get-tuple-element.44.refs_11_.refs_4_), channel_id=1, source_target_pairs={{0,63},{1,0},{2,1},{3,2},{4,3},{5,4},{6,5},{7,6},{8,7},{9,8},{10,9... | collective-permute-start | bytes 589832 | tf_op jit(solution)/shard_map/ppermute | solution.py:319
  28.5 8.0 %collective-permute-done.13.refs_5_ = f32[256,128]{1,0:T(8,128)S(1)} collective-permute-done((f32[256,128]{1,0:T(8,128)S(1)}, f32[256,128]{1,0:T(8,128)S(1)}, u32[]{:S(2)}, u32[]{:S(2)}) %collective-permute-start.13) | collective-permute-done | bytes 131104 | tf_op jit(solution)/shard_map/ppermute | solution.py:319
  36.5 2.5 %collective-permute-start.10 = (f32[512,128]{1,0:T(8,128)S(1)}, f32[512,128]{1,0:T(8,128)S(1)}, u32[]{:S(2)}, u32[]{:S(2)}) collective-permute-start(f32[512,128]{1,0:T(8,128)S(1)} %get-tuple-element.52), channel_id=1, source_target_pairs={{0,1},{1,2},{2,3},{3,4},{4,5},{5,6},{6,7},{7,8},{8,9},{9,10},{10,1... | collective-permute-start | bytes 786440 | tf_op jit(solution)/shard_map/ppermute | solution.py:319
  40.3 11.5 %collective-permute-done.8.refs_2_.refs_1_ = f32[512,128]{1,0:T(8,128)S(1)} collective-permute-done((f32[512,128]{1,0:T(8,128)S(1)}, f32[512,128]{1,0:T(8,128)S(1)}, u32[]{:S(2)}, u32[]{:S(2)}) %collective-permute-start.8) | collective-permute-done | bytes 262176 | tf_op jit(solution)/shard_map/ppermute | solution.py:319
  51.8 5.6 %collective-permute-done.9.refs_3_.refs_2_ = f32[512,128]{1,0:T(8,128)S(1)} collective-permute-done((f32[512,128]{1,0:T(8,128)S(1)}, f32[512,128]{1,0:T(8,128)S(1)}, u32[]{:S(2)}, u32[]{:S(2)}) %collective-permute-start.9) | collective-permute-done | bytes 262176 | tf_op jit(solution)/shard_map/ppermute | solution.py:319
  57.4 5.2 %collective-permute-done.10.refs_4_.refs_3_ = f32[512,128]{1,0:T(8,128)S(1)} collective-permute-done((f32[512,128]{1,0:T(8,128)S(1)}, f32[512,128]{1,0:T(8,128)S(1)}, u32[]{:S(2)}, u32[]{:S(2)}) %collective-permute-start.10) | collective-permute-done | bytes 262176 | tf_op jit(solution)/shard_map/ppermute | solution.py:319
  69.7 2.9 %collective-permute-done.16.b_ref = f32[136,128]{1,0:T(8,128)S(1)} collective-permute-done((f32[136,128]{1,0:T(8,128)S(1)}, f32[136,128]{1,0:T(8,128)S(1)}, u32[]{:S(2)}, u32[]{:S(2)}) %collective-permute-start.16) | collective-permute-done | bytes 69664 | tf_op jit(solution)/shard_map/ppermute | solution.py:326
  72.6 2.1 %roots.3 = (bf16[256,256]{1,0:T(8,128)(2,1)S(1)}, bf16[256,256]{1,0:T(8,128)(2,1)S(1)}, f32[8,128]{1,0:T(8,128)S(1)}) custom-call(f32[136,128]{1,0:T(8,128)S(1)} %add.10.a_ref, f32[136,128]{1,0:T(8,128)S(1)} %collective-permute-done.16.b_ref), custom_call_target="tpu_custom_call" | custom-call | flops 30000000 | bytes 1000000 | tf_op jit(solution)/shard_map/roots/pallas_call | solution.py:154
  76.8 3.1 %shard_map.37 = (f32[4096,256]{1,0:T(8,128)}, f32[512,128]{1,0:T(8,128)S(1)}, f32[512,128]{1,0:T(8,128)}, f32[512,128]{1,0:T(8,128)}, f32[512,128]{1,0:T(8,128)}, /*index=5*/f32[256,128]{1,0:T(8,128)S(1)}) custom-call(f32[512,128]{1,0:T(8,128)S(1)} %collective-permute-done.7.refs_1_.refs_0_, ...), custom_call_target="tpu_custom_call", output_to_operand_aliasing={{0}: (12, {})} | custom-call | flops 905969664 | bytes 5898240 | tf_op jit(solution)/shard_map/pallas_call | solution.py:274
  83.3 5.1 %collective-permute-start.29 = (f32[8,128]{1,0:T(8,128)S(1)}, f32[8,128]{1,0:T(8,128)S(1)}, u32[]{:S(2)}, u32[]{:S(2)}) collective-permute-start(f32[8,128]{1,0:T(8,128)S(1)} %maximum_maximum_fusion), channel_id=1, source_target_pairs={{0,5},{1,6},{2,7},{3,0},{4,1},{5,2},{6,3},{7,4},{8,13},{9,14},{10,... | collective-permute-start | bytes 12296 | tf_op jit(solution)/shard_map/ppermute | solution.py:337
  93.7 3.3 %collective-permute-start.31 = (f32[8,128]{1,0:T(8,128)S(1)}, f32[8,128]{1,0:T(8,128)S(1)}, u32[]{:S(2)}, u32[]{:S(2)}) collective-permute-start(f32[8,128]{1,0:T(8,128)S(1)} %max.31), channel_id=1, source_target_pairs={{0,24},{1,25},{2,26},{3,27},{4,28},{5,29},{6,30},{7,31},{8,0},{9,1... | collective-permute-start | bytes 12296 | tf_op jit(solution)/shard_map/ppermute | solution.py:337
  98.2 3.5 %collective-permute-start.32 = (f32[8,128]{1,0:T(8,128)S(1)}, f32[8,128]{1,0:T(8,128)S(1)}, u32[]{:S(2)}, u32[]{:S(2)}) collective-permute-start(f32[8,128]{1,0:T(8,128)S(1)} %max.32), channel_id=1, source_target_pairs={{0,24},{1,25},{2,26},{3,27},{4,28},{5,29},{6,30},{7,31},{8,0},{9,1... | collective-permute-start | bytes 12296 | tf_op jit(solution)/shard_map/ppermute | solution.py:337
  101.7 3.2 %collective-permute-start.22 = (f32[512,128]{1,0:T(8,128)}, f32[512,128]{1,0:T(8,128)S(1)}, u32[]{:S(2)}, u32[]{:S(2)}) collective-permute-start(f32[512,128]{1,0:T(8,128)} %get-tuple-element.67), channel_id=1, source_target_pairs={{0,1},{1,2},{2,3},{3,4},{4,5},{5,6},{6,7},{7,8},{8,9},{9,10},{10,1... | collective-permute-start | bytes 786440 | tf_op jit(solution)/shard_map/ppermute | solution.py:319
  106.9 2.8 %collective-permute-start.33 = (f32[8,128]{1,0:T(8,128)S(1)}, f32[8,128]{1,0:T(8,128)S(1)}, u32[]{:S(2)}, u32[]{:S(2)}) collective-permute-start(f32[8,128]{1,0:T(8,128)S(1)} %max.33), channel_id=1, source_target_pairs={{0,24},{1,25},{2,26},{3,27},{4,28},{5,29},{6,30},{7,31},{8,0},{9,1... | collective-permute-start | bytes 12296 | tf_op jit(solution)/shard_map/ppermute | solution.py:337
  113.1 3.5 %collective-permute-start.34 = (f32[8,128]{1,0:T(8,128)S(1)}, f32[8,128]{1,0:T(8,128)S(1)}, u32[]{:S(2)}, u32[]{:S(2)}) collective-permute-start(f32[8,128]{1,0:T(8,128)S(1)} %max.34), channel_id=1, source_target_pairs={{0,32},{1,33},{2,34},{3,35},{4,36},{5,37},{6,38},{7,39},{8,40},{9,... | collective-permute-start | bytes 12296 | tf_op jit(solution)/shard_map/ppermute | solution.py:337
  119.6 3.3 %collective-permute-done.25.refs_5_ = f32[256,128]{1,0:T(8,128)S(1)} collective-permute-done((f32[256,128]{1,0:T(8,128)S(1)}, f32[256,128]{1,0:T(8,128)S(1)}, u32[]{:S(2)}, u32[]{:S(2)}) %collective-permute-start.25) | collective-permute-done | bytes 131104 | tf_op jit(solution)/shard_map/ppermute | solution.py:319
  123.1 2.3 %collective-permute-start.17 = (f32[256,128]{1,0:T(8,128)S(1)}, f32[256,128]{1,0:T(8,128)S(1)}, u32[]{:S(2)}, u32[]{:S(2)}) collective-permute-start(f32[256,128]{1,0:T(8,128)S(1)} %get-tuple-element.62), channel_id=1, source_target_pairs={{0,1},{1,2},{2,3},{3,4},{4,5},{5,6},{6,7},{7,8},{8,9},{9,10},{10,1... | collective-permute-start | bytes 393224 | tf_op jit(solution)/shard_map/ppermute | solution.py:319
  127.4 6.2 %collective-permute-done.24.refs_4_ = f32[512,128]{1,0:T(8,128)S(1)} collective-permute-done((f32[512,128]{1,0:T(8,128)}, f32[512,128]{1,0:T(8,128)S(1)}, u32[]{:S(2)}, u32[]{:S(2)}) %collective-permute-start.24) | collective-permute-done | bytes 262176 | tf_op jit(solution)/shard_map/ppermute | solution.py:319
  133.7 5.6 %collective-permute-done.20.refs_0_ = f32[512,128]{1,0:T(8,128)S(1)} collective-permute-done((f32[512,128]{1,0:T(8,128)}, f32[512,128]{1,0:T(8,128)S(1)}, u32[]{:S(2)}, u32[]{:S(2)}) %collective-permute-start.20) | collective-permute-done | bytes 262176 | tf_op jit(solution)/shard_map/ppermute | solution.py:319
  140.4 5.9 %collective-permute-done.19.refs_1_ = f32[384,128]{1,0:T(8,128)S(1)} collective-permute-done((f32[384,128]{1,0:T(8,128)S(1)}, f32[384,128]{1,0:T(8,128)S(1)}, u32[]{:S(2)}, u32[]{:S(2)}) %collective-permute-start.19) | collective-permute-done | bytes 196640 | tf_op jit(solution)/shard_map/ppermute | solution.py:319
  (86 shorter events, 42.8 us)
Async XLA Ops:
  13.0 23.5 %collective-permute-start.6 = (f32[512,128]{1,0:T(8,128)S(1)}, f32[512,128]{1,0:T(8,128)S(1)}, u32[]{:S(2)}, u32[]{:S(2)}) collective-permute-start(f32[512,128]{1,0:T(8,128)S(1)} %get-tuple-element.48), channel_id=1, source_target_pairs={{0,1},{1,2},{2,3},{3,4},{4,5},{5,6},{6,7},{7,8},{8,9},{9,10},{10,1... | collective-permute-start | bytes 786440 | tf_op jit(solution)/shard_map/ppermute | solution.py:319
  15.3 21.1 %collective-permute-start.12 = (f32[384,128]{1,0:T(8,128)S(1)}, f32[384,128]{1,0:T(8,128)S(1)}, u32[]{:S(2)}, u32[]{:S(2)}) collective-permute-start(f32[384,128]{1,0:T(8,128)S(1)} %get-tuple-element.44.refs_11_.refs_4_), channel_id=1, source_target_pairs={{0,63},{1,0},{2,1},{3,2},{4,3},{5,4},{6,5},{7,6},{8,7},{9,8},{10,9... | collective-permute-start | bytes 589832 | tf_op jit(solution)/shard_map/ppermute | solution.py:319
  23.3 15.7 %collective-permute-start.11 = (f32[640,128]{1,0:T(8,128)S(1)}, f32[640,128]{1,0:T(8,128)S(1)}, u32[]{:S(2)}, u32[]{:S(2)}) collective-permute-start(f32[640,128]{1,0:T(8,128)S(1)} %get-tuple-element.43.refs_10_.refs_3_), channel_id=1, source_target_pairs={{0,63},{1,0},{2,1},{3,2},{4,3},{5,4},{6,5},{7,6},{8,7},{9,8},{10,9... | collective-permute-start | bytes 983048 | tf_op jit(solution)/shard_map/ppermute | solution.py:319
  25.3 11.2 %collective-permute-start.13 = (f32[256,128]{1,0:T(8,128)S(1)}, f32[256,128]{1,0:T(8,128)S(1)}, u32[]{:S(2)}, u32[]{:S(2)}) collective-permute-start(f32[256,128]{1,0:T(8,128)S(1)} %get-tuple-element.45.refs_12_.refs_5_), channel_id=1, source_target_pairs={{0,63},{1,0},{2,1},{3,2},{4,3},{5,4},{6,5},{7,6},{8,7},{9,8},{10,9... | collective-permute-start | bytes 393224 | tf_op jit(solution)/shard_map/ppermute | solution.py:319
  27.4 12.2 %collective-permute-start.7 = (f32[512,128]{1,0:T(8,128)S(1)}, f32[512,128]{1,0:T(8,128)S(1)}, u32[]{:S(2)}, u32[]{:S(2)}) collective-permute-start(f32[512,128]{1,0:T(8,128)S(1)} %get-tuple-element.49), channel_id=1, source_target_pairs={{0,1},{1,2},{2,3},{3,4},{4,5},{5,6},{6,7},{7,8},{8,9},{9,10},{10,1... | collective-permute-start | bytes 786440 | tf_op jit(solution)/shard_map/ppermute | solution.py:319
  36.4 15.4 %collective-permute-start.8 = (f32[512,128]{1,0:T(8,128)S(1)}, f32[512,128]{1,0:T(8,128)S(1)}, u32[]{:S(2)}, u32[]{:S(2)}) collective-permute-start(f32[512,128]{1,0:T(8,128)S(1)} %get-tuple-element.50), channel_id=1, source_target_pairs={{0,1},{1,2},{2,3},{3,4},{4,5},{5,6},{6,7},{7,8},{8,9},{9,10},{10,1... | collective-permute-start | bytes 786440 | tf_op jit(solution)/shard_map/ppermute | solution.py:319
  36.5 21.0 %collective-permute-start.9 = (f32[512,128]{1,0:T(8,128)S(1)}, f32[512,128]{1,0:T(8,128)S(1)}, u32[]{:S(2)}, u32[]{:S(2)}) collective-permute-start(f32[512,128]{1,0:T(8,128)S(1)} %get-tuple-element.51), channel_id=1, source_target_pairs={{0,1},{1,2},{2,3},{3,4},{4,5},{5,6},{6,7},{7,8},{8,9},{9,10},{10,1... | collective-permute-start | bytes 786440 | tf_op jit(solution)/shard_map/ppermute | solution.py:319
  36.5 26.2 %collective-permute-start.10 = (f32[512,128]{1,0:T(8,128)S(1)}, f32[512,128]{1,0:T(8,128)S(1)}, u32[]{:S(2)}, u32[]{:S(2)}) collective-permute-start(f32[512,128]{1,0:T(8,128)S(1)} %get-tuple-element.52), channel_id=1, source_target_pairs={{0,1},{1,2},{2,3},{3,4},{4,5},{5,6},{6,7},{7,8},{8,9},{9,10},{10,1... | collective-permute-start | bytes 786440 | tf_op jit(solution)/shard_map/ppermute | solution.py:319
  39.0 25.1 %collective-permute-start.5 = (f32[256,128]{1,0:T(8,128)S(1)}, f32[256,128]{1,0:T(8,128)S(1)}, u32[]{:S(2)}, u32[]{:S(2)}) collective-permute-start(f32[256,128]{1,0:T(8,128)S(1)} %get-tuple-element.46), channel_id=1, source_target_pairs={{0,1},{1,2},{2,3},{3,4},{4,5},{5,6},{6,7},{7,8},{8,9},{9,10},{10,1... | collective-permute-start | bytes 393224 | tf_op jit(solution)/shard_map/ppermute | solution.py:319
  39.7 25.2 %collective-permute-start.14 = (f32[136,128]{1,0:T(8,128)S(1)}, f32[136,128]{1,0:T(8,128)S(1)}, u32[]{:S(2)}, u32[]{:S(2)}) collective-permute-start(f32[136,128]{1,0:T(8,128)S(1)} %shard_map.34), channel_id=1, source_target_pairs={{0,1},{1,2},{2,3},{3,4},{4,5},{5,6},{6,7},{7,8},{8,9},{9,10},{10,1... | collective-permute-start | bytes 208904 | tf_op jit(solution)/shard_map/ppermute | solution.py:319
  69.7 32.1 %collective-permute-start.4 = (f32[256,128]{1,0:T(8,128)}, f32[256,128]{1,0:T(8,128)S(1)}, u32[]{:S(2)}, u32[]{:S(2)}) collective-permute-start(f32[256,128]{1,0:T(8,128)} %copy-done.4), channel_id=1, source_target_pairs={{0,1},{1,2},{2,3},{3,4},{4,5},{5,6},{6,7},{7,8},{8,9},{9,10},{10,1... | collective-permute-start | bytes 393224 | tf_op jit(solution)/shard_map/ppermute | solution.py:319
  69.7 37.3 %collective-permute-start.3 = (f32[384,128]{1,0:T(8,128)}, f32[384,128]{1,0:T(8,128)S(1)}, u32[]{:S(2)}, u32[]{:S(2)}) collective-permute-start(f32[384,128]{1,0:T(8,128)} %copy-done.3), channel_id=1, source_target_pairs={{0,1},{1,2},{2,3},{3,4},{4,5},{5,6},{6,7},{7,8},{8,9},{9,10},{10,1... | collective-permute-start | bytes 589832 | tf_op jit(solution)/shard_map/ppermute | solution.py:319
  74.8 7.2 %collective-permute-start.27 = (f32[8,128]{1,0:T(8,128)S(1)}, f32[8,128]{1,0:T(8,128)S(1)}, u32[]{:S(2)}, u32[]{:S(2)}) collective-permute-start(f32[8,128]{1,0:T(8,128)S(1)} %select_select_fusion), channel_id=1, source_target_pairs={{0,6},{1,7},{2,0},{3,1},{4,2},{5,3},{6,4},{7,5},{8,14},{9,15},{10,... | collective-permute-start | bytes 12296 | tf_op jit(solution)/shard_map/ppermute | solution.py:337
  74.9 8.5 %collective-permute-start.26 = (f32[8,128]{1,0:T(8,128)S(1)}, f32[8,128]{1,0:T(8,128)S(1)}, u32[]{:S(2)}, u32[]{:S(2)}) collective-permute-start(f32[8,128]{1,0:T(8,128)S(1)} %select_select_fusion), channel_id=1, source_target_pairs={{0,7},{1,0},{2,1},{3,2},{4,3},{5,4},{6,5},{7,6},{8,15},{9,8},{10,9... | collective-permute-start | bytes 12296 | tf_op jit(solution)/shard_map/ppermute | solution.py:337
  80.2 32.9 %collective-permute-start.2 = (f32[640,128]{1,0:T(8,128)S(1)}, f32[640,128]{1,0:T(8,128)S(1)}, u32[]{:S(2)}, u32[]{:S(2)}) collective-permute-start(f32[640,128]{1,0:T(8,128)S(1)} %copy-done.2), channel_id=1, source_target_pairs={{0,1},{1,2},{2,3},{3,4},{4,5},{5,6},{6,7},{7,8},{8,9},{9,10},{10,1... | collective-permute-start | bytes 983048 | tf_op jit(solution)/shard_map/ppermute | solution.py:319
  82.0 40.9 %collective-permute-start.21 = (f32[512,128]{1,0:T(8,128)S(1)}, f32[512,128]{1,0:T(8,128)S(1)}, u32[]{:S(2)}, u32[]{:S(2)}) collective-permute-start(f32[512,128]{1,0:T(8,128)S(1)} %get-tuple-element.66), channel_id=1, source_target_pairs={{0,1},{1,2},{2,3},{3,4},{4,5},{5,6},{6,7},{7,8},{8,9},{9,10},{10,1... | collective-permute-start | bytes 786440 | tf_op jit(solution)/shard_map/ppermute | solution.py:319
  101.7 21.4 %collective-permute-start.22 = (f32[512,128]{1,0:T(8,128)}, f32[512,128]{1,0:T(8,128)S(1)}, u32[]{:S(2)}, u32[]{:S(2)}) collective-permute-start(f32[512,128]{1,0:T(8,128)} %get-tuple-element.67), channel_id=1, source_target_pairs={{0,1},{1,2},{2,3},{3,4},{4,5},{5,6},{6,7},{7,8},{8,9},{9,10},{10,1... | collective-permute-start | bytes 786440 | tf_op jit(solution)/shard_map/ppermute | solution.py:319
  104.9 20.5 %collective-permute-start.23 = (f32[512,128]{1,0:T(8,128)}, f32[512,128]{1,0:T(8,128)S(1)}, u32[]{:S(2)}, u32[]{:S(2)}) collective-permute-start(f32[512,128]{1,0:T(8,128)} %get-tuple-element.68), channel_id=1, source_target_pairs={{0,1},{1,2},{2,3},{3,4},{4,5},{5,6},{6,7},{7,8},{8,9},{9,10},{10,1... | collective-permute-start | bytes 786440 | tf_op jit(solution)/shard_map/ppermute | solution.py:319
  111.1 11.9 %collective-permute-start.25 = (f32[256,128]{1,0:T(8,128)S(1)}, f32[256,128]{1,0:T(8,128)S(1)}, u32[]{:S(2)}, u32[]{:S(2)}) collective-permute-start(f32[256,128]{1,0:T(8,128)S(1)} %get-tuple-element.70), channel_id=1, source_target_pairs={{0,1},{1,2},{2,3},{3,4},{4,5},{5,6},{6,7},{7,8},{8,9},{9,10},{10,1... | collective-permute-start | bytes 393224 | tf_op jit(solution)/shard_map/ppermute | solution.py:319
  118.5 15.1 %collective-permute-start.24 = (f32[512,128]{1,0:T(8,128)}, f32[512,128]{1,0:T(8,128)S(1)}, u32[]{:S(2)}, u32[]{:S(2)}) collective-permute-start(f32[512,128]{1,0:T(8,128)} %get-tuple-element.69), channel_id=1, source_target_pairs={{0,1},{1,2},{2,3},{3,4},{4,5},{5,6},{6,7},{7,8},{8,9},{9,10},{10,1... | collective-permute-start | bytes 786440 | tf_op jit(solution)/shard_map/ppermute | solution.py:319
  122.9 16.4 %collective-permute-start.20 = (f32[512,128]{1,0:T(8,128)}, f32[512,128]{1,0:T(8,128)S(1)}, u32[]{:S(2)}, u32[]{:S(2)}) collective-permute-start(f32[512,128]{1,0:T(8,128)} %get-tuple-element.65), channel_id=1, source_target_pairs={{0,1},{1,2},{2,3},{3,4},{4,5},{5,6},{6,7},{7,8},{8,9},{9,10},{10,1... | collective-permute-start | bytes 786440 | tf_op jit(solution)/shard_map/ppermute | solution.py:319
  122.9 23.4 %collective-permute-start.18 = (f32[640,128]{1,0:T(8,128)S(1)}, f32[640,128]{1,0:T(8,128)S(1)}, u32[]{:S(2)}, u32[]{:S(2)}) collective-permute-start(f32[640,128]{1,0:T(8,128)S(1)} %get-tuple-element.63), channel_id=1, source_target_pairs={{0,1},{1,2},{2,3},{3,4},{4,5},{5,6},{6,7},{7,8},{8,9},{9,10},{10,1... | collective-permute-start | bytes 983048 | tf_op jit(solution)/shard_map/ppermute | solution.py:319
  123.1 24.0 %collective-permute-start.17 = (f32[256,128]{1,0:T(8,128)S(1)}, f32[256,128]{1,0:T(8,128)S(1)}, u32[]{:S(2)}, u32[]{:S(2)}) collective-permute-start(f32[256,128]{1,0:T(8,128)S(1)} %get-tuple-element.62), channel_id=1, source_target_pairs={{0,1},{1,2},{2,3},{3,4},{4,5},{5,6},{6,7},{7,8},{8,9},{9,10},{10,1... | collective-permute-start | bytes 393224 | tf_op jit(solution)/shard_map/ppermute | solution.py:319
  125.5 20.9 %collective-permute-start.19 = (f32[384,128]{1,0:T(8,128)S(1)}, f32[384,128]{1,0:T(8,128)S(1)}, u32[]{:S(2)}, u32[]{:S(2)}) collective-permute-start(f32[384,128]{1,0:T(8,128)S(1)} %get-tuple-element.64), channel_id=1, source_target_pairs={{0,1},{1,2},{2,3},{3,4},{4,5},{5,6},{6,7},{7,8},{8,9},{9,10},{10,1... | collective-permute-start | bytes 589832 | tf_op jit(solution)/shard_map/ppermute | solution.py:319
  (16 other events, 219.2 us)

commit v2 on v1

--- a/solution.py
+++ b/solution.py
@@ -108,7 +108,7 @@
     )(matrix)
 
 
-def root_body(a_ref, b_ref, wh_ref, wl_ref, s_ref):
+def root_body(slot, a_ref, b_ref, wh_ref, wl_ref, s_ref):
     total = a_ref[...] + b_ref[...]
     inverse = lax.rsqrt(total[B : B + 8, :])
     first = jnp.broadcast_to(inverse[0:1, :], (B, B)).T
@@ -147,12 +147,14 @@
         high, low = halves(value)
         wh_ref[rows : rows + B, cols : cols + B] = high
         wl_ref[rows : rows + B, cols : cols + B] = low
-    s_ref[...] = jnp.full((8, B), squares, F32)
-
-
-def roots(parts):
-    return pl.pallas_call(
-        root_body,
+    lane = lax.broadcasted_iota(jnp.int32, (8, B), 1)
+    own = STEPS * lax.axis_index("blk") + slot
+    s_ref[...] = jnp.where(lane == own, squares, 0.0)
+
+
+def roots(parts, slot):
+    return pl.pallas_call(
+        functools.partial(root_body, slot),
         in_specs=[VM] * 2,
         out_specs=[VM] * 3,
         out_shape=[
@@ -337,10 +339,11 @@
     return lax.ppermute(value, "blk", [(s, where(s)) for s in range(count)])
 
 
-def of_all_pairs(values):
+def of_all_pairs(tile):
     count = lax.axis_size("blk")
     inner = 8 if count % 8 == 0 else count
     middle = 4 if count % (4 * inner) == 0 else 1
+    outer = count // (inner * middle)
 
     def along_inner(steps):
         return lambda s: s // inner * inner + (s + steps) % inner
@@ -349,29 +352,40 @@
         ring = inner * middle
         return lambda s: s // ring * ring + (s + steps * inner) % ring
 
-    def gathered(tile, moves):
+    reach = min(4, inner)
+    rounds = [[along_inner(-n) for n in range(1, reach)]]
+    while reach < inner:
+        step = min(3, inner - reach)
+        rounds.append([along_inner(-step)])
+        reach += step
+    for _ in range(1, middle):
+        rounds.append([along_middle(-1)])
+    for n in range(1, outer):
+        rounds.append([lambda s, n=n: (s + n * inner * middle) % count])
+    for moves in rounds:
         for part in [moved(tile, where) for where in moves]:
             tile = jnp.maximum(tile, part)
-        return tile
-
-    lane = lax.broadcasted_iota(jnp.int32, (8, B), 1)
-    at = STEPS * lax.axis_index("blk")
-    tile = jnp.zeros((8, B), F32)
-    for step, value in enumerate(values):
-        tile = jnp.where(lane == at + step, value, tile)
-    reach = min(4, inner)
-    if inner > 1:
-        tile = gathered(tile, [along_inner(-n) for n in range(1, reach)])
-    while reach < inner:
-        step = min(3, inner - reach)
-        tile = gathered(tile, [along_inner(-step)])
-        reach += step
-    for _ in range(1, middle):
-        tile = gathered(tile, [along_middle(-1)])
-    outer = count // (inner * middle)
-    for n in range(1, outer):
-        tile = gathered(tile, [lambda s, n=n: (s + n * inner * middle) % count])
-    return tile[0, : STEPS * count].reshape(count, STEPS)
+    return tile
+
+
+def mean_body(count, t_ref, o_ref):
+    lane = lax.broadcasted_iota(jnp.int32, (1, B), 1)
+    line = t_ref[0:1, :]
+    for step in range(STEPS):
+        own = (lane % STEPS == step) & (lane < STEPS * count)
+        o_ref[step] = jnp.sum(jnp.where(own, line, 0.0)) / float(count)
+
+
+def mean_over_pairs(tile):
+    return pl.pallas_call(
+        functools.partial(mean_body, lax.axis_size("blk")),
+        in_specs=[VM],
+        out_specs=pl.BlockSpec(memory_space=pltpu.SMEM),
+        out_shape=jax.ShapeDtypeStruct((STEPS,), F32),
+        compiler_params=params(4),
+        cost_estimate=cost(1000, 1000),
+        name="mean_over_pairs",
+    )(tile)
 
 
 def steps(matrix):
@@ -381,7 +395,7 @@
     back = [n * unit for n in BACK]
     front_rows = sum(front)
 
-    wh, wl, squares0 = roots(of_group(first_gram(matrix)))
+    wh, wl, squares0 = roots(of_group(first_gram(matrix)), 0)
     w = (wh, wl)
 
     xf, rf = update(matrix, w, 0, front[:1])
@@ -397,7 +411,7 @@
     cut = len(got) - 1
     sums = partial(got[:cut], rf[:cut], rb, [])
     sums = partial(got[cut:], rf[cut:], [], [sums, helped])
-    wh, wl, squares1 = roots(of_group(sums))
+    wh, wl, squares1 = roots(of_group(sums), 1)
     w = (wh, wl)
 
     out, *ys = second(got[:1], rf[:1], w, None, rows, 0)
@@ -406,8 +420,7 @@
     ys = [*ys, *more_y, *back_y]
     arrived = [shifted(y, 1) for y in ys]
 
-    totals = jnp.sum(of_all_pairs([squares0, squares1]), axis=0)
-    off_measure = totals / float(lax.axis_size("blk"))
+    off_measure = mean_over_pairs(of_all_pairs(jnp.maximum(squares0, squares1)))
     places, at = [], 0
     for y in ys:
         places.append(at)

time: 149 us -> 147 us (0.987)
  waiting for transfers between devices: 68 us -> 74.2 us
  starting transfers between devices: 56.3 us -> 50.9 us
  Pallas kernels: 21 us -> 19.4 us
    ppermute x22, starting transfers between devices: 32.3 us -> 26.2 us  [shifted(): lax.ppermute(value, 'blk', [(s, (s + steps) % count) for s in range(count)])]
    ppermute x22, waiting for transfers between devices: 52.9 us -> 57.8 us  [shifted(): lax.ppermute(value, 'blk', [(s, (s + steps) % count) for s in range(count)])]
    ppermute x9, waiting for transfers between devices: 6.8 us -> 8.49 us  [moved(): return lax.ppermute(value, 'blk', [(s, where(s)) for s in range(count)])]
    pallas_call x3, Pallas kernels: 6.39 us -> 4.76 us  [second(): pl.pallas_call(functools.partial(second_body, rows0, out is not None, len...]
    pallas_call x2 -> x3, Pallas kernels: 4.13 us -> 4.77 us  [the longest x2 4.13 us: roots(): pl.pallas_call(functools.partial(root_body, slot), in_specs=[VM] * 2, out...]
  transfers between devices with their start and end apart: 35 -> 35, of which waited for: 20 -> 22; matrix products, arithmetic and copies ran while one was open for 0% -> 0% of each run, Pallas kernels for 9% -> 8%
where the time goes in v2:
time: 147 us; the launch traced here: 146 us
  waiting for transfers between devices  74.2 us (50%)
  starting transfers between devices  50.9 us (35%)
  Pallas kernels  19.4 us (13%)
    ppermute x22, waiting for transfers between devices, shifted(): lax.ppermute(value, 'blk', [(s, (s + steps) % count) for s in range(count)])  57.8 us
    ppermute x22, starting transfers between devices, shifted(): lax.ppermute(value, 'blk', [(s, (s + steps) % count) for s in range(count)])  26.2 us
    ppermute x9, starting transfers between devices, moved(): return lax.ppermute(value, 'blk', [(s, where(s)) for s in range(count)])  20.9 us
    ppermute x9, waiting for transfers between devices, moved(): return lax.ppermute(value, 'blk', [(s, where(s)) for s in range(count)])  8.49 us
    ppermute x4, waiting for transfers between devices, from_other(): return lax.ppermute(part, 'row', [(s, s ^ mask) for s in range(count)])  7.95 us
    pallas_call x3, Pallas kernels, second(): pl.pallas_call(functools.partial(second_body, rows0, out is not None, len...  4.76 us
    pallas_call x2, Pallas kernels, roots(): pl.pallas_call(functools.partial(root_body, slot), in_specs=[VM] * 2, out...  4.13 us
    ppermute x4, starting transfers between devices, from_other(): return lax.ppermute(part, 'row', [(s, s ^ mask) for s in range(count)])  3.86 us
  transfers between devices with their start and end apart: 35, of which 22 were waited for; matrix products, arithmetic and copies ran while one was open for 0% of the time, Pallas kernels for 8%

profile of v2, /device:TPU:8, one launch (start us, length us, event | category | flops | bytes accessed | tf_op | source)
XLA Modules:
  0.0 145.6 jit_solution(1585721473094254596)
XLA Ops:
  0.6 3.8 %first_gram.1 = f32[136,128]{1,0:T(8,128)S(1)} custom-call(f32[4096,256]{1,0:T(8,128)} %m_ref.7), custom_call_target="tpu_custom_call" | custom-call | flops 536870912 | bytes 4194304 | tf_op jit(solution)/shard_map/first_gram/pallas_call | solution.py:94
  5.8 2.2 %collective-permute-start.1 = (f32[136,128]{1,0:T(8,128)S(1)}, f32[136,128]{1,0:T(8,128)S(1)}, u32[]{:S(2)}, u32[]{:S(2)}) collective-permute-start(f32[136,128]{1,0:T(8,128)S(1)} %add.6.a_ref), channel_id=1, source_target_pairs={{0,128},{64,192},{128,0},{192,64},{1,129},{65,193},{129,1},{193,65... | collective-permute-start | bytes 208904 | tf_op jit(solution)/shard_map/ppermute | solution.py:328
  8.0 2.5 %collective-permute-done.1.b_ref = f32[136,128]{1,0:T(8,128)S(1)} collective-permute-done((f32[136,128]{1,0:T(8,128)S(1)}, f32[136,128]{1,0:T(8,128)S(1)}, u32[]{:S(2)}, u32[]{:S(2)}) %collective-permute-start.1) | collective-permute-done | bytes 69664 | tf_op jit(solution)/shard_map/ppermute | solution.py:328
  10.5 2.1 %roots.2 = (bf16[256,256]{1,0:T(8,128)(2,1)S(1)}, bf16[256,256]{1,0:T(8,128)(2,1)S(1)}, f32[8,128]{1,0:T(8,128)S(1)}) custom-call(f32[136,128]{1,0:T(8,128)S(1)} %add.6.a_ref, f32[136,128]{1,0:T(8,128)S(1)} %collective-permute-done.1.b_ref), custom_call_target="tpu_custom_call" | custom-call | flops 30000000 | bytes 1000000 | tf_op jit(solution)/shard_map/roots/pallas_call | solution.py:156
  15.3 7.9 %collective-permute-start.12 = (f32[384,128]{1,0:T(8,128)S(1)}, f32[384,128]{1,0:T(8,128)S(1)}, u32[]{:S(2)}, u32[]{:S(2)}) collective-permute-start(f32[384,128]{1,0:T(8,128)S(1)} %get-tuple-element.44.refs_11_.refs_4_), channel_id=1, source_target_pairs={{0,63},{1,0},{2,1},{3,2},{4,3},{5,4},{6,5},{7,6},{8,7},{9,8},{10,9... | collective-permute-start | bytes 589832 | tf_op jit(solution)/shard_map/ppermute | solution.py:321
  28.5 7.9 %collective-permute-done.13.refs_5_ = f32[256,128]{1,0:T(8,128)S(1)} collective-permute-done((f32[256,128]{1,0:T(8,128)S(1)}, f32[256,128]{1,0:T(8,128)S(1)}, u32[]{:S(2)}, u32[]{:S(2)}) %collective-permute-start.13) | collective-permute-done | bytes 131104 | tf_op jit(solution)/shard_map/ppermute | solution.py:321
  36.5 2.5 %collective-permute-start.10 = (f32[512,128]{1,0:T(8,128)S(1)}, f32[512,128]{1,0:T(8,128)S(1)}, u32[]{:S(2)}, u32[]{:S(2)}) collective-permute-start(f32[512,128]{1,0:T(8,128)S(1)} %get-tuple-element.52), channel_id=1, source_target_pairs={{0,1},{1,2},{2,3},{3,4},{4,5},{5,6},{6,7},{7,8},{8,9},{9,10},{10,1... | collective-permute-start | bytes 786440 | tf_op jit(solution)/shard_map/ppermute | solution.py:321
  40.3 11.5 %collective-permute-done.8.refs_2_.refs_1_ = f32[512,128]{1,0:T(8,128)S(1)} collective-permute-done((f32[512,128]{1,0:T(8,128)S(1)}, f32[512,128]{1,0:T(8,128)S(1)}, u32[]{:S(2)}, u32[]{:S(2)}) %collective-permute-start.8) | collective-permute-done | bytes 262176 | tf_op jit(solution)/shard_map/ppermute | solution.py:321
  51.8 5.6 %collective-permute-done.9.refs_3_.refs_2_ = f32[512,128]{1,0:T(8,128)S(1)} collective-permute-done((f32[512,128]{1,0:T(8,128)S(1)}, f32[512,128]{1,0:T(8,128)S(1)}, u32[]{:S(2)}, u32[]{:S(2)}) %collective-permute-start.9) | collective-permute-done | bytes 262176 | tf_op jit(solution)/shard_map/ppermute | solution.py:321
  57.4 5.2 %collective-permute-done.10.refs_4_.refs_3_ = f32[512,128]{1,0:T(8,128)S(1)} collective-permute-done((f32[512,128]{1,0:T(8,128)S(1)}, f32[512,128]{1,0:T(8,128)S(1)}, u32[]{:S(2)}, u32[]{:S(2)}) %collective-permute-start.10) | collective-permute-done | bytes 262176 | tf_op jit(solution)/shard_map/ppermute | solution.py:321
  67.8 3.0 %collective-permute-done.16.b_ref = f32[136,128]{1,0:T(8,128)S(1)} collective-permute-done((f32[136,128]{1,0:T(8,128)S(1)}, f32[136,128]{1,0:T(8,128)S(1)}, u32[]{:S(2)}, u32[]{:S(2)}) %collective-permute-start.16) | collective-permute-done | bytes 69664 | tf_op jit(solution)/shard_map/ppermute | solution.py:328
  70.8 2.1 %roots.3 = (bf16[256,256]{1,0:T(8,128)(2,1)S(1)}, bf16[256,256]{1,0:T(8,128)(2,1)S(1)}, f32[8,128]{1,0:T(8,128)S(1)}) custom-call(f32[136,128]{1,0:T(8,128)S(1)} %add.7.a_ref, f32[136,128]{1,0:T(8,128)S(1)} %collective-permute-done.16.b_ref), custom_call_target="tpu_custom_call" | custom-call | flops 30000000 | bytes 1000000 | tf_op jit(solution)/shard_map/roots/pallas_call | solution.py:156
  74.2 2.1 %shard_map.37 = (f32[4096,256]{1,0:T(8,128)}, f32[512,128]{1,0:T(8,128)S(1)}, f32[512,128]{1,0:T(8,128)S(1)}, f32[512,128]{1,0:T(8,128)S(1)}, f32[512,128]{1,0:T(8,128)S(1)}, /*index=5*/f32[256,128]{1,0:T(8,128)S(1)}) custom-call(f32[512,128]{1,0:T(8,128)S(1)} %collective-permute-done.7.refs_1_.refs_0_, ...), custom_call_target="tpu_custom_call", output_to_operand_aliasing={{0}: (12, {})} | custom-call | flops 905969664 | bytes 5898240 | tf_op jit(solution)/shard_map/pallas_call | solution.py:276
  79.9 5.1 %collective-permute-start.29 = (f32[8,128]{1,0:T(8,128)S(1)}, f32[8,128]{1,0:T(8,128)S(1)}, u32[]{:S(2)}, u32[]{:S(2)}) collective-permute-start(f32[8,128]{1,0:T(8,128)S(1)} %maximum_maximum_fusion), channel_id=1, source_target_pairs={{0,5},{1,6},{2,7},{3,0},{4,1},{5,2},{6,3},{7,4},{8,13},{9,14},{10,... | collective-permute-start | bytes 12296 | tf_op jit(solution)/shard_map/ppermute | solution.py:339
  90.2 3.2 %collective-permute-start.31 = (f32[8,128]{1,0:T(8,128)S(1)}, f32[8,128]{1,0:T(8,128)S(1)}, u32[]{:S(2)}, u32[]{:S(2)}) collective-permute-start(f32[8,128]{1,0:T(8,128)S(1)} %max.35), channel_id=1, source_target_pairs={{0,24},{1,25},{2,26},{3,27},{4,28},{5,29},{6,30},{7,31},{8,0},{9,1... | collective-permute-start | bytes 12296 | tf_op jit(solution)/shard_map/ppermute | solution.py:339
  94.8 3.5 %collective-permute-start.32 = (f32[8,128]{1,0:T(8,128)S(1)}, f32[8,128]{1,0:T(8,128)S(1)}, u32[]{:S(2)}, u32[]{:S(2)}) collective-permute-start(f32[8,128]{1,0:T(8,128)S(1)} %max.36), channel_id=1, source_target_pairs={{0,24},{1,25},{2,26},{3,27},{4,28},{5,29},{6,30},{7,31},{8,0},{9,1... | collective-permute-start | bytes 12296 | tf_op jit(solution)/shard_map/ppermute | solution.py:339
  99.6 3.2 %collective-permute-start.22 = (f32[512,128]{1,0:T(8,128)S(1)}, f32[512,128]{1,0:T(8,128)S(1)}, u32[]{:S(2)}, u32[]{:S(2)}) collective-permute-start(f32[512,128]{1,0:T(8,128)S(1)} %get-tuple-element.67), channel_id=1, source_target_pairs={{0,1},{1,2},{2,3},{3,4},{4,5},{5,6},{6,7},{7,8},{8,9},{9,10},{10,1... | collective-permute-start | bytes 786440 | tf_op jit(solution)/shard_map/ppermute | solution.py:321
  102.8 3.5 %collective-permute-start.33 = (f32[8,128]{1,0:T(8,128)S(1)}, f32[8,128]{1,0:T(8,128)S(1)}, u32[]{:S(2)}, u32[]{:S(2)}) collective-permute-start(f32[8,128]{1,0:T(8,128)S(1)} %max.37), channel_id=1, source_target_pairs={{0,24},{1,25},{2,26},{3,27},{4,28},{5,29},{6,30},{7,31},{8,0},{9,1... | collective-permute-start | bytes 12296 | tf_op jit(solution)/shard_map/ppermute | solution.py:339
  106.2 2.0 %collective-permute-start.25 = (f32[256,128]{1,0:T(8,128)S(1)}, f32[256,128]{1,0:T(8,128)S(1)}, u32[]{:S(2)}, u32[]{:S(2)}) collective-permute-start(f32[256,128]{1,0:T(8,128)S(1)} %get-tuple-element.70), channel_id=1, source_target_pairs={{0,1},{1,2},{2,3},{3,4},{4,5},{5,6},{6,7},{7,8},{8,9},{9,10},{10,1... | collective-permute-start | bytes 393224 | tf_op jit(solution)/shard_map/ppermute | solution.py:321
  109.6 3.6 %collective-permute-start.34 = (f32[8,128]{1,0:T(8,128)S(1)}, f32[8,128]{1,0:T(8,128)S(1)}, u32[]{:S(2)}, u32[]{:S(2)}) collective-permute-start(f32[8,128]{1,0:T(8,128)S(1)} %max.38), channel_id=1, source_target_pairs={{0,32},{1,33},{2,34},{3,35},{4,36},{5,37},{6,38},{7,39},{8,40},{9,... | collective-permute-start | bytes 12296 | tf_op jit(solution)/shard_map/ppermute | solution.py:339
  116.1 2.3 %collective-permute-done.25.refs_5_ = f32[256,128]{1,0:T(8,128)S(1)} collective-permute-done((f32[256,128]{1,0:T(8,128)S(1)}, f32[256,128]{1,0:T(8,128)S(1)}, u32[]{:S(2)}, u32[]{:S(2)}) %collective-permute-start.25) | collective-permute-done | bytes 131104 | tf_op jit(solution)/shard_map/ppermute | solution.py:321
  118.5 5.5 %collective-permute-done.23.refs_3_ = f32[512,128]{1,0:T(8,128)S(1)} collective-permute-done((f32[512,128]{1,0:T(8,128)S(1)}, f32[512,128]{1,0:T(8,128)S(1)}, u32[]{:S(2)}, u32[]{:S(2)}) %collective-permute-start.23) | collective-permute-done | bytes 262176 | tf_op jit(solution)/shard_map/ppermute | solution.py:321
  124.6 12.5 %collective-permute-done.24.refs_4_ = f32[512,128]{1,0:T(8,128)S(1)} collective-permute-done((f32[512,128]{1,0:T(8,128)S(1)}, f32[512,128]{1,0:T(8,128)S(1)}, u32[]{:S(2)}, u32[]{:S(2)}) %collective-permute-start.24) | collective-permute-done | bytes 262176 | tf_op jit(solution)/shard_map/ppermute | solution.py:321
  137.1 4.2 %collective-permute-done.20.refs_0_ = f32[512,128]{1,0:T(8,128)S(1)} collective-permute-done((f32[512,128]{1,0:T(8,128)S(1)}, f32[512,128]{1,0:T(8,128)S(1)}, u32[]{:S(2)}, u32[]{:S(2)}) %collective-permute-start.20) | collective-permute-done | bytes 262176 | tf_op jit(solution)/shard_map/ppermute | solution.py:321
  (74 shorter events, 37.7 us)
Async XLA Ops:
  13.0 23.5 %collective-permute-start.6 = (f32[512,128]{1,0:T(8,128)S(1)}, f32[512,128]{1,0:T(8,128)S(1)}, u32[]{:S(2)}, u32[]{:S(2)}) collective-permute-start(f32[512,128]{1,0:T(8,128)S(1)} %get-tuple-element.48), channel_id=1, source_target_pairs={{0,1},{1,2},{2,3},{3,4},{4,5},{5,6},{6,7},{7,8},{8,9},{9,10},{10,1... | collective-permute-start | bytes 786440 | tf_op jit(solution)/shard_map/ppermute | solution.py:321
  15.3 21.1 %collective-permute-start.12 = (f32[384,128]{1,0:T(8,128)S(1)}, f32[384,128]{1,0:T(8,128)S(1)}, u32[]{:S(2)}, u32[]{:S(2)}) collective-permute-start(f32[384,128]{1,0:T(8,128)S(1)} %get-tuple-element.44.refs_11_.refs_4_), channel_id=1, source_target_pairs={{0,63},{1,0},{2,1},{3,2},{4,3},{5,4},{6,5},{7,6},{8,7},{9,8},{10,9... | collective-permute-start | bytes 589832 | tf_op jit(solution)/shard_map/ppermute | solution.py:321
  23.3 15.7 %collective-permute-start.11 = (f32[640,128]{1,0:T(8,128)S(1)}, f32[640,128]{1,0:T(8,128)S(1)}, u32[]{:S(2)}, u32[]{:S(2)}) collective-permute-start(f32[640,128]{1,0:T(8,128)S(1)} %get-tuple-element.43.refs_10_.refs_3_), channel_id=1, source_target_pairs={{0,63},{1,0},{2,1},{3,2},{4,3},{5,4},{6,5},{7,6},{8,7},{9,8},{10,9... | collective-permute-start | bytes 983048 | tf_op jit(solution)/shard_map/ppermute | solution.py:321
  25.3 11.2 %collective-permute-start.13 = (f32[256,128]{1,0:T(8,128)S(1)}, f32[256,128]{1,0:T(8,128)S(1)}, u32[]{:S(2)}, u32[]{:S(2)}) collective-permute-start(f32[256,128]{1,0:T(8,128)S(1)} %get-tuple-element.45.refs_12_.refs_5_), channel_id=1, source_target_pairs={{0,63},{1,0},{2,1},{3,2},{4,3},{5,4},{6,5},{7,6},{8,7},{9,8},{10,9... | collective-permute-start | bytes 393224 | tf_op jit(solution)/shard_map/ppermute | solution.py:321
  27.4 12.2 %collective-permute-start.7 = (f32[512,128]{1,0:T(8,128)S(1)}, f32[512,128]{1,0:T(8,128)S(1)}, u32[]{:S(2)}, u32[]{:S(2)}) collective-permute-start(f32[512,128]{1,0:T(8,128)S(1)} %get-tuple-element.49), channel_id=1, source_target_pairs={{0,1},{1,2},{2,3},{3,4},{4,5},{5,6},{6,7},{7,8},{8,9},{9,10},{10,1... | collective-permute-start | bytes 786440 | tf_op jit(solution)/shard_map/ppermute | solution.py:321
  36.4 15.4 %collective-permute-start.8 = (f32[512,128]{1,0:T(8,128)S(1)}, f32[512,128]{1,0:T(8,128)S(1)}, u32[]{:S(2)}, u32[]{:S(2)}) collective-permute-start(f32[512,128]{1,0:T(8,128)S(1)} %get-tuple-element.50), channel_id=1, source_target_pairs={{0,1},{1,2},{2,3},{3,4},{4,5},{5,6},{6,7},{7,8},{8,9},{9,10},{10,1... | collective-permute-start | bytes 786440 | tf_op jit(solution)/shard_map/ppermute | solution.py:321
  36.4 21.0 %collective-permute-start.9 = (f32[512,128]{1,0:T(8,128)S(1)}, f32[512,128]{1,0:T(8,128)S(1)}, u32[]{:S(2)}, u32[]{:S(2)}) collective-permute-start(f32[512,128]{1,0:T(8,128)S(1)} %get-tuple-element.51), channel_id=1, source_target_pairs={{0,1},{1,2},{2,3},{3,4},{4,5},{5,6},{6,7},{7,8},{8,9},{9,10},{10,1... | collective-permute-start | bytes 786440 | tf_op jit(solution)/shard_map/ppermute | solution.py:321
  36.5 26.2 %collective-permute-start.10 = (f32[512,128]{1,0:T(8,128)S(1)}, f32[512,128]{1,0:T(8,128)S(1)}, u32[]{:S(2)}, u32[]{:S(2)}) collective-permute-start(f32[512,128]{1,0:T(8,128)S(1)} %get-tuple-element.52), channel_id=1, source_target_pairs={{0,1},{1,2},{2,3},{3,4},{4,5},{5,6},{6,7},{7,8},{8,9},{9,10},{10,1... | collective-permute-start | bytes 786440 | tf_op jit(solution)/shard_map/ppermute | solution.py:321
  38.9 25.1 %collective-permute-start.5 = (f32[256,128]{1,0:T(8,128)S(1)}, f32[256,128]{1,0:T(8,128)S(1)}, u32[]{:S(2)}, u32[]{:S(2)}) collective-permute-start(f32[256,128]{1,0:T(8,128)S(1)} %get-tuple-element.46), channel_id=1, source_target_pairs={{0,1},{1,2},{2,3},{3,4},{4,5},{5,6},{6,7},{7,8},{8,9},{9,10},{10,1... | collective-permute-start | bytes 393224 | tf_op jit(solution)/shard_map/ppermute | solution.py:321
  39.6 25.2 %collective-permute-start.14 = (f32[136,128]{1,0:T(8,128)S(1)}, f32[136,128]{1,0:T(8,128)S(1)}, u32[]{:S(2)}, u32[]{:S(2)}) collective-permute-start(f32[136,128]{1,0:T(8,128)S(1)} %shard_map.34), channel_id=1, source_target_pairs={{0,1},{1,2},{2,3},{3,4},{4,5},{5,6},{6,7},{7,8},{8,9},{9,10},{10,1... | collective-permute-start | bytes 208904 | tf_op jit(solution)/shard_map/ppermute | solution.py:321
  67.8 34.9 %collective-permute-start.4 = (f32[256,128]{1,0:T(8,128)S(1)}, f32[256,128]{1,0:T(8,128)S(1)}, u32[]{:S(2)}, u32[]{:S(2)}) collective-permute-start(f32[256,128]{1,0:T(8,128)S(1)} %get-tuple-element.42.refs_2_), channel_id=1, source_target_pairs={{0,1},{1,2},{2,3},{3,4},{4,5},{5,6},{6,7},{7,8},{8,9},{9,10},{10,1... | collective-permute-start | bytes 393224 | tf_op jit(solution)/shard_map/ppermute | solution.py:321
  67.8 41.8 %collective-permute-start.2 = (f32[640,128]{1,0:T(8,128)S(1)}, f32[640,128]{1,0:T(8,128)S(1)}, u32[]{:S(2)}, u32[]{:S(2)}) collective-permute-start(f32[640,128]{1,0:T(8,128)S(1)} %get-tuple-element.40.refs_0_), channel_id=1, source_target_pairs={{0,1},{1,2},{2,3},{3,4},{4,5},{5,6},{6,7},{7,8},{8,9},{9,10},{10,1... | collective-permute-start | bytes 983048 | tf_op jit(solution)/shard_map/ppermute | solution.py:321
  73.1 6.8 %collective-permute-start.26 = (f32[8,128]{1,0:T(8,128)S(1)}, f32[8,128]{1,0:T(8,128)S(1)}, u32[]{:S(2)}, u32[]{:S(2)}) collective-permute-start(f32[8,128]{1,0:T(8,128)S(1)} %max.30), channel_id=1, source_target_pairs={{0,7},{1,0},{2,1},{3,2},{4,3},{5,4},{6,5},{7,6},{8,15},{9,8},{10,9... | collective-permute-start | bytes 12296 | tf_op jit(solution)/shard_map/ppermute | solution.py:339
  78.4 27.9 %collective-permute-start.3 = (f32[384,128]{1,0:T(8,128)S(1)}, f32[384,128]{1,0:T(8,128)S(1)}, u32[]{:S(2)}, u32[]{:S(2)}) collective-permute-start(f32[384,128]{1,0:T(8,128)S(1)} %get-tuple-element.41.refs_1_), channel_id=1, source_target_pairs={{0,1},{1,2},{2,3},{3,4},{4,5},{5,6},{6,7},{7,8},{8,9},{9,10},{10,1... | collective-permute-start | bytes 589832 | tf_op jit(solution)/shard_map/ppermute | solution.py:321
  78.5 39.9 %collective-permute-start.21 = (f32[512,128]{1,0:T(8,128)S(1)}, f32[512,128]{1,0:T(8,128)S(1)}, u32[]{:S(2)}, u32[]{:S(2)}) collective-permute-start(f32[512,128]{1,0:T(8,128)S(1)} %get-tuple-element.66), channel_id=1, source_target_pairs={{0,1},{1,2},{2,3},{3,4},{4,5},{5,6},{6,7},{7,8},{8,9},{9,10},{10,1... | collective-permute-start | bytes 786440 | tf_op jit(solution)/shard_map/ppermute | solution.py:321
  79.9 6.6 %collective-permute-start.29 = (f32[8,128]{1,0:T(8,128)S(1)}, f32[8,128]{1,0:T(8,128)S(1)}, u32[]{:S(2)}, u32[]{:S(2)}) collective-permute-start(f32[8,128]{1,0:T(8,128)S(1)} %maximum_maximum_fusion), channel_id=1, source_target_pairs={{0,5},{1,6},{2,7},{3,0},{4,1},{5,2},{6,3},{7,4},{8,13},{9,14},{10,... | collective-permute-start | bytes 12296 | tf_op jit(solution)/shard_map/ppermute | solution.py:339
  99.6 18.8 %collective-permute-start.22 = (f32[512,128]{1,0:T(8,128)S(1)}, f32[512,128]{1,0:T(8,128)S(1)}, u32[]{:S(2)}, u32[]{:S(2)}) collective-permute-start(f32[512,128]{1,0:T(8,128)S(1)} %get-tuple-element.67), channel_id=1, source_target_pairs={{0,1},{1,2},{2,3},{3,4},{4,5},{5,6},{6,7},{7,8},{8,9},{9,10},{10,1... | collective-permute-start | bytes 786440 | tf_op jit(solution)/shard_map/ppermute | solution.py:321
  106.2 12.1 %collective-permute-start.25 = (f32[256,128]{1,0:T(8,128)S(1)}, f32[256,128]{1,0:T(8,128)S(1)}, u32[]{:S(2)}, u32[]{:S(2)}) collective-permute-start(f32[256,128]{1,0:T(8,128)S(1)} %get-tuple-element.70), channel_id=1, source_target_pairs={{0,1},{1,2},{2,3},{3,4},{4,5},{5,6},{6,7},{7,8},{8,9},{9,10},{10,1... | collective-permute-start | bytes 393224 | tf_op jit(solution)/shard_map/ppermute | solution.py:321
  108.3 15.7 %collective-permute-start.23 = (f32[512,128]{1,0:T(8,128)S(1)}, f32[512,128]{1,0:T(8,128)S(1)}, u32[]{:S(2)}, u32[]{:S(2)}) collective-permute-start(f32[512,128]{1,0:T(8,128)S(1)} %get-tuple-element.68), channel_id=1, source_target_pairs={{0,1},{1,2},{2,3},{3,4},{4,5},{5,6},{6,7},{7,8},{8,9},{9,10},{10,1... | collective-permute-start | bytes 786440 | tf_op jit(solution)/shard_map/ppermute | solution.py:321
  115.1 28.3 %collective-permute-start.18 = (f32[640,128]{1,0:T(8,128)S(1)}, f32[640,128]{1,0:T(8,128)S(1)}, u32[]{:S(2)}, u32[]{:S(2)}) collective-permute-start(f32[640,128]{1,0:T(8,128)S(1)} %get-tuple-element.63), channel_id=1, source_target_pairs={{0,1},{1,2},{2,3},{3,4},{4,5},{5,6},{6,7},{7,8},{8,9},{9,10},{10,1... | collective-permute-start | bytes 983048 | tf_op jit(solution)/shard_map/ppermute | solution.py:321
  118.4 18.7 %collective-permute-start.24 = (f32[512,128]{1,0:T(8,128)S(1)}, f32[512,128]{1,0:T(8,128)S(1)}, u32[]{:S(2)}, u32[]{:S(2)}) collective-permute-start(f32[512,128]{1,0:T(8,128)S(1)} %get-tuple-element.69), channel_id=1, source_target_pairs={{0,1},{1,2},{2,3},{3,4},{4,5},{5,6},{6,7},{7,8},{8,9},{9,10},{10,1... | collective-permute-start | bytes 786440 | tf_op jit(solution)/shard_map/ppermute | solution.py:321
  118.4 22.9 %collective-permute-start.20 = (f32[512,128]{1,0:T(8,128)S(1)}, f32[512,128]{1,0:T(8,128)S(1)}, u32[]{:S(2)}, u32[]{:S(2)}) collective-permute-start(f32[512,128]{1,0:T(8,128)S(1)} %get-tuple-element.65), channel_id=1, source_target_pairs={{0,1},{1,2},{2,3},{3,4},{4,5},{5,6},{6,7},{7,8},{8,9},{9,10},{10,1... | collective-permute-start | bytes 786440 | tf_op jit(solution)/shard_map/ppermute | solution.py:321
  118.4 25.0 %collective-permute-start.19 = (f32[384,128]{1,0:T(8,128)S(1)}, f32[384,128]{1,0:T(8,128)S(1)}, u32[]{:S(2)}, u32[]{:S(2)}) collective-permute-start(f32[384,128]{1,0:T(8,128)S(1)} %get-tuple-element.64), channel_id=1, source_target_pairs={{0,1},{1,2},{2,3},{3,4},{4,5},{5,6},{6,7},{7,8},{8,9},{9,10},{10,1... | collective-permute-start | bytes 589832 | tf_op jit(solution)/shard_map/ppermute | solution.py:321
  124.0 20.8 %collective-permute-start.17 = (f32[256,128]{1,0:T(8,128)S(1)}, f32[256,128]{1,0:T(8,128)S(1)}, u32[]{:S(2)}, u32[]{:S(2)}) collective-permute-start(f32[256,128]{1,0:T(8,128)S(1)} %get-tuple-element.62), channel_id=1, source_target_pairs={{0,1},{1,2},{2,3},{3,4},{4,5},{5,6},{6,7},{7,8},{8,9},{9,10},{10,1... | collective-permute-start | bytes 393224 | tf_op jit(solution)/shard_map/ppermute | solution.py:321
  (12 other events, 58.9 us)

commit v3 on v2

--- a/solution.py
+++ b/solution.py
@@ -13,8 +13,9 @@
 B = 128
 PACK = 136
 UNITS = 32
-FRONT = (4, 4, 4, 4, 4, 2)
-BACK = (5, 3, 2)
+FRONT = (4, 8, 8)
+BACK = (8, 4)
+RELAYED = 1
 
 VM = pl.BlockSpec(memory_space=pltpu.VMEM)
 ANY = pl.BlockSpec(memory_space=pl.ANY)
@@ -164,7 +165,6 @@
         ],
         compiler_params=params(8),
         cost_estimate=cost(30e6, 1e6),
-        name="roots",
     )(*parts)
 
 
@@ -245,8 +245,10 @@
     )(*operands)
 
 
-def second_body(rows0, aliased, count, *refs):
+def second_body(rows0, aliased, count, joined, *refs):
     xs = refs[:count]
+    others = refs[count : 2 * count] if joined else [None] * count
+    refs = refs[count:] if joined else refs
     rs = refs[count : 2 * count]
     wh_ref, wl_ref = refs[2 * count : 2 * count + 2]
     rest = refs[2 * count + 2 + (1 if aliased else 0) :]
@@ -255,9 +257,10 @@
     held, sem = rest[1 + count :]
     wh, wl = wh_ref[...], wl_ref[...]
     at = 0
-    for x, r, y in zip(xs, rs, ys):
+    for x, other, r, y in zip(xs, others, rs, ys):
         size = x.shape[0]
-        value = mixed(jnp.concatenate([x[...], r[...]], axis=1), wh, wl)
+        left = x[...] if other is None else x[...] + other[...]
+        value = mixed(jnp.concatenate([left, r[...]], axis=1), wh, wl)
         held[at : at + size, :] = value[:, :B]
         y[...] = value[:, B:]
         at += size
@@ -266,15 +269,15 @@
     copy.wait()
 
 
-def second(xs, rs, w, out, rows, rows0):
+def second(xs, rs, w, out, rows, rows0, others=()):
     total = sum(x.shape[0] for x in xs)
     shapes = [jax.ShapeDtypeStruct((rows, 2 * B), F32)] + [
         jax.ShapeDtypeStruct(x.shape, F32) for x in xs
     ]
-    operands = [*xs, *rs, *w] + ([out] if out is not None else [])
-    specs = [VM] * (2 * len(xs) + 2) + ([HBM] if out is not None else [])
-    return pl.pallas_call(
-        functools.partial(second_body, rows0, out is not None, len(xs)),
+    operands = [*xs, *others, *rs, *w] + ([out] if out is not None else [])
+    specs = [VM] * (2 * len(xs) + len(others) + 2) + ([HBM] if out is not None else [])
+    return pl.pallas_call(
+        functools.partial(second_body, rows0, out is not None, len(xs), bool(others)),
         in_specs=specs,
         out_specs=[HBM] + [VM] * len(xs),
         out_shape=shapes,
@@ -316,9 +319,24 @@
     )(*ys, out)
 
 
-def shifted(value, steps):
+def shifted(value, steps, without=()):
     count = lax.axis_size("blk")
-    return lax.ppermute(value, "blk", [(s, (s + steps) % count) for s in range(count)])
+    routes = [(s, (s + steps) % count) for s in range(count) if s not in without]
+    return lax.ppermute(value, "blk", routes)
+
+
+def far_shifts():
+    count = lax.axis_size("blk")
+    plane = 32
+    if count % plane:
+        return {}
+    ends = range(plane - 1, count, plane)
+    return {s: (s - 3, (s + 2) % count, (s + 1) % count) for s in ends}
+
+
+def relayed(value, leg):
+    stops = [(s, *far) for s, far in far_shifts().items()]
+    return lax.ppermute(value, "blk", [(t[leg], t[leg + 1]) for t in stops])
 
 
 def of_group(value):
@@ -352,14 +370,13 @@
         ring = inner * middle
         return lambda s: s // ring * ring + (s + steps * inner) % ring
 
+    rounds = [[along_middle(-1)] for _ in range(1, middle)]
     reach = min(4, inner)
-    rounds = [[along_inner(-n) for n in range(1, reach)]]
+    rounds.append([along_inner(-n) for n in range(1, reach)])
     while reach < inner:
         step = min(3, inner - reach)
         rounds.append([along_inner(-step)])
         reach += step
-    for _ in range(1, middle):
-        rounds.append([along_middle(-1)])
     for n in range(1, outer):
         rounds.append([lambda s, n=n: (s + n * inner * middle) % count])
     for moves in rounds:
@@ -406,7 +423,14 @@
     got = [shifted(x, 1) for x in xf]
     behind = [shifted(r, -1) for r in rb]
     helped = shifted(partial(xb, behind, [], [], False), 1)
-    got_back = [shifted(x, 1) for x in xb]
+    far = far_shifts()
+    got_back = [shifted(x, 1, far) for x in xb]
+    relays = xb[:RELAYED] if far else []
+    for leg in range(3):
+        relays = [relayed(x, leg) for x in relays]
+    if far:
+        near = set(range(lax.axis_size("blk"))) - set(far)
+        relays += [shifted(x, 1, near) for x in xb[RELAYED:]]
 
     cut = len(got) - 1
     sums = partial(got[:cut], rf[:cut], rb, [])
@@ -416,7 +440,7 @@
 
     out, *ys = second(got[:1], rf[:1], w, None, rows, 0)
     out, *more_y = second(got[1:], rf[1:], w, out, rows, front[0])
-    out, *back_y = second(got_back, rb, w, out, rows, front_rows)
+    out, *back_y = second(got_back, rb, w, out, rows, front_rows, relays)
     ys = [*ys, *more_y, *back_y]
     arrived = [shifted(y, 1) for y in ys]
 
@@ -425,7 +449,8 @@
     for y in ys:
         places.append(at)
         at += y.shape[0]
-    for lo, hi in ((0, 6), (6, 8), (8, 9)):
+    last = len(ys) - 1
+    for lo, hi in ((0, last), (last, last + 1)):
         out = place(arrived[lo:hi], places[lo:hi], out)
     return out, off_measure
 

time: 147 us -> 153 us (1.041)
  starting transfers between devices: 50.9 us -> 67.4 us
  waiting for transfers between devices: 74.2 us -> 65.2 us
    ppermute x22 -> x17, waiting for transfers between devices: 57.8 us -> 45.7 us  [the longest x14 45.7 us: shifted(): return lax.ppermute(value, 'blk', routes)]
    ppermute x9, starting transfers between devices: 20.9 us -> 30 us  [moved(): return lax.ppermute(value, 'blk', [(s, where(s)) for s in range(count)])]
    ppermute x22 -> x17, starting transfers between devices: 26.2 us -> 33.3 us  [the longest x14 30.6 us: shifted(): return lax.ppermute(value, 'blk', routes)]
    ppermute x9, waiting for transfers between devices: 8.49 us -> 11.5 us  [moved(): return lax.ppermute(value, 'blk', [(s, where(s)) for s in range(count)])]
  transfers between devices with their start and end apart: 35 -> 30, of which waited for: 22 -> 16; matrix products, arithmetic and copies ran while one was open for 0% -> 0% of each run, Pallas kernels for 8% -> 7%
where the time goes in v3:
time: 153 us; the launch traced here: 152 us
  starting transfers between devices  67.4 us (44%)
  waiting for transfers between devices  65.2 us (43%)
  Pallas kernels  18.6 us (12%)
    ppermute x14, waiting for transfers between devices, shifted(): return lax.ppermute(value, 'blk', routes)  45.7 us
    ppermute x14, starting transfers between devices, shifted(): return lax.ppermute(value, 'blk', routes)  30.6 us
    ppermute x9, starting transfers between devices, moved(): return lax.ppermute(value, 'blk', [(s, where(s)) for s in range(count)])  30 us
    ppermute x9, waiting for transfers between devices, moved(): return lax.ppermute(value, 'blk', [(s, where(s)) for s in range(count)])  11.5 us
    ppermute x4, waiting for transfers between devices, from_other(): return lax.ppermute(part, 'row', [(s, s ^ mask) for s in range(count)])  7.96 us
    pallas_call x3, Pallas kernels, second(): pl.pallas_call(functools.partial(second_body, rows0, out is not None, len...  4.74 us
    pallas_call x2, Pallas kernels, roots(): pl.pallas_call(functools.partial(root_body, slot), in_specs=[VM] * 2, out...  4.13 us
    ppermute x4, starting transfers between devices, from_other(): return lax.ppermute(part, 'row', [(s, s ^ mask) for s in range(count)])  4.04 us
  transfers between devices with their start and end apart: 30, of which 16 were waited for; matrix products, arithmetic and copies ran while one was open for 0% of the time, Pallas kernels for 7%

profile of v3, /device:TPU:8, one launch (start us, length us, event | category | flops | bytes accessed | tf_op | source)
XLA Modules:
  0.0 152.4 jit_solution(6573862943554152057)
XLA Ops:
  0.6 3.8 %first_gram.1 = f32[136,128]{1,0:T(8,128)S(1)} custom-call(f32[4096,256]{1,0:T(8,128)} %m_ref.7), custom_call_target="tpu_custom_call" | custom-call | flops 536870912 | bytes 4194304 | tf_op jit(solution)/shard_map/first_gram/pallas_call | solution.py:95
  5.8 2.2 %collective-permute-start.1 = (f32[136,128]{1,0:T(8,128)S(1)}, f32[136,128]{1,0:T(8,128)S(1)}, u32[]{:S(2)}, u32[]{:S(2)}) collective-permute-start(f32[136,128]{1,0:T(8,128)S(1)} %add.6.a_ref), channel_id=1, source_target_pairs={{0,128},{64,192},{128,0},{192,64},{1,129},{65,193},{129,1},{193,65... | collective-permute-start | bytes 208904 | tf_op jit(solution)/shard_map/ppermute | solution.py:346
  8.0 2.5 %collective-permute-done.1.b_ref = f32[136,128]{1,0:T(8,128)S(1)} collective-permute-done((f32[136,128]{1,0:T(8,128)S(1)}, f32[136,128]{1,0:T(8,128)S(1)}, u32[]{:S(2)}, u32[]{:S(2)}) %collective-permute-start.1) | collective-permute-done | bytes 69664 | tf_op jit(solution)/shard_map/ppermute | solution.py:346
  10.5 2.1 %shard_map.30 = (bf16[256,256]{1,0:T(8,128)(2,1)S(1)}, bf16[256,256]{1,0:T(8,128)(2,1)S(1)}, f32[8,128]{1,0:T(8,128)S(1)}) custom-call(f32[136,128]{1,0:T(8,128)S(1)} %add.6.a_ref, f32[136,128]{1,0:T(8,128)S(1)} %collective-permute-done.1.b_ref), custom_call_target="tpu_custom_call" | custom-call | flops 30000000 | bytes 1000000 | tf_op jit(solution)/shard_map/pallas_call | solution.py:157
  14.1 12.7 %collective-permute-start.11 = (f32[1024,128]{1,0:T(8,128)S(1)}, f32[1024,128]{1,0:T(8,128)S(1)}, u32[]{:S(2)}, u32[]{:S(2)}) collective-permute-start(f32[1024,128]{1,0:T(8,128)S(1)} %get-tuple-element.30.refs_4_), channel_id=1, source_target_pairs={{0,63},{1,0},{2,1},{3,2},{4,3},{5,4},{6,5},{7,6},{8,7},{9,8},{10,9... | collective-permute-start | bytes 1572872 | tf_op jit(solution)/shard_map/ppermute | solution.py:325
  27.5 12.3 %collective-permute-start.12 = (f32[512,128]{1,0:T(8,128)S(1)}, f32[512,128]{1,0:T(8,128)S(1)}, u32[]{:S(2)}, u32[]{:S(2)}) collective-permute-start(f32[512,128]{1,0:T(8,128)S(1)} %get-tuple-element.31.refs_5_), channel_id=1, source_target_pairs={{0,63},{1,0},{2,1},{3,2},{4,3},{5,4},{6,5},{7,6},{8,7},{9,8},{10,9... | collective-permute-start | bytes 786440 | tf_op jit(solution)/shard_map/ppermute | solution.py:325
  41.3 2.3 %collective-permute-done.12.refs_3_ = f32[512,128]{1,0:T(8,128)S(1)} collective-permute-done((f32[512,128]{1,0:T(8,128)S(1)}, f32[512,128]{1,0:T(8,128)S(1)}, u32[]{:S(2)}, u32[]{:S(2)}) %collective-permute-start.12) | collective-permute-done | bytes 262176 | tf_op jit(solution)/shard_map/ppermute | solution.py:325
  46.7 26.5 %collective-permute-done.9.refs_0_ = f32[512,128]{1,0:T(8,128)S(1)} collective-permute-done((f32[512,128]{1,0:T(8,128)S(1)}, f32[512,128]{1,0:T(8,128)S(1)}, u32[]{:S(2)}, u32[]{:S(2)}) %collective-permute-start.9) | collective-permute-done | bytes 262176 | tf_op jit(solution)/shard_map/ppermute | solution.py:325
  76.2 7.1 %collective-permute-done.13.refs_3_ = f32[136,128]{1,0:T(8,128)S(1)} collective-permute-done((f32[136,128]{1,0:T(8,128)S(1)}, f32[136,128]{1,0:T(8,128)S(1)}, u32[]{:S(2)}, u32[]{:S(2)}) %collective-permute-start.13) | collective-permute-done | bytes 69664 | tf_op jit(solution)/shard_map/ppermute | solution.py:325
  86.7 3.0 %collective-permute-done.15.b_ref = f32[136,128]{1,0:T(8,128)S(1)} collective-permute-done((f32[136,128]{1,0:T(8,128)S(1)}, f32[136,128]{1,0:T(8,128)S(1)}, u32[]{:S(2)}, u32[]{:S(2)}) %collective-permute-start.15) | collective-permute-done | bytes 69664 | tf_op jit(solution)/shard_map/ppermute | solution.py:346
  89.7 2.1 %shard_map.37 = (bf16[256,256]{1,0:T(8,128)(2,1)S(1)}, bf16[256,256]{1,0:T(8,128)(2,1)S(1)}, f32[8,128]{1,0:T(8,128)S(1)}) custom-call(f32[136,128]{1,0:T(8,128)S(1)} %add.7.a_ref, f32[136,128]{1,0:T(8,128)S(1)} %collective-permute-done.15.b_ref), custom_call_target="tpu_custom_call" | custom-call | flops 30000000 | bytes 1000000 | tf_op jit(solution)/shard_map/pallas_call | solution.py:157
  92.9 2.0 %shard_map.39 = (f32[4096,256]{1,0:T(8,128)}, f32[1024,128]{1,0:T(8,128)S(1)}, f32[1024,128]{1,0:T(8,128)S(1)}) custom-call(f32[1024,128]{1,0:T(8,128)S(1)} %collective-permute-done.10.refs_1_.refs_0_, f32[1024,128]{1,0:T(8,128)S(1)} %collective-permute-done.8.refs_0_.refs_1_, ...), custom_call_target="tpu_custom_call", output_to_operand_aliasing={{0}: (6, {})} | custom-call | flops 805306368 | bytes 5242880 | tf_op jit(solution)/shard_map/pallas_call | solution.py:279
  96.9 2.1 %collective-permute-start.21 = (f32[8,128]{1,0:T(8,128)S(1)}, f32[8,128]{1,0:T(8,128)S(1)}, u32[]{:S(2)}, u32[]{:S(2)}) collective-permute-start(f32[8,128]{1,0:T(8,128)S(1)} %max.30), channel_id=1, source_target_pairs={{0,24},{1,25},{2,26},{3,27},{4,28},{5,29},{6,30},{7,31},{8,0},{9,1... | collective-permute-start | bytes 12296 | tf_op jit(solution)/shard_map/ppermute | solution.py:357
  100.5 3.3 %collective-permute-start.22 = (f32[8,128]{1,0:T(8,128)S(1)}, f32[8,128]{1,0:T(8,128)S(1)}, u32[]{:S(2)}, u32[]{:S(2)}) collective-permute-start(f32[8,128]{1,0:T(8,128)S(1)} %max.31), channel_id=1, source_target_pairs={{0,24},{1,25},{2,26},{3,27},{4,28},{5,29},{6,30},{7,31},{8,0},{9,1... | collective-permute-start | bytes 12296 | tf_op jit(solution)/shard_map/ppermute | solution.py:357
  105.2 3.5 %collective-permute-start.23 = (f32[8,128]{1,0:T(8,128)S(1)}, f32[8,128]{1,0:T(8,128)S(1)}, u32[]{:S(2)}, u32[]{:S(2)}) collective-permute-start(f32[8,128]{1,0:T(8,128)S(1)} %max.32), channel_id=1, source_target_pairs={{0,24},{1,25},{2,26},{3,27},{4,28},{5,29},{6,30},{7,31},{8,0},{9,1... | collective-permute-start | bytes 12296 | tf_op jit(solution)/shard_map/ppermute | solution.py:357
  110.0 4.5 %collective-permute-start.24 = (f32[8,128]{1,0:T(8,128)S(1)}, f32[8,128]{1,0:T(8,128)S(1)}, u32[]{:S(2)}, u32[]{:S(2)}) collective-permute-start(f32[8,128]{1,0:T(8,128)S(1)} %max.33), channel_id=1, source_target_pairs={{0,7},{1,0},{2,1},{3,2},{4,3},{5,4},{6,5},{7,6},{8,15},{9,8},{10,9... | collective-permute-start | bytes 12296 | tf_op jit(solution)/shard_map/ppermute | solution.py:357
  114.5 3.3 %collective-permute-start.25 = (f32[8,128]{1,0:T(8,128)S(1)}, f32[8,128]{1,0:T(8,128)S(1)}, u32[]{:S(2)}, u32[]{:S(2)}) collective-permute-start(f32[8,128]{1,0:T(8,128)S(1)} %max.33), channel_id=1, source_target_pairs={{0,6},{1,7},{2,0},{3,1},{4,2},{5,3},{6,4},{7,5},{8,14},{9,15},{10,... | collective-permute-start | bytes 12296 | tf_op jit(solution)/shard_map/ppermute | solution.py:357
  117.8 3.0 %collective-permute-start.26 = (f32[8,128]{1,0:T(8,128)S(1)}, f32[8,128]{1,0:T(8,128)S(1)}, u32[]{:S(2)}, u32[]{:S(2)}) collective-permute-start(f32[8,128]{1,0:T(8,128)S(1)} %max.33), channel_id=1, source_target_pairs={{0,5},{1,6},{2,7},{3,0},{4,1},{5,2},{6,3},{7,4},{8,13},{9,14},{10,... | collective-permute-start | bytes 12296 | tf_op jit(solution)/shard_map/ppermute | solution.py:357
  120.8 2.4 %collective-permute-done.26 = f32[8,128]{1,0:T(8,128)S(1)} collective-permute-done((f32[8,128]{1,0:T(8,128)S(1)}, f32[8,128]{1,0:T(8,128)S(1)}, u32[]{:S(2)}, u32[]{:S(2)}) %collective-permute-start.26) | collective-permute-done | bytes 4128 | tf_op jit(solution)/shard_map/ppermute | solution.py:357
  123.2 4.2 %collective-permute-start.27 = (f32[8,128]{1,0:T(8,128)S(1)}, f32[8,128]{1,0:T(8,128)S(1)}, u32[]{:S(2)}, u32[]{:S(2)}) collective-permute-start(f32[8,128]{1,0:T(8,128)S(1)} %maximum_maximum_fusion), channel_id=1, source_target_pairs={{0,5},{1,6},{2,7},{3,0},{4,1},{5,2},{6,3},{7,4},{8,13},{9,14},{10,... | collective-permute-start | bytes 12296 | tf_op jit(solution)/shard_map/ppermute | solution.py:357
  128.7 3.8 %collective-permute-start.28 = (f32[8,128]{1,0:T(8,128)S(1)}, f32[8,128]{1,0:T(8,128)S(1)}, u32[]{:S(2)}, u32[]{:S(2)}) collective-permute-start(f32[8,128]{1,0:T(8,128)S(1)} %max.37), channel_id=1, source_target_pairs={{0,7},{1,0},{2,1},{3,2},{4,3},{5,4},{6,5},{7,6},{8,15},{9,8},{10,9... | collective-permute-start | bytes 12296 | tf_op jit(solution)/shard_map/ppermute | solution.py:357
  133.9 2.3 %collective-permute-start.29 = (f32[8,128]{1,0:T(8,128)S(1)}, f32[8,128]{1,0:T(8,128)S(1)}, u32[]{:S(2)}, u32[]{:S(2)}) collective-permute-start(f32[8,128]{1,0:T(8,128)S(1)} %max.38), channel_id=1, source_target_pairs={{0,32},{1,33},{2,34},{3,35},{4,36},{5,37},{6,38},{7,39},{8,40},{9,... | collective-permute-start | bytes 12296 | tf_op jit(solution)/shard_map/ppermute | solution.py:357
  137.0 2.3 %collective-permute-done.29 = f32[8,128]{1,0:T(8,128)S(1)} collective-permute-done((f32[8,128]{1,0:T(8,128)S(1)}, f32[8,128]{1,0:T(8,128)S(1)}, u32[]{:S(2)}, u32[]{:S(2)}) %collective-permute-start.29) | collective-permute-done | bytes 4128 | tf_op jit(solution)/shard_map/ppermute | solution.py:357
  140.5 7.7 %collective-permute-done.17.refs_0_ = f32[512,128]{1,0:T(8,128)S(1)} collective-permute-done((f32[512,128]{1,0:T(8,128)S(1)}, f32[512,128]{1,0:T(8,128)S(1)}, u32[]{:S(2)}, u32[]{:S(2)}) %collective-permute-start.17) | collective-permute-done | bytes 262176 | tf_op jit(solution)/shard_map/ppermute | solution.py:325
  (63 shorter events, 30.4 us)
Async XLA Ops:
  13.4 13.4 %collective-permute-start.4 = (f32[1024,128]{1,0:T(8,128)S(1)}, f32[1024,128]{1,0:T(8,128)S(1)}, u32[]{:S(2)}, u32[]{:S(2)}) collective-permute-start(f32[1024,128]{1,0:T(8,128)S(1)} %get-tuple-element.28.refs_0_), channel_id=1, source_target_pairs={{31,28},{63,60},{95,92},{127,124},{159,156},{191,188},{223,220},{2... | collective-permute-start | bytes 1572872 | tf_op jit(solution)/shard_map/ppermute | solution.py:339
  14.1 29.5 %collective-permute-start.11 = (f32[1024,128]{1,0:T(8,128)S(1)}, f32[1024,128]{1,0:T(8,128)S(1)}, u32[]{:S(2)}, u32[]{:S(2)}) collective-permute-start(f32[1024,128]{1,0:T(8,128)S(1)} %get-tuple-element.30.refs_4_), channel_id=1, source_target_pairs={{0,63},{1,0},{2,1},{3,2},{4,3},{5,4},{6,5},{7,6},{8,7},{9,8},{10,9... | collective-permute-start | bytes 1572872 | tf_op jit(solution)/shard_map/ppermute | solution.py:325
  26.8 18.2 %collective-permute-start.5 = (f32[1024,128]{1,0:T(8,128)S(1)}, f32[1024,128]{1,0:T(8,128)S(1)}, u32[]{:S(2)}, u32[]{:S(2)}) collective-permute-start(f32[1024,128]{1,0:T(8,128)S(1)} %collective-permute-done.4), channel_id=1, source_target_pairs={{28,33},{60,1},{92,97},{124,65},{156,161},{188,129},{220,225},{252... | collective-permute-start | bytes 1572872 | tf_op jit(solution)/shard_map/ppermute | solution.py:339
  27.5 16.1 %collective-permute-start.12 = (f32[512,128]{1,0:T(8,128)S(1)}, f32[512,128]{1,0:T(8,128)S(1)}, u32[]{:S(2)}, u32[]{:S(2)}) collective-permute-start(f32[512,128]{1,0:T(8,128)S(1)} %get-tuple-element.31.refs_5_), channel_id=1, source_target_pairs={{0,63},{1,0},{2,1},{3,2},{4,3},{5,4},{6,5},{7,6},{8,7},{9,8},{10,9... | collective-permute-start | bytes 786440 | tf_op jit(solution)/shard_map/ppermute | solution.py:325
  40.7 32.5 %collective-permute-start.10 = (f32[1024,128]{1,0:T(8,128)S(1)}, f32[1024,128]{1,0:T(8,128)S(1)}, u32[]{:S(2)}, u32[]{:S(2)}) collective-permute-start(f32[1024,128]{1,0:T(8,128)S(1)} %get-tuple-element.35), channel_id=1, source_target_pairs={{0,1},{1,2},{2,3},{3,4},{4,5},{5,6},{6,7},{7,8},{8,9},{9,10},{10,1... | collective-permute-start | bytes 1572872 | tf_op jit(solution)/shard_map/ppermute | solution.py:325
  40.8 33.7 %collective-permute-start.8 = (f32[1024,128]{1,0:T(8,128)S(1)}, f32[1024,128]{1,0:T(8,128)S(1)}, u32[]{:S(2)}, u32[]{:S(2)}) collective-permute-start(f32[1024,128]{1,0:T(8,128)S(1)} %get-tuple-element.32), channel_id=1, source_target_pairs={{0,1},{1,2},{2,3},{3,4},{4,5},{5,6},{6,7},{7,8},{8,9},{9,10},{10,1... | collective-permute-start | bytes 1572872 | tf_op jit(solution)/shard_map/ppermute | solution.py:325
  43.6 29.6 %collective-permute-start.9 = (f32[512,128]{1,0:T(8,128)S(1)}, f32[512,128]{1,0:T(8,128)S(1)}, u32[]{:S(2)}, u32[]{:S(2)}) collective-permute-start(f32[512,128]{1,0:T(8,128)S(1)} %get-tuple-element.34), channel_id=1, source_target_pairs={{0,1},{1,2},{2,3},{3,4},{4,5},{5,6},{6,7},{7,8},{8,9},{9,10},{10,1... | collective-permute-start | bytes 786440 | tf_op jit(solution)/shard_map/ppermute | solution.py:325
  43.6 51.4 %collective-permute-start.2 = (f32[1024,128]{1,0:T(8,128)S(1)}, f32[1024,128]{1,0:T(8,128)S(1)}, u32[]{:S(2)}, u32[]{:S(2)}) collective-permute-start(f32[1024,128]{1,0:T(8,128)S(1)} %get-tuple-element.28.refs_0_), channel_id=1, source_target_pairs={{0,1},{1,2},{2,3},{3,4},{4,5},{5,6},{6,7},{7,8},{8,9},{9,10},{10,1... | collective-permute-start | bytes 1572872 | tf_op jit(solution)/shard_map/ppermute | solution.py:325
  44.9 50.1 %collective-permute-start.6 = (f32[1024,128]{1,0:T(8,128)S(1)}, f32[1024,128]{1,0:T(8,128)S(1)}, u32[]{:S(2)}, u32[]{:S(2)}) collective-permute-start(f32[1024,128]{1,0:T(8,128)S(1)} %collective-permute-done.5), channel_id=1, source_target_pairs={{33,32},{1,0},{97,96},{65,64},{161,160},{129,128},{225,224},{193,1... | collective-permute-start | bytes 1572872 | tf_op jit(solution)/shard_map/ppermute | solution.py:339
  73.2 10.2 %collective-permute-start.13 = (f32[136,128]{1,0:T(8,128)S(1)}, f32[136,128]{1,0:T(8,128)S(1)}, u32[]{:S(2)}, u32[]{:S(2)}) collective-permute-start(f32[136,128]{1,0:T(8,128)S(1)} %shard_map.35), channel_id=1, source_target_pairs={{0,1},{1,2},{2,3},{3,4},{4,5},{5,6},{6,7},{7,8},{8,9},{9,10},{10,1... | collective-permute-start | bytes 208904 | tf_op jit(solution)/shard_map/ppermute | solution.py:325
  73.2 21.7 %collective-permute-start.3 = (f32[512,128]{1,0:T(8,128)S(1)}, f32[512,128]{1,0:T(8,128)S(1)}, u32[]{:S(2)}, u32[]{:S(2)}) collective-permute-start(f32[512,128]{1,0:T(8,128)S(1)} %get-tuple-element.29.refs_1_), channel_id=1, source_target_pairs={{0,1},{1,2},{2,3},{3,4},{4,5},{5,6},{6,7},{7,8},{8,9},{9,10},{10,1... | collective-permute-start | bytes 786440 | tf_op jit(solution)/shard_map/ppermute | solution.py:325
  74.5 20.5 %collective-permute-start.7 = (f32[512,128]{1,0:T(8,128)S(1)}, f32[512,128]{1,0:T(8,128)S(1)}, u32[]{:S(2)}, u32[]{:S(2)}) collective-permute-start(f32[512,128]{1,0:T(8,128)S(1)} %get-tuple-element.29.refs_1_), channel_id=1, source_target_pairs={{31,32},{63,0},{95,96},{127,64},{159,160},{191,128},{223,224},{255... | collective-permute-start | bytes 786440 | tf_op jit(solution)/shard_map/ppermute | solution.py:325
  94.8 53.4 %collective-permute-start.18 = (f32[1024,128]{1,0:T(8,128)S(1)}, f32[1024,128]{1,0:T(8,128)S(1)}, u32[]{:S(2)}, u32[]{:S(2)}) collective-permute-start(f32[1024,128]{1,0:T(8,128)S(1)} %get-tuple-element.44), channel_id=1, source_target_pairs={{0,1},{1,2},{2,3},{3,4},{4,5},{5,6},{6,7},{7,8},{8,9},{9,10},{10,1... | collective-permute-start | bytes 1572872 | tf_op jit(solution)/shard_map/ppermute | solution.py:325
  94.9 53.3 %collective-permute-start.19 = (f32[1024,128]{1,0:T(8,128)S(1)}, f32[1024,128]{1,0:T(8,128)S(1)}, u32[]{:S(2)}, u32[]{:S(2)}) collective-permute-start(f32[1024,128]{1,0:T(8,128)S(1)} %get-tuple-element.45), channel_id=1, source_target_pairs={{0,1},{1,2},{2,3},{3,4},{4,5},{5,6},{6,7},{7,8},{8,9},{9,10},{10,1... | collective-permute-start | bytes 1572872 | tf_op jit(solution)/shard_map/ppermute | solution.py:325
  96.8 51.5 %collective-permute-start.20 = (f32[1024,128]{1,0:T(8,128)S(1)}, f32[1024,128]{1,0:T(8,128)S(1)}, u32[]{:S(2)}, u32[]{:S(2)}) collective-permute-start(f32[1024,128]{1,0:T(8,128)S(1)} %get-tuple-element.46), channel_id=1, source_target_pairs={{0,1},{1,2},{2,3},{3,4},{4,5},{5,6},{6,7},{7,8},{8,9},{9,10},{10,1... | collective-permute-start | bytes 1572872 | tf_op jit(solution)/shard_map/ppermute | solution.py:325
  105.2 4.8 %collective-permute-start.23 = (f32[8,128]{1,0:T(8,128)S(1)}, f32[8,128]{1,0:T(8,128)S(1)}, u32[]{:S(2)}, u32[]{:S(2)}) collective-permute-start(f32[8,128]{1,0:T(8,128)S(1)} %max.32), channel_id=1, source_target_pairs={{0,24},{1,25},{2,26},{3,27},{4,28},{5,29},{6,30},{7,31},{8,0},{9,1... | collective-permute-start | bytes 12296 | tf_op jit(solution)/shard_map/ppermute | solution.py:357
  110.0 7.8 %collective-permute-start.24 = (f32[8,128]{1,0:T(8,128)S(1)}, f32[8,128]{1,0:T(8,128)S(1)}, u32[]{:S(2)}, u32[]{:S(2)}) collective-permute-start(f32[8,128]{1,0:T(8,128)S(1)} %max.33), channel_id=1, source_target_pairs={{0,7},{1,0},{2,1},{3,2},{4,3},{5,4},{6,5},{7,6},{8,15},{9,8},{10,9... | collective-permute-start | bytes 12296 | tf_op jit(solution)/shard_map/ppermute | solution.py:357
  114.5 6.3 %collective-permute-start.25 = (f32[8,128]{1,0:T(8,128)S(1)}, f32[8,128]{1,0:T(8,128)S(1)}, u32[]{:S(2)}, u32[]{:S(2)}) collective-permute-start(f32[8,128]{1,0:T(8,128)S(1)} %max.33), channel_id=1, source_target_pairs={{0,6},{1,7},{2,0},{3,1},{4,2},{5,3},{6,4},{7,5},{8,14},{9,15},{10,... | collective-permute-start | bytes 12296 | tf_op jit(solution)/shard_map/ppermute | solution.py:357
  117.8 5.4 %collective-permute-start.26 = (f32[8,128]{1,0:T(8,128)S(1)}, f32[8,128]{1,0:T(8,128)S(1)}, u32[]{:S(2)}, u32[]{:S(2)}) collective-permute-start(f32[8,128]{1,0:T(8,128)S(1)} %max.33), channel_id=1, source_target_pairs={{0,5},{1,6},{2,7},{3,0},{4,1},{5,2},{6,3},{7,4},{8,13},{9,14},{10,... | collective-permute-start | bytes 12296 | tf_op jit(solution)/shard_map/ppermute | solution.py:357
  123.2 5.5 %collective-permute-start.27 = (f32[8,128]{1,0:T(8,128)S(1)}, f32[8,128]{1,0:T(8,128)S(1)}, u32[]{:S(2)}, u32[]{:S(2)}) collective-permute-start(f32[8,128]{1,0:T(8,128)S(1)} %maximum_maximum_fusion), channel_id=1, source_target_pairs={{0,5},{1,6},{2,7},{3,0},{4,1},{5,2},{6,3},{7,4},{8,13},{9,14},{10,... | collective-permute-start | bytes 12296 | tf_op jit(solution)/shard_map/ppermute | solution.py:357
  128.7 5.1 %collective-permute-start.28 = (f32[8,128]{1,0:T(8,128)S(1)}, f32[8,128]{1,0:T(8,128)S(1)}, u32[]{:S(2)}, u32[]{:S(2)}) collective-permute-start(f32[8,128]{1,0:T(8,128)S(1)} %max.37), channel_id=1, source_target_pairs={{0,7},{1,0},{2,1},{3,2},{4,3},{5,4},{6,5},{7,6},{8,15},{9,8},{10,9... | collective-permute-start | bytes 12296 | tf_op jit(solution)/shard_map/ppermute | solution.py:357
  133.9 5.5 %collective-permute-start.29 = (f32[8,128]{1,0:T(8,128)S(1)}, f32[8,128]{1,0:T(8,128)S(1)}, u32[]{:S(2)}, u32[]{:S(2)}) collective-permute-start(f32[8,128]{1,0:T(8,128)S(1)} %max.38), channel_id=1, source_target_pairs={{0,32},{1,33},{2,34},{3,35},{4,36},{5,37},{6,38},{7,39},{8,40},{9,... | collective-permute-start | bytes 12296 | tf_op jit(solution)/shard_map/ppermute | solution.py:357
  136.2 12.1 %collective-permute-start.17 = (f32[512,128]{1,0:T(8,128)S(1)}, f32[512,128]{1,0:T(8,128)S(1)}, u32[]{:S(2)}, u32[]{:S(2)}) collective-permute-start(f32[512,128]{1,0:T(8,128)S(1)} %get-tuple-element.43), channel_id=1, source_target_pairs={{0,1},{1,2},{2,3},{3,4},{4,5},{5,6},{6,7},{7,8},{8,9},{9,10},{10,1... | collective-permute-start | bytes 786440 | tf_op jit(solution)/shard_map/ppermute | solution.py:325
  139.3 12.2 %collective-permute-start.16 = (f32[512,128]{1,0:T(8,128)S(1)}, f32[512,128]{1,0:T(8,128)S(1)}, u32[]{:S(2)}, u32[]{:S(2)}) collective-permute-start(f32[512,128]{1,0:T(8,128)S(1)} %get-tuple-element.42), channel_id=1, source_target_pairs={{0,1},{1,2},{2,3},{3,4},{4,5},{5,6},{6,7},{7,8},{8,9},{9,10},{10,1... | collective-permute-start | bytes 786440 | tf_op jit(solution)/shard_map/ppermute | solution.py:325
  (7 other events, 32.3 us)

commit v4 on v3

--- a/solution.py
+++ b/solution.py
@@ -13,7 +13,7 @@
 B = 128
 PACK = 136
 UNITS = 32
-FRONT = (4, 8, 8)
+FRONT = (4, 16)
 BACK = (8, 4)
 RELAYED = 1
 
@@ -95,15 +95,17 @@
     return pl.pallas_call(
         functools.partial(gram_body, 8),
         in_specs=[HBM],
-        out_specs=VM,
-        out_shape=jax.ShapeDtypeStruct((PACK, B), F32),
+        out_specs=[VM, VM],
+        out_shape=[
+            jax.ShapeDtypeStruct((PACK, B), F32),
+            jax.ShapeDtypeStruct(matrix.shape, F32),
+        ],
         scratch_shapes=[
-            pltpu.VMEM(matrix.shape, F32),
             pltpu.VMEM((B, B), F32),
             pltpu.VMEM((8, 2 * B), F32),
             pltpu.SemaphoreType.DMA((8,)),
         ],
-        compiler_params=params(52),
+        compiler_params=params(48),
         cost_estimate=cost(rows * B * B * 8, rows * B * 8),
         name="first_gram",
     )(matrix)
@@ -412,7 +414,8 @@
     back = [n * unit for n in BACK]
     front_rows = sum(front)
 
-    wh, wl, squares0 = roots(of_group(first_gram(matrix)), 0)
+    sums, matrix = first_gram(matrix)
+    wh, wl, squares0 = roots(of_group(sums), 0)
     w = (wh, wl)
 
     xf, rf = update(matrix, w, 0, front[:1])

time: 153 us -> 160 us (1.046)
  waiting for transfers between devices: 65.2 us -> 71.4 us
    ppermute x9, waiting for transfers between devices: 11.5 us -> 20.3 us  [moved(): return lax.ppermute(value, 'blk', [(s, where(s)) for s in range(count)])]
    ppermute x9, starting transfers between devices: 30 us -> 22 us  [moved(): return lax.ppermute(value, 'blk', [(s, where(s)) for s in range(count)])]
    ppermute x14 -> x12, starting transfers between devices: 30.6 us -> 38.1 us  [shifted(): return lax.ppermute(value, 'blk', routes)]
    ppermute x4, waiting for transfers between devices: 7.96 us -> 5.33 us  [from_other(): return lax.ppermute(part, 'row', [(s, s ^ mask) for s in range(count)])]
    ppermute x14 -> x12, waiting for transfers between devices: 45.7 us -> 45.8 us  [shifted(): return lax.ppermute(value, 'blk', routes)]
  transfers between devices with their start and end apart: 30 -> 28, of which waited for: 16 -> 17; matrix products, arithmetic and copies ran while one was open for 0% -> 0% of each run, Pallas kernels for 7% -> 7%
where the time goes in v4:
time: 160 us; the launch traced here: 158 us
  waiting for transfers between devices  71.4 us (45%)
  starting transfers between devices  66.8 us (42%)
  Pallas kernels  18.6 us (12%)
    ppermute x12, waiting for transfers between devices, shifted(): return lax.ppermute(value, 'blk', routes)  45.8 us
    ppermute x12, starting transfers between devices, shifted(): return lax.ppermute(value, 'blk', routes)  38.1 us
    ppermute x9, starting transfers between devices, moved(): return lax.ppermute(value, 'blk', [(s, where(s)) for s in range(count)])  22 us
    ppermute x9, waiting for transfers between devices, moved(): return lax.ppermute(value, 'blk', [(s, where(s)) for s in range(count)])  20.3 us
    ppermute x4, waiting for transfers between devices, from_other(): return lax.ppermute(part, 'row', [(s, s ^ mask) for s in range(count)])  5.33 us
    pallas_call x3, Pallas kernels, second(): pl.pallas_call(functools.partial(second_body, rows0, out is not None, len...  4.74 us
    pallas_call x2, Pallas kernels, roots(): pl.pallas_call(functools.partial(root_body, slot), in_specs=[VM] * 2, out...  4.14 us
    ppermute x4, starting transfers between devices, from_other(): return lax.ppermute(part, 'row', [(s, s ^ mask) for s in range(count)])  4.05 us
  transfers between devices with their start and end apart: 28, of which 17 were waited for; matrix products, arithmetic and copies ran while one was open for 0% of the time, Pallas kernels for 7%

profile of v4, /device:TPU:8, one launch (start us, length us, event | category | flops | bytes accessed | tf_op | source)
XLA Modules:
  0.0 157.9 jit_solution(14193529220968557387)
XLA Ops:
  0.6 3.7 %first_gram.1 = (f32[136,128]{1,0:T(8,128)S(1)}, f32[4096,256]{1,0:T(8,128)S(1)}) custom-call(f32[4096,256]{1,0:T(8,128)} %m_ref.1), custom_call_target="tpu_custom_call" | custom-call | flops 536870912 | bytes 4194304 | tf_op jit(solution)/shard_map/first_gram/pallas_call | solution.py:95
  5.7 2.2 %collective-permute-start.1 = (f32[136,128]{1,0:T(8,128)S(1)}, f32[136,128]{1,0:T(8,128)S(1)}, u32[]{:S(2)}, u32[]{:S(2)}) collective-permute-start(f32[136,128]{1,0:T(8,128)S(1)} %add.6.a_ref), channel_id=1, source_target_pairs={{0,128},{64,192},{128,0},{192,64},{1,129},{65,193},{129,1},{193,65... | collective-permute-start | bytes 208904 | tf_op jit(solution)/shard_map/ppermute | solution.py:348
  7.9 2.5 %collective-permute-done.1.b_ref = f32[136,128]{1,0:T(8,128)S(1)} collective-permute-done((f32[136,128]{1,0:T(8,128)S(1)}, f32[136,128]{1,0:T(8,128)S(1)}, u32[]{:S(2)}, u32[]{:S(2)}) %collective-permute-start.1) | collective-permute-done | bytes 69664 | tf_op jit(solution)/shard_map/ppermute | solution.py:348
  16.6 12.1 %collective-permute-start.10 = (f32[1024,128]{1,0:T(8,128)S(1)}, f32[1024,128]{1,0:T(8,128)S(1)}, u32[]{:S(2)}, u32[]{:S(2)}) collective-permute-start(f32[1024,128]{1,0:T(8,128)S(1)} %get-tuple-element.31.refs_2_.refs_4_), channel_id=1, source_target_pairs={{0,63},{1,0},{2,1},{3,2},{4,3},{5,4},{6,5},{7,6},{8,7},{9,8},{10,9... | collective-permute-start | bytes 1572872 | tf_op jit(solution)/shard_map/ppermute | solution.py:327
  29.5 12.3 %collective-permute-start.11 = (f32[512,128]{1,0:T(8,128)S(1)}, f32[512,128]{1,0:T(8,128)S(1)}, u32[]{:S(2)}, u32[]{:S(2)}) collective-permute-start(f32[512,128]{1,0:T(8,128)S(1)} %get-tuple-element.32.refs_3_.refs_5_), channel_id=1, source_target_pairs={{0,63},{1,0},{2,1},{3,2},{4,3},{5,4},{6,5},{7,6},{8,7},{9,8},{10,9... | collective-permute-start | bytes 786440 | tf_op jit(solution)/shard_map/ppermute | solution.py:327
  42.2 3.4 %collective-permute-done.11.refs_3_ = f32[512,128]{1,0:T(8,128)S(1)} collective-permute-done((f32[512,128]{1,0:T(8,128)S(1)}, f32[512,128]{1,0:T(8,128)S(1)}, u32[]{:S(2)}, u32[]{:S(2)}) %collective-permute-start.11) | collective-permute-done | bytes 262176 | tf_op jit(solution)/shard_map/ppermute | solution.py:327
  46.1 8.1 %collective-permute-done.9.refs_0_ = f32[512,128]{1,0:T(8,128)S(1)} collective-permute-done((f32[512,128]{1,0:T(8,128)S(1)}, f32[512,128]{1,0:T(8,128)S(1)}, u32[]{:S(2)}, u32[]{:S(2)}) %collective-permute-start.9) | collective-permute-done | bytes 262176 | tf_op jit(solution)/shard_map/ppermute | solution.py:327
  54.6 3.9 %collective-permute-done.12.refs_3_ = f32[136,128]{1,0:T(8,128)S(1)} collective-permute-done((f32[136,128]{1,0:T(8,128)S(1)}, f32[136,128]{1,0:T(8,128)S(1)}, u32[]{:S(2)}, u32[]{:S(2)}) %collective-permute-start.12) | collective-permute-done | bytes 69664 | tf_op jit(solution)/shard_map/ppermute | solution.py:327
  70.0 2.4 %collective-permute-start.17 = (f32[2048,128]{1,0:T(8,128)S(1)}, f32[2048,128]{1,0:T(8,128)S(1)}, u32[]{:S(2)}, u32[]{:S(2)}) collective-permute-start(f32[2048,128]{1,0:T(8,128)S(1)} %get-tuple-element.43), channel_id=1, source_target_pairs={{0,1},{1,2},{2,3},{3,4},{4,5},{5,6},{6,7},{7,8},{8,9},{9,10},{10,1... | collective-permute-start | bytes 3145736 | tf_op jit(solution)/shard_map/ppermute | solution.py:327
  75.7 27.1 %collective-permute-done.3.refs_1_ = f32[512,128]{1,0:T(8,128)S(1)} collective-permute-done((f32[512,128]{1,0:T(8,128)S(1)}, f32[512,128]{1,0:T(8,128)S(1)}, u32[]{:S(2)}, u32[]{:S(2)}) %collective-permute-start.3) | collective-permute-done | bytes 262176 | tf_op jit(solution)/shard_map/ppermute | solution.py:327
  102.8 3.3 %collective-permute-done.7.refs_3_ = f32[512,128]{1,0:T(8,128)S(1)} collective-permute-done((f32[512,128]{1,0:T(8,128)S(1)}, f32[512,128]{1,0:T(8,128)S(1)}, u32[]{:S(2)}, u32[]{:S(2)}) %collective-permute-start.7) | collective-permute-done | bytes 262176 | tf_op jit(solution)/shard_map/ppermute | solution.py:327
  108.0 2.5 %collective-permute-start.16 = (f32[512,128]{1,0:T(8,128)S(1)}, f32[512,128]{1,0:T(8,128)S(1)}, u32[]{:S(2)}, u32[]{:S(2)}) collective-permute-start(f32[512,128]{1,0:T(8,128)S(1)} %get-tuple-element.42), channel_id=1, source_target_pairs={{0,1},{1,2},{2,3},{3,4},{4,5},{5,6},{6,7},{7,8},{8,9},{9,10},{10,1... | collective-permute-start | bytes 786440 | tf_op jit(solution)/shard_map/ppermute | solution.py:327
  110.5 2.4 %collective-permute-start.15 = (f32[512,128]{1,0:T(8,128)S(1)}, f32[512,128]{1,0:T(8,128)S(1)}, u32[]{:S(2)}, u32[]{:S(2)}) collective-permute-start(f32[512,128]{1,0:T(8,128)S(1)} %get-tuple-element.41), channel_id=1, source_target_pairs={{0,1},{1,2},{2,3},{3,4},{4,5},{5,6},{6,7},{7,8},{8,9},{9,10},{10,1... | collective-permute-start | bytes 786440 | tf_op jit(solution)/shard_map/ppermute | solution.py:327
  112.9 3.6 %collective-permute-done.20 = f32[8,128]{1,0:T(8,128)S(1)} collective-permute-done((f32[8,128]{1,0:T(8,128)S(1)}, f32[8,128]{1,0:T(8,128)S(1)}, u32[]{:S(2)}, u32[]{:S(2)}) %collective-permute-start.20) | collective-permute-done | bytes 4128 | tf_op jit(solution)/shard_map/ppermute | solution.py:359
  117.7 2.4 %collective-permute-done.21 = f32[8,128]{1,0:T(8,128)S(1)} collective-permute-done((f32[8,128]{1,0:T(8,128)S(1)}, f32[8,128]{1,0:T(8,128)S(1)}, u32[]{:S(2)}, u32[]{:S(2)}) %collective-permute-start.21) | collective-permute-done | bytes 4128 | tf_op jit(solution)/shard_map/ppermute | solution.py:359
  120.1 4.8 %collective-permute-start.22 = (f32[8,128]{1,0:T(8,128)S(1)}, f32[8,128]{1,0:T(8,128)S(1)}, u32[]{:S(2)}, u32[]{:S(2)}) collective-permute-start(f32[8,128]{1,0:T(8,128)S(1)} %max.33), channel_id=1, source_target_pairs={{0,7},{1,0},{2,1},{3,2},{4,3},{5,4},{6,5},{7,6},{8,15},{9,8},{10,9... | collective-permute-start | bytes 12296 | tf_op jit(solution)/shard_map/ppermute | solution.py:359
  127.9 2.8 %collective-permute-done.23 = f32[8,128]{1,0:T(8,128)S(1)} collective-permute-done((f32[8,128]{1,0:T(8,128)S(1)}, f32[8,128]{1,0:T(8,128)S(1)}, u32[]{:S(2)}, u32[]{:S(2)}) %collective-permute-start.23) | collective-permute-done | bytes 4128 | tf_op jit(solution)/shard_map/ppermute | solution.py:359
  130.7 3.2 %collective-permute-start.24 = (f32[8,128]{1,0:T(8,128)S(1)}, f32[8,128]{1,0:T(8,128)S(1)}, u32[]{:S(2)}, u32[]{:S(2)}) collective-permute-start(f32[8,128]{1,0:T(8,128)S(1)} %max.33), channel_id=1, source_target_pairs={{0,5},{1,6},{2,7},{3,0},{4,1},{5,2},{6,3},{7,4},{8,13},{9,14},{10,... | collective-permute-start | bytes 12296 | tf_op jit(solution)/shard_map/ppermute | solution.py:359
  133.9 3.3 %collective-permute-done.24 = f32[8,128]{1,0:T(8,128)S(1)} collective-permute-done((f32[8,128]{1,0:T(8,128)S(1)}, f32[8,128]{1,0:T(8,128)S(1)}, u32[]{:S(2)}, u32[]{:S(2)}) %collective-permute-start.24) | collective-permute-done | bytes 4128 | tf_op jit(solution)/shard_map/ppermute | solution.py:359
  137.3 3.3 %collective-permute-start.25 = (f32[8,128]{1,0:T(8,128)S(1)}, f32[8,128]{1,0:T(8,128)S(1)}, u32[]{:S(2)}, u32[]{:S(2)}) collective-permute-start(f32[8,128]{1,0:T(8,128)S(1)} %maximum_maximum_fusion), channel_id=1, source_target_pairs={{0,5},{1,6},{2,7},{3,0},{4,1},{5,2},{6,3},{7,4},{8,13},{9,14},{10,... | collective-permute-start | bytes 12296 | tf_op jit(solution)/shard_map/ppermute | solution.py:359
  140.6 3.3 %collective-permute-done.25 = f32[8,128]{1,0:T(8,128)S(1)} collective-permute-done((f32[8,128]{1,0:T(8,128)S(1)}, f32[8,128]{1,0:T(8,128)S(1)}, u32[]{:S(2)}, u32[]{:S(2)}) %collective-permute-start.25) | collective-permute-done | bytes 4128 | tf_op jit(solution)/shard_map/ppermute | solution.py:359
  143.9 4.8 %collective-permute-start.26 = (f32[8,128]{1,0:T(8,128)S(1)}, f32[8,128]{1,0:T(8,128)S(1)}, u32[]{:S(2)}, u32[]{:S(2)}) collective-permute-start(f32[8,128]{1,0:T(8,128)S(1)} %max.37), channel_id=1, source_target_pairs={{0,7},{1,0},{2,1},{3,2},{4,3},{5,4},{6,5},{7,6},{8,15},{9,8},{10,9... | collective-permute-start | bytes 12296 | tf_op jit(solution)/shard_map/ppermute | solution.py:359
  150.0 2.9 %collective-permute-start.27 = (f32[8,128]{1,0:T(8,128)S(1)}, f32[8,128]{1,0:T(8,128)S(1)}, u32[]{:S(2)}, u32[]{:S(2)}) collective-permute-start(f32[8,128]{1,0:T(8,128)S(1)} %max.38), channel_id=1, source_target_pairs={{0,32},{1,33},{2,34},{3,35},{4,36},{5,37},{6,38},{7,39},{8,40},{9,... | collective-permute-start | bytes 12296 | tf_op jit(solution)/shard_map/ppermute | solution.py:359
  152.8 2.3 %collective-permute-done.27 = f32[8,128]{1,0:T(8,128)S(1)} collective-permute-done((f32[8,128]{1,0:T(8,128)S(1)}, f32[8,128]{1,0:T(8,128)S(1)}, u32[]{:S(2)}, u32[]{:S(2)}) %collective-permute-start.27) | collective-permute-done | bytes 4128 | tf_op jit(solution)/shard_map/ppermute | solution.py:359
  (57 shorter events, 34.4 us)
Async XLA Ops:
  5.7 4.7 %collective-permute-start.1 = (f32[136,128]{1,0:T(8,128)S(1)}, f32[136,128]{1,0:T(8,128)S(1)}, u32[]{:S(2)}, u32[]{:S(2)}) collective-permute-start(f32[136,128]{1,0:T(8,128)S(1)} %add.6.a_ref), channel_id=1, source_target_pairs={{0,128},{64,192},{128,0},{192,64},{1,129},{65,193},{129,1},{193,65... | collective-permute-start | bytes 208904 | tf_op jit(solution)/shard_map/ppermute | solution.py:348
  13.5 44.9 %collective-permute-start.8 = (f32[2048,128]{1,0:T(8,128)S(1)}, f32[2048,128]{1,0:T(8,128)S(1)}, u32[]{:S(2)}, u32[]{:S(2)}) collective-permute-start(f32[2048,128]{1,0:T(8,128)S(1)} %get-tuple-element.33), channel_id=1, source_target_pairs={{0,1},{1,2},{2,3},{3,4},{4,5},{5,6},{6,7},{7,8},{8,9},{9,10},{10,1... | collective-permute-start | bytes 3145736 | tf_op jit(solution)/shard_map/ppermute | solution.py:327
  15.9 12.8 %collective-permute-start.4 = (f32[1024,128]{1,0:T(8,128)S(1)}, f32[1024,128]{1,0:T(8,128)S(1)}, u32[]{:S(2)}, u32[]{:S(2)}) collective-permute-start(f32[1024,128]{1,0:T(8,128)S(1)} %get-tuple-element.29.refs_0_), channel_id=1, source_target_pairs={{31,28},{63,60},{95,92},{127,124},{159,156},{191,188},{223,220},{2... | collective-permute-start | bytes 1572872 | tf_op jit(solution)/shard_map/ppermute | solution.py:341
  16.6 29.0 %collective-permute-start.10 = (f32[1024,128]{1,0:T(8,128)S(1)}, f32[1024,128]{1,0:T(8,128)S(1)}, u32[]{:S(2)}, u32[]{:S(2)}) collective-permute-start(f32[1024,128]{1,0:T(8,128)S(1)} %get-tuple-element.31.refs_2_.refs_4_), channel_id=1, source_target_pairs={{0,63},{1,0},{2,1},{3,2},{4,3},{5,4},{6,5},{7,6},{8,7},{9,8},{10,9... | collective-permute-start | bytes 1572872 | tf_op jit(solution)/shard_map/ppermute | solution.py:327
  28.8 34.5 %collective-permute-start.5 = (f32[1024,128]{1,0:T(8,128)S(1)}, f32[1024,128]{1,0:T(8,128)S(1)}, u32[]{:S(2)}, u32[]{:S(2)}) collective-permute-start(f32[1024,128]{1,0:T(8,128)S(1)} %collective-permute-done.4), channel_id=1, source_target_pairs={{28,33},{60,1},{92,97},{124,65},{156,161},{188,129},{220,225},{252... | collective-permute-start | bytes 1572872 | tf_op jit(solution)/shard_map/ppermute | solution.py:341
  29.5 16.1 %collective-permute-start.11 = (f32[512,128]{1,0:T(8,128)S(1)}, f32[512,128]{1,0:T(8,128)S(1)}, u32[]{:S(2)}, u32[]{:S(2)}) collective-permute-start(f32[512,128]{1,0:T(8,128)S(1)} %get-tuple-element.32.refs_3_.refs_5_), channel_id=1, source_target_pairs={{0,63},{1,0},{2,1},{3,2},{4,3},{5,4},{6,5},{7,6},{8,7},{9,8},{10,9... | collective-permute-start | bytes 786440 | tf_op jit(solution)/shard_map/ppermute | solution.py:327
  42.1 12.2 %collective-permute-start.9 = (f32[512,128]{1,0:T(8,128)S(1)}, f32[512,128]{1,0:T(8,128)S(1)}, u32[]{:S(2)}, u32[]{:S(2)}) collective-permute-start(f32[512,128]{1,0:T(8,128)S(1)} %get-tuple-element.35), channel_id=1, source_target_pairs={{0,1},{1,2},{2,3},{3,4},{4,5},{5,6},{6,7},{7,8},{8,9},{9,10},{10,1... | collective-permute-start | bytes 786440 | tf_op jit(solution)/shard_map/ppermute | solution.py:327
  46.1 12.4 %collective-permute-start.12 = (f32[136,128]{1,0:T(8,128)S(1)}, f32[136,128]{1,0:T(8,128)S(1)}, u32[]{:S(2)}, u32[]{:S(2)}) collective-permute-start(f32[136,128]{1,0:T(8,128)S(1)} %shard_map.35), channel_id=1, source_target_pairs={{0,1},{1,2},{2,3},{3,4},{4,5},{5,6},{6,7},{7,8},{8,9},{9,10},{10,1... | collective-permute-start | bytes 208904 | tf_op jit(solution)/shard_map/ppermute | solution.py:327
  60.3 4.6 %collective-permute-start.14 = (f32[136,128]{1,0:T(8,128)S(1)}, f32[136,128]{1,0:T(8,128)S(1)}, u32[]{:S(2)}, u32[]{:S(2)}) collective-permute-start(f32[136,128]{1,0:T(8,128)S(1)} %add.7.a_ref), channel_id=1, source_target_pairs={{0,128},{64,192},{128,0},{192,64},{1,129},{65,193},{129,1},{193,65... | collective-permute-start | bytes 208904 | tf_op jit(solution)/shard_map/ppermute | solution.py:348
  61.9 44.2 %collective-permute-start.2 = (f32[1024,128]{1,0:T(8,128)S(1)}, f32[1024,128]{1,0:T(8,128)S(1)}, u32[]{:S(2)}, u32[]{:S(2)}) collective-permute-start(f32[1024,128]{1,0:T(8,128)S(1)} %get-tuple-element.29.refs_0_), channel_id=1, source_target_pairs={{0,1},{1,2},{2,3},{3,4},{4,5},{5,6},{6,7},{7,8},{8,9},{9,10},{10,1... | collective-permute-start | bytes 1572872 | tf_op jit(solution)/shard_map/ppermute | solution.py:327
  63.3 42.8 %collective-permute-start.6 = (f32[1024,128]{1,0:T(8,128)S(1)}, f32[1024,128]{1,0:T(8,128)S(1)}, u32[]{:S(2)}, u32[]{:S(2)}) collective-permute-start(f32[1024,128]{1,0:T(8,128)S(1)} %collective-permute-done.5), channel_id=1, source_target_pairs={{33,32},{1,0},{97,96},{65,64},{161,160},{129,128},{225,224},{193,1... | collective-permute-start | bytes 1572872 | tf_op jit(solution)/shard_map/ppermute | solution.py:341
  70.0 85.7 %collective-permute-start.17 = (f32[2048,128]{1,0:T(8,128)S(1)}, f32[2048,128]{1,0:T(8,128)S(1)}, u32[]{:S(2)}, u32[]{:S(2)}) collective-permute-start(f32[2048,128]{1,0:T(8,128)S(1)} %get-tuple-element.43), channel_id=1, source_target_pairs={{0,1},{1,2},{2,3},{3,4},{4,5},{5,6},{6,7},{7,8},{8,9},{9,10},{10,1... | collective-permute-start | bytes 3145736 | tf_op jit(solution)/shard_map/ppermute | solution.py:327
  72.5 30.3 %collective-permute-start.3 = (f32[512,128]{1,0:T(8,128)S(1)}, f32[512,128]{1,0:T(8,128)S(1)}, u32[]{:S(2)}, u32[]{:S(2)}) collective-permute-start(f32[512,128]{1,0:T(8,128)S(1)} %get-tuple-element.30.refs_1_), channel_id=1, source_target_pairs={{0,1},{1,2},{2,3},{3,4},{4,5},{5,6},{6,7},{7,8},{8,9},{9,10},{10,1... | collective-permute-start | bytes 786440 | tf_op jit(solution)/shard_map/ppermute | solution.py:327
  74.4 31.7 %collective-permute-start.7 = (f32[512,128]{1,0:T(8,128)S(1)}, f32[512,128]{1,0:T(8,128)S(1)}, u32[]{:S(2)}, u32[]{:S(2)}) collective-permute-start(f32[512,128]{1,0:T(8,128)S(1)} %get-tuple-element.30.refs_1_), channel_id=1, source_target_pairs={{31,32},{63,0},{95,96},{127,64},{159,160},{191,128},{223,224},{255... | collective-permute-start | bytes 786440 | tf_op jit(solution)/shard_map/ppermute | solution.py:327
  107.8 48.0 %collective-permute-start.18 = (f32[1024,128]{1,0:T(8,128)S(1)}, f32[1024,128]{1,0:T(8,128)S(1)}, u32[]{:S(2)}, u32[]{:S(2)}) collective-permute-start(f32[1024,128]{1,0:T(8,128)S(1)} %get-tuple-element.44), channel_id=1, source_target_pairs={{0,1},{1,2},{2,3},{3,4},{4,5},{5,6},{6,7},{7,8},{8,9},{9,10},{10,1... | collective-permute-start | bytes 1572872 | tf_op jit(solution)/shard_map/ppermute | solution.py:327
  107.9 5.0 %collective-permute-start.19 = (f32[8,128]{1,0:T(8,128)S(1)}, f32[8,128]{1,0:T(8,128)S(1)}, u32[]{:S(2)}, u32[]{:S(2)}) collective-permute-start(f32[8,128]{1,0:T(8,128)S(1)} %max.30), channel_id=1, source_target_pairs={{0,24},{1,25},{2,26},{3,27},{4,28},{5,29},{6,30},{7,31},{8,0},{9,1... | collective-permute-start | bytes 12296 | tf_op jit(solution)/shard_map/ppermute | solution.py:359
  108.0 47.8 %collective-permute-start.16 = (f32[512,128]{1,0:T(8,128)S(1)}, f32[512,128]{1,0:T(8,128)S(1)}, u32[]{:S(2)}, u32[]{:S(2)}) collective-permute-start(f32[512,128]{1,0:T(8,128)S(1)} %get-tuple-element.42), channel_id=1, source_target_pairs={{0,1},{1,2},{2,3},{3,4},{4,5},{5,6},{6,7},{7,8},{8,9},{9,10},{10,1... | collective-permute-start | bytes 786440 | tf_op jit(solution)/shard_map/ppermute | solution.py:327
  110.5 46.5 %collective-permute-start.15 = (f32[512,128]{1,0:T(8,128)S(1)}, f32[512,128]{1,0:T(8,128)S(1)}, u32[]{:S(2)}, u32[]{:S(2)}) collective-permute-start(f32[512,128]{1,0:T(8,128)S(1)} %get-tuple-element.41), channel_id=1, source_target_pairs={{0,1},{1,2},{2,3},{3,4},{4,5},{5,6},{6,7},{7,8},{8,9},{9,10},{10,1... | collective-permute-start | bytes 786440 | tf_op jit(solution)/shard_map/ppermute | solution.py:327
  120.1 6.1 %collective-permute-start.22 = (f32[8,128]{1,0:T(8,128)S(1)}, f32[8,128]{1,0:T(8,128)S(1)}, u32[]{:S(2)}, u32[]{:S(2)}) collective-permute-start(f32[8,128]{1,0:T(8,128)S(1)} %max.33), channel_id=1, source_target_pairs={{0,7},{1,0},{2,1},{3,2},{4,3},{5,4},{6,5},{7,6},{8,15},{9,8},{10,9... | collective-permute-start | bytes 12296 | tf_op jit(solution)/shard_map/ppermute | solution.py:359
  126.2 4.5 %collective-permute-start.23 = (f32[8,128]{1,0:T(8,128)S(1)}, f32[8,128]{1,0:T(8,128)S(1)}, u32[]{:S(2)}, u32[]{:S(2)}) collective-permute-start(f32[8,128]{1,0:T(8,128)S(1)} %max.33), channel_id=1, source_target_pairs={{0,6},{1,7},{2,0},{3,1},{4,2},{5,3},{6,4},{7,5},{8,14},{9,15},{10,... | collective-permute-start | bytes 12296 | tf_op jit(solution)/shard_map/ppermute | solution.py:359
  130.7 6.5 %collective-permute-start.24 = (f32[8,128]{1,0:T(8,128)S(1)}, f32[8,128]{1,0:T(8,128)S(1)}, u32[]{:S(2)}, u32[]{:S(2)}) collective-permute-start(f32[8,128]{1,0:T(8,128)S(1)} %max.33), channel_id=1, source_target_pairs={{0,5},{1,6},{2,7},{3,0},{4,1},{5,2},{6,3},{7,4},{8,13},{9,14},{10,... | collective-permute-start | bytes 12296 | tf_op jit(solution)/shard_map/ppermute | solution.py:359
  137.3 6.6 %collective-permute-start.25 = (f32[8,128]{1,0:T(8,128)S(1)}, f32[8,128]{1,0:T(8,128)S(1)}, u32[]{:S(2)}, u32[]{:S(2)}) collective-permute-start(f32[8,128]{1,0:T(8,128)S(1)} %maximum_maximum_fusion), channel_id=1, source_target_pairs={{0,5},{1,6},{2,7},{3,0},{4,1},{5,2},{6,3},{7,4},{8,13},{9,14},{10,... | collective-permute-start | bytes 12296 | tf_op jit(solution)/shard_map/ppermute | solution.py:359
  143.9 6.1 %collective-permute-start.26 = (f32[8,128]{1,0:T(8,128)S(1)}, f32[8,128]{1,0:T(8,128)S(1)}, u32[]{:S(2)}, u32[]{:S(2)}) collective-permute-start(f32[8,128]{1,0:T(8,128)S(1)} %max.37), channel_id=1, source_target_pairs={{0,7},{1,0},{2,1},{3,2},{4,3},{5,4},{6,5},{7,6},{8,15},{9,8},{10,9... | collective-permute-start | bytes 12296 | tf_op jit(solution)/shard_map/ppermute | solution.py:359
  150.0 5.1 %collective-permute-start.27 = (f32[8,128]{1,0:T(8,128)S(1)}, f32[8,128]{1,0:T(8,128)S(1)}, u32[]{:S(2)}, u32[]{:S(2)}) collective-permute-start(f32[8,128]{1,0:T(8,128)S(1)} %max.38), channel_id=1, source_target_pairs={{0,32},{1,33},{2,34},{3,35},{4,36},{5,37},{6,38},{7,39},{8,40},{9,... | collective-permute-start | bytes 12296 | tf_op jit(solution)/shard_map/ppermute | solution.py:359
  (4 other events, 9.9 us)

commit v5 on v4

--- a/solution.py
+++ b/solution.py
@@ -76,15 +76,20 @@
         load(i).wait()
         x = held_ref[i * block : (i + 1) * block, :]
         squares = column_squares(x)
-        product = gram_tile(x[:, :B], x[:, B:])
+        high, low = halves(x)
+        product = dot_rows(
+            jnp.concatenate([high[:, :B], low[:, :B]], 1),
+            jnp.concatenate([high[:, B:], low[:, B:]], 1),
+        )
         if i == 0:
             n_acc[...] = squares
             c_acc[...] = product
         else:
             n_acc[...] += squares
             c_acc[...] += product
+    full = c_acc[...]
     norms = jnp.sum(n_acc[...], axis=0, keepdims=True)
-    o_ref[:B, :] = c_acc[...]
+    o_ref[:B, :] = (full[:B, :B] + full[B:, B:]) + (full[:B, B:] + full[B:, :B])
     o_ref[B:, :] = jnp.concatenate(
         [norms[:, :B], norms[:, B:], jnp.zeros((PACK - B - 2, B), F32)], axis=0
     )
@@ -93,7 +98,7 @@
 def first_gram(matrix):
     rows = matrix.shape[0]
     return pl.pallas_call(
-        functools.partial(gram_body, 8),
+        functools.partial(gram_body, 4),
         in_specs=[HBM],
         out_specs=[VM, VM],
         out_shape=[
@@ -101,9 +106,9 @@
             jax.ShapeDtypeStruct(matrix.shape, F32),
         ],
         scratch_shapes=[
-            pltpu.VMEM((B, B), F32),
+            pltpu.VMEM((2 * B, 2 * B), F32),
             pltpu.VMEM((8, 2 * B), F32),
-            pltpu.SemaphoreType.DMA((8,)),
+            pltpu.SemaphoreType.DMA((4,)),
         ],
         compiler_params=params(48),
         cost_estimate=cost(rows * B * B * 8, rows * B * 8),
@@ -437,7 +442,7 @@
 
     cut = len(got) - 1
     sums = partial(got[:cut], rf[:cut], rb, [])
-    sums = partial(got[cut:], rf[cut:], [], [sums, helped])
+    sums = partial(got[cut:], rf[cut:], [], [sums]) + helped
     wh, wl, squares1 = roots(of_group(sums), 1)
     w = (wh, wl)
 

time: 160 us -> 159 us (level)
  no operation moved by 1% of the time
where the time goes in v5:
time: 159 us; the launch traced here: 156 us
  waiting for transfers between devices  70.3 us (44%)
  starting transfers between devices  67.2 us (42%)
  Pallas kernels  17.8 us (11%)
    ppermute x12, waiting for transfers between devices, shifted(): return lax.ppermute(value, 'blk', routes)  45.3 us
    ppermute x12, starting transfers between devices, shifted(): return lax.ppermute(value, 'blk', routes)  38.1 us
    ppermute x9, starting transfers between devices, moved(): return lax.ppermute(value, 'blk', [(s, where(s)) for s in range(count)])  22.4 us
    ppermute x9, waiting for transfers between devices, moved(): return lax.ppermute(value, 'blk', [(s, where(s)) for s in range(count)])  19.9 us
    ppermute x4, waiting for transfers between devices, from_other(): return lax.ppermute(part, 'row', [(s, s ^ mask) for s in range(count)])  5.15 us
    pallas_call x3, Pallas kernels, second(): pl.pallas_call(functools.partial(second_body, rows0, out is not None, len...  4.74 us
    pallas_call x2, Pallas kernels, roots(): pl.pallas_call(functools.partial(root_body, slot), in_specs=[VM] * 2, out...  4.13 us
    ppermute x4, starting transfers between devices, from_other(): return lax.ppermute(part, 'row', [(s, s ^ mask) for s in range(count)])  3.86 us
  transfers between devices with their start and end apart: 28, of which 17 were waited for; matrix products, arithmetic and copies ran while one was open for 0% of the time, Pallas kernels for 7%

profile of v5, /device:TPU:8, one launch (start us, length us, event | category | flops | bytes accessed | tf_op | source)
XLA Modules:
  0.0 156.4 jit_solution(15189363474337863588)
XLA Ops:
  0.6 2.8 %first_gram.1 = (f32[136,128]{1,0:T(8,128)S(1)}, f32[4096,256]{1,0:T(8,128)S(1)}) custom-call(f32[4096,256]{1,0:T(8,128)} %m_ref.1), custom_call_target="tpu_custom_call" | custom-call | flops 536870912 | bytes 4194304 | tf_op jit(solution)/shard_map/first_gram/pallas_call | solution.py:100
  4.8 2.2 %collective-permute-start.1 = (f32[136,128]{1,0:T(8,128)S(1)}, f32[136,128]{1,0:T(8,128)S(1)}, u32[]{:S(2)}, u32[]{:S(2)}) collective-permute-start(f32[136,128]{1,0:T(8,128)S(1)} %add.9.a_ref), channel_id=1, source_target_pairs={{0,128},{64,192},{128,0},{192,64},{1,129},{65,193},{129,1},{193,65... | collective-permute-start | bytes 208904 | tf_op jit(solution)/shard_map/ppermute | solution.py:353
  7.1 2.5 %collective-permute-done.1.b_ref = f32[136,128]{1,0:T(8,128)S(1)} collective-permute-done((f32[136,128]{1,0:T(8,128)S(1)}, f32[136,128]{1,0:T(8,128)S(1)}, u32[]{:S(2)}, u32[]{:S(2)}) %collective-permute-start.1) | collective-permute-done | bytes 69664 | tf_op jit(solution)/shard_map/ppermute | solution.py:353
  15.8 12.1 %collective-permute-start.10 = (f32[1024,128]{1,0:T(8,128)S(1)}, f32[1024,128]{1,0:T(8,128)S(1)}, u32[]{:S(2)}, u32[]{:S(2)}) collective-permute-start(f32[1024,128]{1,0:T(8,128)S(1)} %get-tuple-element.31.refs_2_.refs_4_), channel_id=1, source_target_pairs={{0,63},{1,0},{2,1},{3,2},{4,3},{5,4},{6,5},{7,6},{8,7},{9,8},{10,9... | collective-permute-start | bytes 1572872 | tf_op jit(solution)/shard_map/ppermute | solution.py:332
  28.6 12.3 %collective-permute-start.11 = (f32[512,128]{1,0:T(8,128)S(1)}, f32[512,128]{1,0:T(8,128)S(1)}, u32[]{:S(2)}, u32[]{:S(2)}) collective-permute-start(f32[512,128]{1,0:T(8,128)S(1)} %get-tuple-element.32.refs_3_.refs_5_), channel_id=1, source_target_pairs={{0,63},{1,0},{2,1},{3,2},{4,3},{5,4},{6,5},{7,6},{8,7},{9,8},{10,9... | collective-permute-start | bytes 786440 | tf_op jit(solution)/shard_map/ppermute | solution.py:332
  41.4 3.4 %collective-permute-done.11.refs_3_ = f32[512,128]{1,0:T(8,128)S(1)} collective-permute-done((f32[512,128]{1,0:T(8,128)S(1)}, f32[512,128]{1,0:T(8,128)S(1)}, u32[]{:S(2)}, u32[]{:S(2)}) %collective-permute-start.11) | collective-permute-done | bytes 262176 | tf_op jit(solution)/shard_map/ppermute | solution.py:332
  45.3 8.1 %collective-permute-done.9.refs_0_ = f32[512,128]{1,0:T(8,128)S(1)} collective-permute-done((f32[512,128]{1,0:T(8,128)S(1)}, f32[512,128]{1,0:T(8,128)S(1)}, u32[]{:S(2)}, u32[]{:S(2)}) %collective-permute-start.9) | collective-permute-done | bytes 262176 | tf_op jit(solution)/shard_map/ppermute | solution.py:332
  54.3 3.3 %collective-permute-done.12 = f32[136,128]{1,0:T(8,128)S(1)} collective-permute-done((f32[136,128]{1,0:T(8,128)S(1)}, f32[136,128]{1,0:T(8,128)S(1)}, u32[]{:S(2)}, u32[]{:S(2)}) %collective-permute-start.12) | collective-permute-done | bytes 69664 | tf_op jit(solution)/shard_map/ppermute | solution.py:332
  68.5 2.6 %collective-permute-start.17 = (f32[2048,128]{1,0:T(8,128)S(1)}, f32[2048,128]{1,0:T(8,128)S(1)}, u32[]{:S(2)}, u32[]{:S(2)}) collective-permute-start(f32[2048,128]{1,0:T(8,128)S(1)} %get-tuple-element.43), channel_id=1, source_target_pairs={{0,1},{1,2},{2,3},{3,4},{4,5},{5,6},{6,7},{7,8},{8,9},{9,10},{10,1... | collective-permute-start | bytes 3145736 | tf_op jit(solution)/shard_map/ppermute | solution.py:332
  74.4 26.9 %collective-permute-done.3.refs_1_ = f32[512,128]{1,0:T(8,128)S(1)} collective-permute-done((f32[512,128]{1,0:T(8,128)S(1)}, f32[512,128]{1,0:T(8,128)S(1)}, u32[]{:S(2)}, u32[]{:S(2)}) %collective-permute-start.3) | collective-permute-done | bytes 262176 | tf_op jit(solution)/shard_map/ppermute | solution.py:332
  101.3 3.5 %collective-permute-done.7.refs_3_ = f32[512,128]{1,0:T(8,128)S(1)} collective-permute-done((f32[512,128]{1,0:T(8,128)S(1)}, f32[512,128]{1,0:T(8,128)S(1)}, u32[]{:S(2)}, u32[]{:S(2)}) %collective-permute-start.7) | collective-permute-done | bytes 262176 | tf_op jit(solution)/shard_map/ppermute | solution.py:332
  106.6 2.3 %collective-permute-start.16 = (f32[512,128]{1,0:T(8,128)S(1)}, f32[512,128]{1,0:T(8,128)S(1)}, u32[]{:S(2)}, u32[]{:S(2)}) collective-permute-start(f32[512,128]{1,0:T(8,128)S(1)} %get-tuple-element.42), channel_id=1, source_target_pairs={{0,1},{1,2},{2,3},{3,4},{4,5},{5,6},{6,7},{7,8},{8,9},{9,10},{10,1... | collective-permute-start | bytes 786440 | tf_op jit(solution)/shard_map/ppermute | solution.py:332
  109.0 2.4 %collective-permute-start.15 = (f32[512,128]{1,0:T(8,128)S(1)}, f32[512,128]{1,0:T(8,128)S(1)}, u32[]{:S(2)}, u32[]{:S(2)}) collective-permute-start(f32[512,128]{1,0:T(8,128)S(1)} %get-tuple-element.41), channel_id=1, source_target_pairs={{0,1},{1,2},{2,3},{3,4},{4,5},{5,6},{6,7},{7,8},{8,9},{9,10},{10,1... | collective-permute-start | bytes 786440 | tf_op jit(solution)/shard_map/ppermute | solution.py:332
  111.4 3.5 %collective-permute-done.20 = f32[8,128]{1,0:T(8,128)S(1)} collective-permute-done((f32[8,128]{1,0:T(8,128)S(1)}, f32[8,128]{1,0:T(8,128)S(1)}, u32[]{:S(2)}, u32[]{:S(2)}) %collective-permute-start.20) | collective-permute-done | bytes 4128 | tf_op jit(solution)/shard_map/ppermute | solution.py:364
  116.3 2.3 %collective-permute-done.21 = f32[8,128]{1,0:T(8,128)S(1)} collective-permute-done((f32[8,128]{1,0:T(8,128)S(1)}, f32[8,128]{1,0:T(8,128)S(1)}, u32[]{:S(2)}, u32[]{:S(2)}) %collective-permute-start.21) | collective-permute-done | bytes 4128 | tf_op jit(solution)/shard_map/ppermute | solution.py:364
  118.5 4.8 %collective-permute-start.22 = (f32[8,128]{1,0:T(8,128)S(1)}, f32[8,128]{1,0:T(8,128)S(1)}, u32[]{:S(2)}, u32[]{:S(2)}) collective-permute-start(f32[8,128]{1,0:T(8,128)S(1)} %max.33), channel_id=1, source_target_pairs={{0,7},{1,0},{2,1},{3,2},{4,3},{5,4},{6,5},{7,6},{8,15},{9,8},{10,9... | collective-permute-start | bytes 12296 | tf_op jit(solution)/shard_map/ppermute | solution.py:364
  126.4 2.8 %collective-permute-done.23 = f32[8,128]{1,0:T(8,128)S(1)} collective-permute-done((f32[8,128]{1,0:T(8,128)S(1)}, f32[8,128]{1,0:T(8,128)S(1)}, u32[]{:S(2)}, u32[]{:S(2)}) %collective-permute-start.23) | collective-permute-done | bytes 4128 | tf_op jit(solution)/shard_map/ppermute | solution.py:364
  129.2 3.2 %collective-permute-start.24 = (f32[8,128]{1,0:T(8,128)S(1)}, f32[8,128]{1,0:T(8,128)S(1)}, u32[]{:S(2)}, u32[]{:S(2)}) collective-permute-start(f32[8,128]{1,0:T(8,128)S(1)} %max.33), channel_id=1, source_target_pairs={{0,5},{1,6},{2,7},{3,0},{4,1},{5,2},{6,3},{7,4},{8,13},{9,14},{10,... | collective-permute-start | bytes 12296 | tf_op jit(solution)/shard_map/ppermute | solution.py:364
  132.4 3.3 %collective-permute-done.24 = f32[8,128]{1,0:T(8,128)S(1)} collective-permute-done((f32[8,128]{1,0:T(8,128)S(1)}, f32[8,128]{1,0:T(8,128)S(1)}, u32[]{:S(2)}, u32[]{:S(2)}) %collective-permute-start.24) | collective-permute-done | bytes 4128 | tf_op jit(solution)/shard_map/ppermute | solution.py:364
  135.7 3.3 %collective-permute-start.25 = (f32[8,128]{1,0:T(8,128)S(1)}, f32[8,128]{1,0:T(8,128)S(1)}, u32[]{:S(2)}, u32[]{:S(2)}) collective-permute-start(f32[8,128]{1,0:T(8,128)S(1)} %maximum_maximum_fusion), channel_id=1, source_target_pairs={{0,5},{1,6},{2,7},{3,0},{4,1},{5,2},{6,3},{7,4},{8,13},{9,14},{10,... | collective-permute-start | bytes 12296 | tf_op jit(solution)/shard_map/ppermute | solution.py:364
  139.0 3.3 %collective-permute-done.25 = f32[8,128]{1,0:T(8,128)S(1)} collective-permute-done((f32[8,128]{1,0:T(8,128)S(1)}, f32[8,128]{1,0:T(8,128)S(1)}, u32[]{:S(2)}, u32[]{:S(2)}) %collective-permute-start.25) | collective-permute-done | bytes 4128 | tf_op jit(solution)/shard_map/ppermute | solution.py:364
  142.3 4.8 %collective-permute-start.26 = (f32[8,128]{1,0:T(8,128)S(1)}, f32[8,128]{1,0:T(8,128)S(1)}, u32[]{:S(2)}, u32[]{:S(2)}) collective-permute-start(f32[8,128]{1,0:T(8,128)S(1)} %max.37), channel_id=1, source_target_pairs={{0,7},{1,0},{2,1},{3,2},{4,3},{5,4},{6,5},{7,6},{8,15},{9,8},{10,9... | collective-permute-start | bytes 12296 | tf_op jit(solution)/shard_map/ppermute | solution.py:364
  148.5 3.0 %collective-permute-start.27 = (f32[8,128]{1,0:T(8,128)S(1)}, f32[8,128]{1,0:T(8,128)S(1)}, u32[]{:S(2)}, u32[]{:S(2)}) collective-permute-start(f32[8,128]{1,0:T(8,128)S(1)} %max.38), channel_id=1, source_target_pairs={{0,32},{1,33},{2,34},{3,35},{4,36},{5,37},{6,38},{7,39},{8,40},{9,... | collective-permute-start | bytes 12296 | tf_op jit(solution)/shard_map/ppermute | solution.py:364
  151.5 2.1 %collective-permute-done.27 = f32[8,128]{1,0:T(8,128)S(1)} collective-permute-done((f32[8,128]{1,0:T(8,128)S(1)}, f32[8,128]{1,0:T(8,128)S(1)}, u32[]{:S(2)}, u32[]{:S(2)}) %collective-permute-start.27) | collective-permute-done | bytes 4128 | tf_op jit(solution)/shard_map/ppermute | solution.py:364
  (58 shorter events, 34.5 us)
Async XLA Ops:
  4.8 4.7 %collective-permute-start.1 = (f32[136,128]{1,0:T(8,128)S(1)}, f32[136,128]{1,0:T(8,128)S(1)}, u32[]{:S(2)}, u32[]{:S(2)}) collective-permute-start(f32[136,128]{1,0:T(8,128)S(1)} %add.9.a_ref), channel_id=1, source_target_pairs={{0,128},{64,192},{128,0},{192,64},{1,129},{65,193},{129,1},{193,65... | collective-permute-start | bytes 208904 | tf_op jit(solution)/shard_map/ppermute | solution.py:353
  12.7 41.1 %collective-permute-start.8 = (f32[2048,128]{1,0:T(8,128)S(1)}, f32[2048,128]{1,0:T(8,128)S(1)}, u32[]{:S(2)}, u32[]{:S(2)}) collective-permute-start(f32[2048,128]{1,0:T(8,128)S(1)} %get-tuple-element.33), channel_id=1, source_target_pairs={{0,1},{1,2},{2,3},{3,4},{4,5},{5,6},{6,7},{7,8},{8,9},{9,10},{10,1... | collective-permute-start | bytes 3145736 | tf_op jit(solution)/shard_map/ppermute | solution.py:332
  15.1 12.8 %collective-permute-start.4 = (f32[1024,128]{1,0:T(8,128)S(1)}, f32[1024,128]{1,0:T(8,128)S(1)}, u32[]{:S(2)}, u32[]{:S(2)}) collective-permute-start(f32[1024,128]{1,0:T(8,128)S(1)} %get-tuple-element.29.refs_0_), channel_id=1, source_target_pairs={{31,28},{63,60},{95,92},{127,124},{159,156},{191,188},{223,220},{2... | collective-permute-start | bytes 1572872 | tf_op jit(solution)/shard_map/ppermute | solution.py:346
  15.8 28.9 %collective-permute-start.10 = (f32[1024,128]{1,0:T(8,128)S(1)}, f32[1024,128]{1,0:T(8,128)S(1)}, u32[]{:S(2)}, u32[]{:S(2)}) collective-permute-start(f32[1024,128]{1,0:T(8,128)S(1)} %get-tuple-element.31.refs_2_.refs_4_), channel_id=1, source_target_pairs={{0,63},{1,0},{2,1},{3,2},{4,3},{5,4},{6,5},{7,6},{8,7},{9,8},{10,9... | collective-permute-start | bytes 1572872 | tf_op jit(solution)/shard_map/ppermute | solution.py:332
  27.9 33.8 %collective-permute-start.5 = (f32[1024,128]{1,0:T(8,128)S(1)}, f32[1024,128]{1,0:T(8,128)S(1)}, u32[]{:S(2)}, u32[]{:S(2)}) collective-permute-start(f32[1024,128]{1,0:T(8,128)S(1)} %collective-permute-done.4), channel_id=1, source_target_pairs={{28,33},{60,1},{92,97},{124,65},{156,161},{188,129},{220,225},{252... | collective-permute-start | bytes 1572872 | tf_op jit(solution)/shard_map/ppermute | solution.py:346
  28.6 16.2 %collective-permute-start.11 = (f32[512,128]{1,0:T(8,128)S(1)}, f32[512,128]{1,0:T(8,128)S(1)}, u32[]{:S(2)}, u32[]{:S(2)}) collective-permute-start(f32[512,128]{1,0:T(8,128)S(1)} %get-tuple-element.32.refs_3_.refs_5_), channel_id=1, source_target_pairs={{0,63},{1,0},{2,1},{3,2},{4,3},{5,4},{6,5},{7,6},{8,7},{9,8},{10,9... | collective-permute-start | bytes 786440 | tf_op jit(solution)/shard_map/ppermute | solution.py:332
  41.3 12.2 %collective-permute-start.9 = (f32[512,128]{1,0:T(8,128)S(1)}, f32[512,128]{1,0:T(8,128)S(1)}, u32[]{:S(2)}, u32[]{:S(2)}) collective-permute-start(f32[512,128]{1,0:T(8,128)S(1)} %get-tuple-element.35), channel_id=1, source_target_pairs={{0,1},{1,2},{2,3},{3,4},{4,5},{5,6},{6,7},{7,8},{8,9},{9,10},{10,1... | collective-permute-start | bytes 786440 | tf_op jit(solution)/shard_map/ppermute | solution.py:332
  45.2 12.4 %collective-permute-start.12 = (f32[136,128]{1,0:T(8,128)S(1)}, f32[136,128]{1,0:T(8,128)S(1)}, u32[]{:S(2)}, u32[]{:S(2)}) collective-permute-start(f32[136,128]{1,0:T(8,128)S(1)} %shard_map.36), channel_id=1, source_target_pairs={{0,1},{1,2},{2,3},{3,4},{4,5},{5,6},{6,7},{7,8},{8,9},{9,10},{10,1... | collective-permute-start | bytes 208904 | tf_op jit(solution)/shard_map/ppermute | solution.py:332
  59.0 4.4 %collective-permute-start.14 = (f32[136,128]{1,0:T(8,128)S(1)}, f32[136,128]{1,0:T(8,128)S(1)}, u32[]{:S(2)}, u32[]{:S(2)}) collective-permute-start(f32[136,128]{1,0:T(8,128)S(1)} %add.11.a_ref), channel_id=1, source_target_pairs={{0,128},{64,192},{128,0},{192,64},{1,129},{65,193},{129,1},{193,65... | collective-permute-start | bytes 208904 | tf_op jit(solution)/shard_map/ppermute | solution.py:353
  60.4 44.3 %collective-permute-start.2 = (f32[1024,128]{1,0:T(8,128)S(1)}, f32[1024,128]{1,0:T(8,128)S(1)}, u32[]{:S(2)}, u32[]{:S(2)}) collective-permute-start(f32[1024,128]{1,0:T(8,128)S(1)} %get-tuple-element.29.refs_0_), channel_id=1, source_target_pairs={{0,1},{1,2},{2,3},{3,4},{4,5},{5,6},{6,7},{7,8},{8,9},{9,10},{10,1... | collective-permute-start | bytes 1572872 | tf_op jit(solution)/shard_map/ppermute | solution.py:332
  61.7 43.0 %collective-permute-start.6 = (f32[1024,128]{1,0:T(8,128)S(1)}, f32[1024,128]{1,0:T(8,128)S(1)}, u32[]{:S(2)}, u32[]{:S(2)}) collective-permute-start(f32[1024,128]{1,0:T(8,128)S(1)} %collective-permute-done.5), channel_id=1, source_target_pairs={{33,32},{1,0},{97,96},{65,64},{161,160},{129,128},{225,224},{193,1... | collective-permute-start | bytes 1572872 | tf_op jit(solution)/shard_map/ppermute | solution.py:346
  68.5 85.7 %collective-permute-start.17 = (f32[2048,128]{1,0:T(8,128)S(1)}, f32[2048,128]{1,0:T(8,128)S(1)}, u32[]{:S(2)}, u32[]{:S(2)}) collective-permute-start(f32[2048,128]{1,0:T(8,128)S(1)} %get-tuple-element.43), channel_id=1, source_target_pairs={{0,1},{1,2},{2,3},{3,4},{4,5},{5,6},{6,7},{7,8},{8,9},{9,10},{10,1... | collective-permute-start | bytes 3145736 | tf_op jit(solution)/shard_map/ppermute | solution.py:332
  71.1 30.1 %collective-permute-start.3 = (f32[512,128]{1,0:T(8,128)S(1)}, f32[512,128]{1,0:T(8,128)S(1)}, u32[]{:S(2)}, u32[]{:S(2)}) collective-permute-start(f32[512,128]{1,0:T(8,128)S(1)} %get-tuple-element.30.refs_1_), channel_id=1, source_target_pairs={{0,1},{1,2},{2,3},{3,4},{4,5},{5,6},{6,7},{7,8},{8,9},{9,10},{10,1... | collective-permute-start | bytes 786440 | tf_op jit(solution)/shard_map/ppermute | solution.py:332
  73.1 31.7 %collective-permute-start.7 = (f32[512,128]{1,0:T(8,128)S(1)}, f32[512,128]{1,0:T(8,128)S(1)}, u32[]{:S(2)}, u32[]{:S(2)}) collective-permute-start(f32[512,128]{1,0:T(8,128)S(1)} %get-tuple-element.30.refs_1_), channel_id=1, source_target_pairs={{31,32},{63,0},{95,96},{127,64},{159,160},{191,128},{223,224},{255... | collective-permute-start | bytes 786440 | tf_op jit(solution)/shard_map/ppermute | solution.py:332
  106.4 47.8 %collective-permute-start.18 = (f32[1024,128]{1,0:T(8,128)S(1)}, f32[1024,128]{1,0:T(8,128)S(1)}, u32[]{:S(2)}, u32[]{:S(2)}) collective-permute-start(f32[1024,128]{1,0:T(8,128)S(1)} %get-tuple-element.44), channel_id=1, source_target_pairs={{0,1},{1,2},{2,3},{3,4},{4,5},{5,6},{6,7},{7,8},{8,9},{9,10},{10,1... | collective-permute-start | bytes 1572872 | tf_op jit(solution)/shard_map/ppermute | solution.py:332
  106.5 4.8 %collective-permute-start.19 = (f32[8,128]{1,0:T(8,128)S(1)}, f32[8,128]{1,0:T(8,128)S(1)}, u32[]{:S(2)}, u32[]{:S(2)}) collective-permute-start(f32[8,128]{1,0:T(8,128)S(1)} %max.30), channel_id=1, source_target_pairs={{0,24},{1,25},{2,26},{3,27},{4,28},{5,29},{6,30},{7,31},{8,0},{9,1... | collective-permute-start | bytes 12296 | tf_op jit(solution)/shard_map/ppermute | solution.py:364
  106.6 47.6 %collective-permute-start.16 = (f32[512,128]{1,0:T(8,128)S(1)}, f32[512,128]{1,0:T(8,128)S(1)}, u32[]{:S(2)}, u32[]{:S(2)}) collective-permute-start(f32[512,128]{1,0:T(8,128)S(1)} %get-tuple-element.42), channel_id=1, source_target_pairs={{0,1},{1,2},{2,3},{3,4},{4,5},{5,6},{6,7},{7,8},{8,9},{9,10},{10,1... | collective-permute-start | bytes 786440 | tf_op jit(solution)/shard_map/ppermute | solution.py:332
  109.0 46.6 %collective-permute-start.15 = (f32[512,128]{1,0:T(8,128)S(1)}, f32[512,128]{1,0:T(8,128)S(1)}, u32[]{:S(2)}, u32[]{:S(2)}) collective-permute-start(f32[512,128]{1,0:T(8,128)S(1)} %get-tuple-element.41), channel_id=1, source_target_pairs={{0,1},{1,2},{2,3},{3,4},{4,5},{5,6},{6,7},{7,8},{8,9},{9,10},{10,1... | collective-permute-start | bytes 786440 | tf_op jit(solution)/shard_map/ppermute | solution.py:332
  118.5 6.1 %collective-permute-start.22 = (f32[8,128]{1,0:T(8,128)S(1)}, f32[8,128]{1,0:T(8,128)S(1)}, u32[]{:S(2)}, u32[]{:S(2)}) collective-permute-start(f32[8,128]{1,0:T(8,128)S(1)} %max.33), channel_id=1, source_target_pairs={{0,7},{1,0},{2,1},{3,2},{4,3},{5,4},{6,5},{7,6},{8,15},{9,8},{10,9... | collective-permute-start | bytes 12296 | tf_op jit(solution)/shard_map/ppermute | solution.py:364
  124.7 4.5 %collective-permute-start.23 = (f32[8,128]{1,0:T(8,128)S(1)}, f32[8,128]{1,0:T(8,128)S(1)}, u32[]{:S(2)}, u32[]{:S(2)}) collective-permute-start(f32[8,128]{1,0:T(8,128)S(1)} %max.33), channel_id=1, source_target_pairs={{0,6},{1,7},{2,0},{3,1},{4,2},{5,3},{6,4},{7,5},{8,14},{9,15},{10,... | collective-permute-start | bytes 12296 | tf_op jit(solution)/shard_map/ppermute | solution.py:364
  129.2 6.5 %collective-permute-start.24 = (f32[8,128]{1,0:T(8,128)S(1)}, f32[8,128]{1,0:T(8,128)S(1)}, u32[]{:S(2)}, u32[]{:S(2)}) collective-permute-start(f32[8,128]{1,0:T(8,128)S(1)} %max.33), channel_id=1, source_target_pairs={{0,5},{1,6},{2,7},{3,0},{4,1},{5,2},{6,3},{7,4},{8,13},{9,14},{10,... | collective-permute-start | bytes 12296 | tf_op jit(solution)/shard_map/ppermute | solution.py:364
  135.7 6.6 %collective-permute-start.25 = (f32[8,128]{1,0:T(8,128)S(1)}, f32[8,128]{1,0:T(8,128)S(1)}, u32[]{:S(2)}, u32[]{:S(2)}) collective-permute-start(f32[8,128]{1,0:T(8,128)S(1)} %maximum_maximum_fusion), channel_id=1, source_target_pairs={{0,5},{1,6},{2,7},{3,0},{4,1},{5,2},{6,3},{7,4},{8,13},{9,14},{10,... | collective-permute-start | bytes 12296 | tf_op jit(solution)/shard_map/ppermute | solution.py:364
  142.3 6.1 %collective-permute-start.26 = (f32[8,128]{1,0:T(8,128)S(1)}, f32[8,128]{1,0:T(8,128)S(1)}, u32[]{:S(2)}, u32[]{:S(2)}) collective-permute-start(f32[8,128]{1,0:T(8,128)S(1)} %max.37), channel_id=1, source_target_pairs={{0,7},{1,0},{2,1},{3,2},{4,3},{5,4},{6,5},{7,6},{8,15},{9,8},{10,9... | collective-permute-start | bytes 12296 | tf_op jit(solution)/shard_map/ppermute | solution.py:364
  148.5 5.1 %collective-permute-start.27 = (f32[8,128]{1,0:T(8,128)S(1)}, f32[8,128]{1,0:T(8,128)S(1)}, u32[]{:S(2)}, u32[]{:S(2)}) collective-permute-start(f32[8,128]{1,0:T(8,128)S(1)} %max.38), channel_id=1, source_target_pairs={{0,32},{1,33},{2,34},{3,35},{4,36},{5,37},{6,38},{7,39},{8,40},{9,... | collective-permute-start | bytes 12296 | tf_op jit(solution)/shard_map/ppermute | solution.py:364
  (4 other events, 9.9 us)
